TPU v7x, 32 devices: a whole 2x2x4 slice. The times are simulated.
32 devices in a mesh: curve: 8 (over z, x), grp: 4 (over y, core).
Axes of the slice: x: 2, y: 2, z: 4, core: 2. Of those that a mesh axis runs over, the one named last changes fastest.
Arguments:
- state: float32 [2, 512, 4, 12288], P(None, None, 'grp', 'curve'), may hold values from -6 to 6
- coef: float32 [512, 4, 12288], P(None, 'grp', 'curve'), may hold values from 0.2 to 4
- counts: int32 [4, 8], P('grp', 'curve'), may hold values from 512 to 1536, as said below
Outputs:
- smoothed: float32 [512, 4, 8192], P(None, 'grp', 'curve')
Inputs may be any that keep to these rules, and one draw needn't show every extreme that they name: `counts`: each rank's count is 1024 plus the drift at its own end minus the drift at the end of the rank before it; drifts lie in -256 to 256, are zero before the first rank and at the last rank, so the curve holds 8192 blocks; in every curve one rank holds exactly 1536 blocks.
All inputs are finite; a program needn't handle non-finite values.
Results may differ from a plain program's by a relative error of at most 0.00002.
Values sent between devices are 32-bit elements; how exact they have to be, the bound alone decides.
No kernel may reach another device: no remote copies, remote signals or barrier semaphores. Data moves between devices by JAX's collectives and lax.ppermute only.
A program may use at most 128 MiB of HBM per device.

v0:
```python
import jax
import jax.numpy as jnp
from jax import lax
from jax.sharding import PartitionSpec as P

AVG = 1024
HALF = 256
CAP = 1536
SWEEPS = 2


def from_behind(value, axis, steps):
    count = lax.axis_size(axis)
    initial, last = (max(0, -steps), min(count, count - steps))
    return lax.ppermute(value, axis, [(source, source + steps) for source in range(initial, last)])


def extended(block, sides, width):
    for axis, dim in sides:
        count = lax.axis_size(axis)
        forward = [(i, i + 1) for i in range(count - 1)]
        backward = [(target, source) for source, target in forward]
        low = lax.ppermute(
            lax.slice_in_dim(block, block.shape[dim] - width, None, axis=dim), axis, forward
        )
        high = lax.ppermute(lax.slice_in_dim(block, 0, width, axis=dim), axis, backward)
        block = jnp.concatenate([low, block, high], axis=dim)
    return block


def smooth(field, source, coef, left_block, right_block, low_face, high_face):
    xplus = jnp.concatenate(
        [field[1:], jnp.concatenate([field[0:1, :, :, :, 1:], right_block[0:1]], axis=4)], axis=0
    )
    xminus = jnp.concatenate(
        [jnp.concatenate([left_block[7:8], field[7:8, :, :, :, :-1]], axis=4), field[:-1]], axis=0
    )
    yplus = jnp.concatenate([field[:, 1:], high_face[:, None]], axis=1)
    yminus = jnp.concatenate([low_face[:, None], field[:, :-1]], axis=1)
    zeroes = jnp.zeros_like(field[:, :, 0:1])
    zplus = jnp.concatenate([field[:, :, 1:], zeroes], axis=2)
    zminus = jnp.concatenate([zeroes, field[:, :, :-1]], axis=2)
    total = xplus + xminus + yplus + yminus + zplus + zminus
    return (source + total) / (6.0 + coef)


def local(state, coef, counts):
    held = counts[0, 0]
    rank = lax.axis_index("curve")
    every = lax.all_gather(counts, "curve", axis=1, tiled=True)
    order = jnp.arange(every.shape[1], dtype=jnp.int32)
    before = jnp.sum(jnp.where(order < rank, every[0], 0))
    drift_prev = before - rank * AVG
    drift_next = before + held - (rank + 1) * AVG
    tail_state = lax.dynamic_slice_in_dim(state, held - HALF, HALF, 3)
    tail_coef = lax.dynamic_slice_in_dim(coef, held - HALF, HALF, 2)
    from_left = from_behind((tail_state, tail_coef), "curve", 1)
    from_right = from_behind((state[:, :, :, :HALF], coef[:, :, :HALF]), "curve", -1)
    joined_state = jnp.concatenate([from_left[0], state, from_right[0]], axis=3)
    joined_coef = jnp.concatenate([from_left[1], coef, from_right[1]], axis=2)
    slot = jnp.arange(AVG, dtype=jnp.int32)
    keep_own = slot < AVG + drift_next
    first_start = HALF - drift_prev
    second_start = HALF + CAP - AVG - drift_next
    own_state = lax.dynamic_slice_in_dim(joined_state, first_start, AVG, 3)
    next_state = lax.dynamic_slice_in_dim(joined_state, second_start, AVG, 3)
    own_coef = lax.dynamic_slice_in_dim(joined_coef, first_start, AVG, 2)
    next_coef = lax.dynamic_slice_in_dim(joined_coef, second_start, AVG, 2)
    moved = jnp.where(keep_own, own_state, next_state)
    moved_coef = jnp.where(keep_own, own_coef, next_coef)
    field = moved[0].reshape(8, 8, 8, 1, AVG)
    source = moved[1].reshape(8, 8, 8, 1, AVG)
    cellcoef = moved_coef.reshape(8, 8, 8, 1, AVG)
    for sweep in range(SWEEPS):
        widened = extended(field, (("curve", 4),), 1)
        planes = jnp.stack([field[:, 0], field[:, 7]], axis=1)
        sides = extended(planes, (("grp", 3),), 1)
        low_face = sides[:, 1, :, 0:1]
        high_face = sides[:, 0, :, 2:3]
        field = smooth(
            field, source, cellcoef, widened[..., 0:1], widened[..., -1:], low_face, high_face
        )
    return field.reshape(512, 1, AVG)


def solution(mesh):
    placed = (P(None, None, "grp", "curve"), P(None, "grp", "curve"), P("grp", "curve"))
    return jax.shard_map(
        local, mesh=mesh, in_specs=placed, out_specs=P(None, "grp", "curve"), check_vma=False
    )
```

profile of v0, /device:TPU:15, one launch (start us, length us, event | category | flops | bytes accessed | tf_op | source)
XLA Modules:
  0.0 240.0 jit_solution(8155359105987020125)
XLA Ops:
  0.7 3.7 %fusion.9 = (f32[512,1,256]{2,1,0:T(1,128)}, f32[512,1,256]{2,1,0:T(1,128)}) fusion(f32[512,1,1536]{2,1,0:T(1,128)} %param.4, s32[]{:T(128)S(6)} %select_n.25), kind=kLoop, calls=%fused_computation.28 | loop fusion | bytes 2097156 | tf_op jit(solution)/shard_map/slice | solution.py:58
  6.6 4.3 %collective-permute-start.6 = (f32[512,1,256]{2,1,0:T(1,128)}, f32[512,1,256]{2,1,0:T(1,128)}, u32[]{:S(2)}, u32[]{:S(2)}) collective-permute-start(f32[512,1,256]{2,1,0:T(1,128)} %get-tuple-element.12), channel_id=1, source_target_pairs={{0,4},{4,8},{8,12},{12,16},{16,20},{20,24},{24,28},{1,5},{5,9},{9,... | collective-permute-start | bytes 1572872 | tf_op jit(solution)/shard_map/ppermute | solution.py:15
  10.8 5.9 %fusion.6 = (f32[2,512,1,256]{3,2,1,0:T(1,128)}, f32[2,512,1,256]{3,2,1,0:T(1,128)}) fusion(f32[2,512,1,1536]{3,2,1,0:T(1,128)} %param.3, s32[]{:T(128)S(6)} %select_n.25), kind=kLoop, calls=%fused_computation.25 | loop fusion | bytes 4194308 | tf_op jit(solution)/shard_map/slice | solution.py:58
  19.9 4.3 %collective-permute-start = (f32[2,512,1,256]{3,2,1,0:T(1,128)}, f32[2,512,1,256]{3,2,1,0:T(1,128)}, u32[]{:S(2)}, u32[]{:S(2)}) collective-permute-start(f32[2,512,1,256]{3,2,1,0:T(1,128)} %get-tuple-element.6), channel_id=1, source_target_pairs={{0,4},{4,8},{8,12},{12,16},{16,20},{20,24},{24,28},{1,5},{5,9},{9,... | collective-permute-start | bytes 3145736 | tf_op jit(solution)/shard_map/ppermute | solution.py:15
  24.2 58.0 %all-reduce.4 = s32[8]{0:T(128)S(1)} all-reduce(s32[8]{0:T(128)S(1)} %bitcast_dynamic-update-slice_fusion), channel_id=1, replica_groups=mesh['curve'=8,'grp'=4] {'curve'}, use_global_device_ids=true, to_apply=%add.4 | all-reduce | flops 8 | bytes 64 | tf_op jit(solution)/shard_map/squeeze | solution.py:52
  89.6 9.1 %fusion = f32[512,1,1024]{2,1,0:T(1,128)S(1)} fusion(pred[1024]{0:T(1024)(128)(4,1)S(1)} %iota_compare_fusion, f32[512,1,2048]{2,1,0:T(1,128)S(1)} %constant_dynamic-update-slice_fusion.3, s32[]{:T(128)S(6)} %select_n.27, s32[]{:T(128)S(6)} %select_n.26), kind=kLoop, calls=%fused_computation.2 | loop fusion | flops 1048576 | bytes 6292488 | tf_op jit(solution)/shard_map/add | solution.py:44
  98.7 3.0 %constant_dynamic-update-slice_fusion.2 = f32[2,512,1,2048]{3,2,1,0:T(1,128)} fusion(f32[2,512,1,256]{3,2,1,0:T(1,128)} %collective-permute-done), kind=kLoop, calls=%fused_computation.15 | loop fusion | bytes 2097152
  101.7 5.5 %constant_dynamic-update-slice_fusion.1 = f32[2,512,1,2048]{3,2,1,0:T(1,128)} fusion(f32[2,512,1,2048]{3,2,1,0:T(1,128)} %constant_dynamic-update-slice_fusion.2, f32[2,512,1,1536]{3,2,1,0:T(1,128)S(1)} %bitcast.23), kind=kLoop, calls=%fused_computation.14 | loop fusion | bytes 12582912
  107.2 3.0 %constant_dynamic-update-slice_fusion = f32[2,512,1,2048]{3,2,1,0:T(1,128)} fusion(f32[2,512,1,2048]{3,2,1,0:T(1,128)} %constant_dynamic-update-slice_fusion.1, f32[2,512,1,256]{3,2,1,0:T(1,128)} %collective-permute-done.1), kind=kLoop, calls=%fused_computation.13 | loop fusion | bytes 2097152 | tf_op jit(solution)/shard_map/concatenate | solution.py:59
  110.1 23.2 %broadcast_select_fusion = f32[2,512,1,1024]{3,2,1,0:T(1,128)} fusion(pred[1024]{0:T(1024)(128)(4,1)S(1)} %iota_compare_fusion, f32[2,512,1,2048]{3,2,1,0:T(1,128)} %constant_dynamic-update-slice_fusion, s32[]{:T(128)S(6)} %select_n.27, s32[]{:T(128)S(6)} %select_n.26), kind=kLoop, calls=%fused_computation | loop fusion | flops 1048576 | bytes 12583944 | tf_op jit(solution)/shard_map/jit(_where)/select_n | solution.py:69
  133.4 4.7 %fusion.7 = (f32[1,448,1,1024]{3,2,1,0:T(1,128)S(1)}, f32[1,448,1,1024]{3,2,1,0:T(1,128)S(1)}) fusion(f32[2,512,1,1024]{3,2,1,0:T(1,128)} %broadcast_select_fusion), kind=kLoop, calls=%fused_computation.26 | loop fusion | bytes 7340032 | tf_op jit(solution)/shard_map/slice | solution.py:33
  143.1 4.8 %collective-permute-start.4 = (f32[8,2,8,1,1024]{4,3,2,1,0:T(1,128)S(1)}, f32[8,2,8,1,1024]{4,3,2,1,0:T(1,128)S(1)}, u32[]{:S(2)}, u32[]{:S(2)}) collective-permute-start(f32[8,2,8,1,1024]{4,3,2,1,0:T(1,128)S(1)} %pad_maximum_fusion), channel_id=1, source_target_pairs={{1,0},{2,1},{3,2},{5,4},{6,5},{7,6},{9,8},{10,9},{11,10},{13,12},{... | collective-permute-start | bytes 1572872 | tf_op jit(solution)/shard_map/ppermute | solution.py:26
  147.8 3.7 %fusion.18 = (f32[8,7,8,1,1024]{4,3,2,1,0:T(1,128)S(1)}, f32[8,7,8,1,1024]{4,3,2,1,0:T(1,128)S(1)}) fusion(f32[8,8,8,1,1024]{4,3,2,1,0:T(1,128)S(1)} %bitcast.14), kind=kLoop, calls=%fused_computation.37 | loop fusion | bytes 7340032 | tf_op jit(solution)/shard_map/slice | solution.py:38
  156.7 4.3 %collective-permute-start.3 = (f32[8,8,8,1,1]{4,3,2,1,0:T(1,128)S(1)}, f32[8,8,8,1,1]{4,3,2,1,0:T(1,128)S(1)}, u32[]{:S(2)}, u32[]{:S(2)}) collective-permute-start(f32[8,8,8,1,1]{4,3,2,1,0:T(1,128)S(1)} %get-tuple-element.28), channel_id=1, source_target_pairs={{0,4},{4,8},{8,12},{12,16},{16,20},{20,24},{24,28},{1,5},{5,9},{9,... | collective-permute-start | bytes 6152 | tf_op jit(solution)/shard_map/ppermute | solution.py:23
  161.6 5.0 %collective-permute-done.2 = f32[8,8,8,1,1]{4,3,2,1,0:T(1,128)S(1)} collective-permute-done((f32[8,8,8,1,1]{4,3,2,1,0:T(1,128)S(1)}, f32[8,8,8,1,1]{4,3,2,1,0:T(1,128)S(1)}, u32[]{:S(2)}, u32[]{:S(2)}) %collective-permute-start.2) | collective-permute-done | bytes 2080 | tf_op jit(solution)/shard_map/ppermute | solution.py:26
  166.5 4.9 %collective-permute-done.3 = f32[8,8,8,1,1]{4,3,2,1,0:T(1,128)S(1)} collective-permute-done((f32[8,8,8,1,1]{4,3,2,1,0:T(1,128)S(1)}, f32[8,8,8,1,1]{4,3,2,1,0:T(1,128)S(1)}, u32[]{:S(2)}, u32[]{:S(2)}) %collective-permute-start.3) | collective-permute-done | bytes 2080 | tf_op jit(solution)/shard_map/ppermute | solution.py:23
  171.5 16.7 %add_divide_fusion.1 = f32[8,8,8,1,1024]{4,3,2,1,0:T(1,128)S(1)} fusion(f32[8,8,8,1,1024]{4,3,2,1,0:T(1,128)S(1)} %bitcast.18, f32[8,8,8,1,1024]{4,3,2,1,0:T(1,128)S(1)} %bitcast.20, f32[8,8,7,1,1024]{4,3,2,1,0:T(1,128)S(1)} %get-tuple-element.34, f32[8,8,7,1,1024]{4,3,2,1,0:T(1,128)S(1)} %get-tuple-element.33, ...), kind=kLoop, calls=%fused_computation.10 | loop fusion | flops 6815744 | bytes 18350080 | tf_op jit(solution)/shard_map/div | solution.py:44
  190.2 3.3 %collective-permute-start.10 = (f32[8,2,8,1,1024]{4,3,2,1,0:T(1,128)S(1)}, f32[8,2,8,1,1024]{4,3,2,1,0:T(1,128)S(1)}, u32[]{:S(2)}, u32[]{:S(2)}) collective-permute-start(f32[8,2,8,1,1024]{4,3,2,1,0:T(1,128)S(1)} %pad_maximum_fusion.1), channel_id=1, source_target_pairs={{1,0},{2,1},{3,2},{5,4},{6,5},{7,6},{9,8},{10,9},{11,10},{13,12},{... | collective-permute-start | bytes 1572872 | tf_op jit(solution)/shard_map/ppermute | solution.py:26
  196.0 5.2 %fusion.10 = (f32[7,8,8,1,1024]{4,3,2,1,0:T(1,128)S(1)}, f32[7,8,8,1,1024]{4,3,2,1,0:T(1,128)S(1)}) fusion(f32[8,8,8,1,1024]{4,3,2,1,0:T(1,128)S(1)} %add_divide_fusion.1), kind=kLoop, calls=%fused_computation.29 | loop fusion | bytes 7340032 | tf_op jit(solution)/shard_map/slice | solution.py:33
  201.3 3.6 %fusion.13 = (f32[8,7,8,1,1024]{4,3,2,1,0:T(1,128)S(1)}, f32[8,7,8,1,1024]{4,3,2,1,0:T(1,128)S(1)}) fusion(f32[8,8,8,1,1024]{4,3,2,1,0:T(1,128)S(1)} %add_divide_fusion.1), kind=kLoop, calls=%fused_computation.32 | loop fusion | bytes 7340032 | tf_op jit(solution)/shard_map/slice | solution.py:38
  207.5 4.3 %collective-permute-start.9 = (f32[8,8,8,1,1]{4,3,2,1,0:T(1,128)S(1)}, f32[8,8,8,1,1]{4,3,2,1,0:T(1,128)S(1)}, u32[]{:S(2)}, u32[]{:S(2)}) collective-permute-start(f32[8,8,8,1,1]{4,3,2,1,0:T(1,128)S(1)} %get-tuple-element.18), channel_id=1, source_target_pairs={{0,4},{4,8},{8,12},{12,16},{16,20},{20,24},{24,28},{1,5},{5,9},{9,... | collective-permute-start | bytes 6152 | tf_op jit(solution)/shard_map/ppermute | solution.py:23
  212.4 5.0 %collective-permute-done.8 = f32[8,8,8,1,1]{4,3,2,1,0:T(1,128)S(1)} collective-permute-done((f32[8,8,8,1,1]{4,3,2,1,0:T(1,128)S(1)}, f32[8,8,8,1,1]{4,3,2,1,0:T(1,128)S(1)}, u32[]{:S(2)}, u32[]{:S(2)}) %collective-permute-start.8) | collective-permute-done | bytes 2080 | tf_op jit(solution)/shard_map/ppermute | solution.py:26
  217.4 4.9 %collective-permute-done.9 = f32[8,8,8,1,1]{4,3,2,1,0:T(1,128)S(1)} collective-permute-done((f32[8,8,8,1,1]{4,3,2,1,0:T(1,128)S(1)}, f32[8,8,8,1,1]{4,3,2,1,0:T(1,128)S(1)}, u32[]{:S(2)}, u32[]{:S(2)}) %collective-permute-start.9) | collective-permute-done | bytes 2080 | tf_op jit(solution)/shard_map/ppermute | solution.py:23
  222.3 17.4 %add_divide_fusion = f32[8,8,8,1,1024]{4,3,2,1,0:T(1,128)} fusion(f32[8,8,8,1,1024]{4,3,2,1,0:T(1,128)S(1)} %bitcast.19, f32[8,8,8,1,1024]{4,3,2,1,0:T(1,128)S(1)} %bitcast.21, f32[8,8,7,1,1024]{4,3,2,1,0:T(1,128)S(1)} %get-tuple-element.24, f32[8,8,7,1,1024]{4,3,2,1,0:T(1,128)S(1)} %get-tuple-element.23, f32[8,7,8,1,1024]{4,3,2,1,0:T(1,128)S(1)} %get-tuple-element.20, ...), kind=kLoop, calls=%fused_computation.9 | loop fusion | flops 6815744 | bytes 18350080 | tf_op jit(solution)/shard_map/div | solution.py:44
  (52 shorter events, 30.0 us)
Async XLA Ops:
  4.4 83.6 %collective-permute-start.7 = (f32[512,1,256]{2,1,0:T(1,128)}, f32[512,1,256]{2,1,0:T(1,128)}, u32[]{:S(2)}, u32[]{:S(2)}) collective-permute-start(f32[512,1,256]{2,1,0:T(1,128)} %get-tuple-element.11), channel_id=1, source_target_pairs={{4,0},{8,4},{12,8},{16,12},{20,16},{24,20},{28,24},{5,1},{9,5},{13... | collective-permute-start | bytes 1572872 | tf_op jit(solution)/shard_map/ppermute | solution.py:15
  6.5 12.2 %copy-start.2 = (u32[32]{0:T(128)S(1)}, u32[32]{0:T(128)}, u32[]{:S(2)}) copy-start(u32[32]{0:T(128)} %constant.43) | copy-start | bytes 388
  6.5 78.9 %copy-start.1 = (f32[512,1,1536]{2,1,0:T(1,128)S(1)}, f32[512,1,1536]{2,1,0:T(1,128)}, u32[]{:S(2)}) copy-start(f32[512,1,1536]{2,1,0:T(1,128)} %param.4) | copy-start | bytes 9437188
  6.6 77.5 %collective-permute-start.6 = (f32[512,1,256]{2,1,0:T(1,128)}, f32[512,1,256]{2,1,0:T(1,128)}, u32[]{:S(2)}, u32[]{:S(2)}) collective-permute-start(f32[512,1,256]{2,1,0:T(1,128)} %get-tuple-element.12), channel_id=1, source_target_pairs={{0,4},{4,8},{8,12},{12,16},{16,20},{20,24},{24,28},{1,5},{5,9},{9,... | collective-permute-start | bytes 1572872 | tf_op jit(solution)/shard_map/ppermute | solution.py:15
  16.8 90.4 %collective-permute-start.1 = (f32[2,512,1,256]{3,2,1,0:T(1,128)}, f32[2,512,1,256]{3,2,1,0:T(1,128)}, u32[]{:S(2)}, u32[]{:S(2)}) collective-permute-start(f32[2,512,1,256]{3,2,1,0:T(1,128)} %get-tuple-element.5), channel_id=1, source_target_pairs={{4,0},{8,4},{12,8},{16,12},{20,16},{24,20},{28,24},{5,1},{9,5},{13... | collective-permute-start | bytes 3145736 | tf_op jit(solution)/shard_map/ppermute | solution.py:15
  19.9 78.8 %collective-permute-start = (f32[2,512,1,256]{3,2,1,0:T(1,128)}, f32[2,512,1,256]{3,2,1,0:T(1,128)}, u32[]{:S(2)}, u32[]{:S(2)}) collective-permute-start(f32[2,512,1,256]{3,2,1,0:T(1,128)} %get-tuple-element.6), channel_id=1, source_target_pairs={{0,4},{4,8},{8,12},{12,16},{16,20},{20,24},{24,28},{1,5},{5,9},{9,... | collective-permute-start | bytes 3145736 | tf_op jit(solution)/shard_map/ppermute | solution.py:15
  85.5 16.2 %slice-start = ((s8[6291456]{0:T(1024)(128)(4,1)}), s8[2097152]{0:T(1024)(128)(4,1)S(1)}, s32[]{:S(2)}) async-start(s8[6291456]{0:T(1024)(128)(4,1)} %bitcast.22), calls=%async_computation | async-start | bytes 4194304
  89.6 12.1 %slice-start.1 = ((s8[6291456]{0:T(1024)(128)(4,1)}), s8[4194304]{0:T(1024)(128)(4,1)S(1)}, s32[]{:S(2)}) async-start(s8[6291456]{0:T(1024)(128)(4,1)} %bitcast.22), calls=%async_computation.1 | async-start | bytes 8388608
  133.4 4.7 %copy-start = (f32[2,512,1,1024]{3,2,1,0:T(1,128)S(1)}, f32[2,512,1,1024]{3,2,1,0:T(1,128)}, u32[]{:S(2)}) copy-start(f32[2,512,1,1024]{3,2,1,0:T(1,128)} %broadcast_select_fusion) | copy-start | bytes 12582916
  141.5 29.8 %collective-permute-start.5 = (f32[8,2,8,1,1024]{4,3,2,1,0:T(1,128)S(1)}, f32[8,2,8,1,1024]{4,3,2,1,0:T(1,128)S(1)}, u32[]{:S(2)}, u32[]{:S(2)}) collective-permute-start(f32[8,2,8,1,1024]{4,3,2,1,0:T(1,128)S(1)} %pad_maximum_fusion), channel_id=1, source_target_pairs={{0,1},{1,2},{2,3},{4,5},{5,6},{6,7},{8,9},{9,10},{10,11},{12,13},{... | collective-permute-start | bytes 1572872 | tf_op jit(solution)/shard_map/ppermute | solution.py:23
  143.1 28.4 %collective-permute-start.4 = (f32[8,2,8,1,1024]{4,3,2,1,0:T(1,128)S(1)}, f32[8,2,8,1,1024]{4,3,2,1,0:T(1,128)S(1)}, u32[]{:S(2)}, u32[]{:S(2)}) collective-permute-start(f32[8,2,8,1,1024]{4,3,2,1,0:T(1,128)S(1)} %pad_maximum_fusion), channel_id=1, source_target_pairs={{1,0},{2,1},{3,2},{5,4},{6,5},{7,6},{9,8},{10,9},{11,10},{13,12},{... | collective-permute-start | bytes 1572872 | tf_op jit(solution)/shard_map/ppermute | solution.py:26
  154.8 11.8 %collective-permute-start.2 = (f32[8,8,8,1,1]{4,3,2,1,0:T(1,128)S(1)}, f32[8,8,8,1,1]{4,3,2,1,0:T(1,128)S(1)}, u32[]{:S(2)}, u32[]{:S(2)}) collective-permute-start(f32[8,8,8,1,1]{4,3,2,1,0:T(1,128)S(1)} %get-tuple-element.27), channel_id=1, source_target_pairs={{4,0},{8,4},{12,8},{16,12},{20,16},{24,20},{28,24},{5,1},{9,5},{13... | collective-permute-start | bytes 6152 | tf_op jit(solution)/shard_map/ppermute | solution.py:26
  156.7 14.7 %collective-permute-start.3 = (f32[8,8,8,1,1]{4,3,2,1,0:T(1,128)S(1)}, f32[8,8,8,1,1]{4,3,2,1,0:T(1,128)S(1)}, u32[]{:S(2)}, u32[]{:S(2)}) collective-permute-start(f32[8,8,8,1,1]{4,3,2,1,0:T(1,128)S(1)} %get-tuple-element.28), channel_id=1, source_target_pairs={{0,4},{4,8},{8,12},{12,16},{16,20},{20,24},{24,28},{1,5},{5,9},{9,... | collective-permute-start | bytes 6152 | tf_op jit(solution)/shard_map/ppermute | solution.py:23
  188.9 33.4 %collective-permute-start.11 = (f32[8,2,8,1,1024]{4,3,2,1,0:T(1,128)S(1)}, f32[8,2,8,1,1024]{4,3,2,1,0:T(1,128)S(1)}, u32[]{:S(2)}, u32[]{:S(2)}) collective-permute-start(f32[8,2,8,1,1024]{4,3,2,1,0:T(1,128)S(1)} %pad_maximum_fusion.1), channel_id=1, source_target_pairs={{0,1},{1,2},{2,3},{4,5},{5,6},{6,7},{8,9},{9,10},{10,11},{12,13},{... | collective-permute-start | bytes 1572872 | tf_op jit(solution)/shard_map/ppermute | solution.py:23
  190.2 32.1 %collective-permute-start.10 = (f32[8,2,8,1,1024]{4,3,2,1,0:T(1,128)S(1)}, f32[8,2,8,1,1024]{4,3,2,1,0:T(1,128)S(1)}, u32[]{:S(2)}, u32[]{:S(2)}) collective-permute-start(f32[8,2,8,1,1024]{4,3,2,1,0:T(1,128)S(1)} %pad_maximum_fusion.1), channel_id=1, source_target_pairs={{1,0},{2,1},{3,2},{5,4},{6,5},{7,6},{9,8},{10,9},{11,10},{13,12},{... | collective-permute-start | bytes 1572872 | tf_op jit(solution)/shard_map/ppermute | solution.py:26
  205.6 11.8 %collective-permute-start.8 = (f32[8,8,8,1,1]{4,3,2,1,0:T(1,128)S(1)}, f32[8,8,8,1,1]{4,3,2,1,0:T(1,128)S(1)}, u32[]{:S(2)}, u32[]{:S(2)}) collective-permute-start(f32[8,8,8,1,1]{4,3,2,1,0:T(1,128)S(1)} %get-tuple-element.17), channel_id=1, source_target_pairs={{4,0},{8,4},{12,8},{16,12},{20,16},{24,20},{28,24},{5,1},{9,5},{13... | collective-permute-start | bytes 6152 | tf_op jit(solution)/shard_map/ppermute | solution.py:26
  207.5 14.7 %collective-permute-start.9 = (f32[8,8,8,1,1]{4,3,2,1,0:T(1,128)S(1)}, f32[8,8,8,1,1]{4,3,2,1,0:T(1,128)S(1)}, u32[]{:S(2)}, u32[]{:S(2)}) collective-permute-start(f32[8,8,8,1,1]{4,3,2,1,0:T(1,128)S(1)} %get-tuple-element.18), channel_id=1, source_target_pairs={{0,4},{4,8},{8,12},{12,16},{16,20},{20,24},{24,28},{1,5},{5,9},{9,... | collective-permute-start | bytes 6152 | tf_op jit(solution)/shard_map/ppermute | solution.py:23
where the time goes:
time: 245 us; the launch traced here: 240 us
  other arithmetic  68.3 us (28%)
  blocking collectives  58 us (24%)
  local copies, waits for them, and re-layouts  55.7 us (23%)
  starting transfers between devices  35.8 us (15%)
  waiting for transfers between devices  19.7 us (8%)
  between operations  2.48 us (1%)
    squeeze x1, blocking collectives, local(): before = jnp.sum(jnp.where(order < rank, every[0], 0))  58 us
    div x2, other arithmetic, smooth(): return (source + total) / (6.0 + coef)  34.2 us
    select_n x1, other arithmetic, local(): moved = jnp.where(keep_own, own_state, next_state)  23.2 us
    unnamed x17, local copies, waits for them, and re-layouts  13.5 us
    ppermute x4, starting transfers between devices, from_behind(): lax.ppermute(value, axis, [(source, source + steps) for source in range(i...  12.6 us
    ppermute x4, starting transfers between devices, extended(): lax.ppermute(lax.slice_in_dim(block, 0, width, axis=dim), axis, backward)  11.9 us
    ppermute x4, starting transfers between devices, extended(): lax.ppermute(lax.slice_in_dim(block, block.shape[dim] - width, None, axis...  11.3 us
    slice x2, local copies, waits for them, and re-layouts, smooth(): field[1:]  9.94 us
  transfers between devices with their start and end apart: 12, of which 4 were waited for; matrix products, arithmetic and copies ran while one was open for 21% of the time, Pallas kernels for 0%

commit v1 on v0

v1 whole, which is shorter than its diff:
```python
import jax
import jax.numpy as jnp
from jax import lax
from jax.experimental import pallas as pl
from jax.experimental.pallas import tpu as pltpu
from jax.sharding import PartitionSpec as P

AVG = 1024
HALF = 256
CAP = 1536
SWEEPS = 2

LANES = 128
OWN = CAP // LANES
ZONE = HALF // LANES
WIN = AVG // LANES
SLAB = 8 * OWN
CELLS = 512
PAD = 16
F32 = jnp.float32
ANY = pl.BlockSpec(memory_space=pl.ANY)
SMEM = pl.BlockSpec(memory_space=pltpu.SMEM)


def iota(shape, dim):
    return lax.broadcasted_iota(jnp.int32, shape, dim)


def copies(pairs, sems):
    return [pltpu.make_async_copy(a, b, sems.at[i]) for i, (a, b) in enumerate(pairs)]


def run_copies(pairs, sems):
    todo = copies(pairs, sems)
    for copy in todo:
        copy.start()
    for copy in todo:
        copy.wait()


def tail_place(held):
    first = held - HALF
    return lax.div(first, LANES), lax.rem(first, LANES)


def put_zones(load, tail, head, base, place):
    row, shift = place
    lane = iota((8, LANES), 1)
    for i in range(ZONE):
        head[pl.ds(base + i, 8, stride=ZONE), :] = load(i)
    rows = [load(jnp.minimum(row + i, OWN - 1)) for i in range(ZONE + 1)]
    back = lax.rem(LANES - shift, LANES)
    for i in range(ZONE):
        both = jnp.where(lane >= shift, rows[i], rows[i + 1])
        tail[pl.ds(base + i, 8, stride=ZONE), :] = pltpu.roll(both, back, 1)


def send_zones(tail, head, even_out, odd_out, sem, even):
    @pl.when(even)
    def _():
        run_copies([(tail, even_out), (head, odd_out)], sem)

    @pl.when(jnp.logical_not(even))
    def _():
        run_copies([(head, even_out), (tail, odd_out)], sem)


def take_zones(even_in, odd_in, tail, head, sem, even):
    @pl.when(even)
    def _():
        run_copies([(odd_in, tail), (even_in, head)], sem)

    @pl.when(jnp.logical_not(even))
    def _():
        run_copies([(even_in, tail), (odd_in, head)], sem)


def is_even(axis):
    return lax.rem(lax.axis_index(axis), 2) == 0


def up8(v):
    n = v.shape[0]
    z = lax.rem(iota(v.shape, 0), 8)
    return jnp.where(z < 7, pltpu.roll(v, n - 1, 0), 0.0)


def down8(v):
    z = lax.rem(iota(v.shape, 0), 8)
    return jnp.where(z > 0, pltpu.roll(v, 1, 0), 0.0)


def edge_rows(u_ref, s_ref, c_ref, outer, row, lane, extra_row):
    inner = 6 if outer == 7 else 1

    def at(ref, x, r):
        return ref[pl.ds(PAD + x * 8 * SLAB + r, 64, stride=OWN), :]

    u = at(u_ref, outer, row)
    side = s_ref[pl.ds(row, 64, stride=OWN), :] + at(u_ref, inner, row) + up8(u) + down8(u)
    zero = jnp.zeros((8, LANES), F32)
    side += jnp.concatenate([zero, u[:-8]], 0) + jnp.concatenate([u[8:], zero], 0)
    parts = [(u, side), (c_ref[pl.ds(row, 64, stride=OWN), :], at(u_ref, outer, extra_row))]
    back = lax.rem(LANES - lane, LANES)
    rows = []
    for pair in parts:
        square = pltpu.roll(jnp.concatenate(pair, 0), back, 1)
        rows.append(jnp.transpose(square)[0:1])
    return rows


def spread(packed):
    return jnp.transpose(jnp.broadcast_to(packed, (LANES, LANES)))


def faces_kernel(held_ref, state, coef, even_out, odd_out, u, s, c, tail, head, sem):
    held = held_ref[0, 0]
    rows = 8 * SLAB
    run_copies(
        [
            (state.at[0], u.at[pl.ds(PAD, 8 * rows)]),
            (state.at[1, pl.ds(0, rows)], s.at[0]),
            (state.at[1, pl.ds(7 * rows, rows)], s.at[1]),
            (coef.at[pl.ds(0, rows)], c.at[0]),
            (coef.at[pl.ds(7 * rows, rows)], c.at[1]),
        ],
        sem,
    )
    place = tail_place(held)
    for plane in range(2):
        for x in range(8):
            start = PAD + (x * 8 + 7 * plane) * SLAB
            load = lambda r, start=start: u[pl.ds(start + r, 8, stride=OWN), :]
            put_zones(load, tail, head, (plane * 8 + x) * 8 * ZONE, place)
    end = held - 1
    row, lane = lax.div(end, LANES), lax.rem(end, LANES)
    edge = 2 * 64 * ZONE
    blank = jnp.zeros((6, LANES), F32)
    first = edge_rows(u, s.at[0], c.at[0], 0, 0, 0, ZONE)
    head[pl.ds(edge, 8), :] = jnp.concatenate(first + [blank], 0)
    last = edge_rows(u, s.at[1], c.at[1], 7, row, lane, row - ZONE)
    tail[pl.ds(edge, 8), :] = jnp.concatenate(last + [blank], 0)
    send_zones(tail, head, even_out, odd_out, sem, is_even("curve"))


def rest_kernel(held_ref, state, coef, even_out, odd_out, u, s, c, tail, head, sem):
    run_copies(
        [(state.at[0, :, y], u.at[i]) for i, y in enumerate((1, 6))]
        + [(state.at[1, :, y], s.at[i]) for i, y in enumerate((0, 7))]
        + [(coef.at[:, y], c.at[i]) for i, y in enumerate((0, 1, 6, 7))],
        sem,
    )
    place = tail_place(held_ref[0, 0])

    def at(ref, i, x):
        return lambda r: ref[i, x, pl.ds(r, 8, stride=OWN), :]

    def both(i, x):
        return lambda r: at(u, i, x)(r) + at(s, i, x)(r)

    def body(x, carry):
        loads = [both(0, x)] + [at(c, i, x) for i in range(4)] + [both(1, x)]
        for plane, load in enumerate(loads):
            put_zones(load, tail, head, (plane * 8 + x) * 8 * ZONE, place)
        return carry

    lax.fori_loop(0, 8, body, 0)
    send_zones(tail, head, even_out, odd_out, sem, is_even("curve"))


def sweep_kernel(held_ref, state, coef, even_in, odd_in, pack, even_out, odd_out, u, s, c, v, w, edges, tail, head, sem):
    held = held_ref[0, 0]
    even = is_even("curve")
    rank, ranks = lax.axis_index("curve"), lax.axis_size("curve")
    rows = CELLS * OWN
    edge = 2 * 64 * ZONE
    run_copies(
        [
            (state.at[0], u.at[pl.ds(PAD, rows)]),
            (state.at[1], s),
            (coef, c),
        ],
        sem,
    )
    take_zones(
        even_in.at[pl.ds(edge, 8)], odd_in.at[pl.ds(edge, 8)], edges.at[0], edges.at[1], sem, even
    )
    row96 = iota((SLAB, LANES), 0)
    lane96 = iota((SLAB, LANES), 1)
    slot = lax.rem(row96, OWN) * LANES + lane96
    zlast, zfirst = row96 >= SLAB - OWN, row96 < OWN
    last_lane, first_lane = lane96 == LANES - 1, lane96 == 0
    starts = slot == 0
    ends = slot == held - 1

    def zsum(ref, b):
        up = jnp.where(zlast, 0.0, ref[pl.ds(b + OWN, SLAB), :])
        down = jnp.where(zfirst, 0.0, ref[pl.ds(b - OWN, SLAB), :])
        return up + down

    step = 8 * SLAB

    def left(ref, b):
        both = jnp.where(last_lane, ref[pl.ds(b - 1, SLAB), :], ref[pl.ds(b, SLAB), :])
        return jnp.where(starts, 0.0, pltpu.roll(both, 1, 1))

    def right(ref, b):
        both = jnp.where(first_lane, ref[pl.ds(b + 1, SLAB), :], ref[pl.ds(b, SLAB), :])
        return jnp.where(ends, 0.0, pltpu.roll(both, LANES - 1, 1))

    def xsum(ref, b, kind):
        if kind == 0:
            return left(ref, b + 7 * step) + ref[pl.ds(b + step, SLAB), :]
        if kind == 2:
            return ref[pl.ds(b - step, SLAB), :] + right(ref, b - 7 * step)
        return ref[pl.ds(b - step, SLAB), :] + ref[pl.ds(b + step, SLAB), :]

    def first(x, kind):
        def body(y, carry):
            b = (x * 8 + y) * SLAB
            if not isinstance(b, int):
                b = pl.multiple_of(b, 8)
            p = b + PAD
            total = s[pl.ds(b, SLAB), :] + zsum(u, p) + xsum(u, p, kind)
            total += u[pl.ds(p - SLAB, SLAB), :] + u[pl.ds(p + SLAB, SLAB), :]
            v[pl.ds(p, SLAB), :] = total / (6.0 + c[pl.ds(b, SLAB), :])
            return carry

        lax.fori_loop(1, 7, body, 0)

    each_x(first)

    end_row, end_lane = lax.div(held - 1, LANES), lax.rem(held - 1, LANES)
    lane = iota((64, LANES), 1)
    mine = []
    for side, x, at_row, at_lane, there in (
        (0, 0, 0, 0, rank > 0),
        (1, 7, end_row, end_lane, rank < ranks - 1),
    ):
        a = spread(edges[side, 0:1, :])
        b = spread(edges[side, 1:2, :])
        place = pl.ds(PAD + x * step + at_row, 64, stride=OWN)
        plain = pl.ds(x * step + at_row, 64, stride=OWN)
        hit = lane == at_lane
        cell = c[plain, :]
        v[place, :] = v[place, :] + jnp.where(hit, a[:64] / (6.0 + cell), 0.0)
        beyond = (a[64:] + u[place, :]) / (6.0 + b[:64])
        mine.append(jnp.where(jnp.logical_and(hit, there), beyond, 0.0))

    def second(x, kind):
        def at(y):
            b = (x * 8 + y) * SLAB
            if not isinstance(b, int):
                b = pl.multiple_of(b, 8)
            return b, b + PAD

        def put(y, value):
            o = (y * 8 + x) * SLAB
            if not isinstance(o, int):
                o = pl.multiple_of(o, 8)
            w[pl.ds(o, SLAB), :] = value

        for y, inner in ((0, 1), (7, 6)):
            put(y, s[pl.ds(at(y)[0], SLAB), :] + v[pl.ds(at(inner)[1], SLAB), :])
        for y, inner in ((1, 2), (6, 5)):
            b, p = at(y)
            total = s[pl.ds(b, SLAB), :] + zsum(v, p) + xsum(v, p, kind)
            put(y, total + v[pl.ds(at(inner)[1], SLAB), :])

        def body(y, carry):
            b = (x * 8 + y) * SLAB
            b = b if isinstance(b, int) else pl.multiple_of(b, 8)
            p = b + PAD
            total = s[pl.ds(b, SLAB), :] + zsum(v, p) + xsum(v, p, kind)
            total += v[pl.ds(p - SLAB, SLAB), :] + v[pl.ds(p + SLAB, SLAB), :]
            o = pl.multiple_of((y * 8 + x) * SLAB, 8)
            w[pl.ds(o, SLAB), :] = total / (6.0 + c[pl.ds(b, SLAB), :])
            return carry

        lax.fori_loop(2, 6, body, 0)

    each_x(second)

    for side, x, at_row in ((0, 0, 0), (1, 7, end_row)):
        for y in range(1, 7):
            o = pl.ds((y * 8 + x) * SLAB + at_row, 8, stride=OWN)
            more = mine[side][8 * y : 8 * y + 8]
            if 2 <= y <= 5:
                more = more / (6.0 + c[pl.ds((x * 8 + y) * SLAB + at_row, 8, stride=OWN), :])
            w[o, :] = w[o, :] + more

    place = tail_place(held)

    def body(i, carry):
        load = lambda r: w[pl.ds(i * SLAB + r, 8, stride=OWN), :]
        put_zones(load, tail, head, pl.multiple_of(i * 8 * ZONE, 8), place)
        return carry

    lax.fori_loop(0, 64, body, 0)
    save = pltpu.make_async_copy(w, pack, sem.at[7])
    save.start()
    send_zones(tail, head, even_out, odd_out, sem, even)
    save.wait()


class Window:
    def __init__(self, before, after):
        self.lane = iota((WIN, LANES), 1)
        self.row = iota((WIN, LANES), 0)
        j = self.row * LANES + self.lane
        down = lambda n: lax.shift_right_arithmetic(n, 7)
        self.own_row = down(-before)
        self.own_lane = jnp.bitwise_and(-before, LANES - 1)
        self.head_row = down(-AVG - after)
        self.head_lane = jnp.bitwise_and(-AVG - after, LANES - 1)
        self.tail_row = self.own_row + ZONE
        self.from_tail = j < before
        self.from_head = j >= AVG + after

    def take(self, ref, start, row, shift):
        a = ref[pl.ds(start + row, WIN), :]
        b = ref[pl.ds(start + row + 1, WIN), :]
        return pltpu.roll(
            jnp.where(self.lane >= shift, a, b), jnp.bitwise_and(LANES - shift, LANES - 1), 1
        )

    def __call__(self, own, own_at, tail, tail_at, head, head_at):
        mine = self.take(own, own_at, self.own_row, self.own_lane)
        prev = self.take(tail, tail_at, self.tail_row, self.own_lane)
        after = self.take(head, head_at, self.head_row, self.head_lane)
        return jnp.where(self.from_tail, prev, jnp.where(self.from_head, after, mine))


def drifts(held_ref, before_ref):
    rank = lax.axis_index("curve")
    before = before_ref[0, 0] - rank * AVG
    return before, before + held_ref[0, 0] - AVG


def face_planes(ref, state_or_coef, planes, where):
    size = 8 * SLAB
    return [
        (state_or_coef.at[:, y], ref.at[pl.ds(PAD + i * size, size)].reshape(8, SLAB, LANES))
        for y, i in zip(planes, where)
    ]


def send_faces(low, high, even_out, odd_out, sem):
    even = is_even("grp")

    @pl.when(even)
    def _():
        run_copies([(high, even_out), (low, odd_out)], sem)

    @pl.when(jnp.logical_not(even))
    def _():
        run_copies([(low, even_out), (high, odd_out)], sem)


def take_faces(even_in, odd_in, low, high, sem):
    even = is_even("grp")

    @pl.when(even)
    def _():
        run_copies([(odd_in, low), (even_in, high)], sem)

    @pl.when(jnp.logical_not(even))
    def _():
        run_copies([(even_in, low), (odd_in, high)], sem)


def align_kernel(
    held_ref, before_ref, state, even_in, odd_in,
    even_out, odd_out, faces, sides,
    own, tail, head, edges, sem,
):
    before, after = drifts(held_ref, before_ref)
    even = is_even("curve")
    edge = 2 * 64 * ZONE
    run_copies(face_planes(own, state.at[0], (0, 7), (0, 1)), sem)
    zone = pl.ds(PAD, edge)
    take_zones(
        even_in.at[pl.ds(0, edge)], odd_in.at[pl.ds(0, edge)], tail.at[zone], head.at[zone], sem, even
    )
    packed = pl.ds(edge, 8)
    take_zones(even_in.at[packed], odd_in.at[packed], edges.at[0], edges.at[1], sem, even)
    here = Window(before, after)

    def body(i, carry):
        at = PAD + i * OWN
        zat = PAD + i * ZONE
        faces[pl.ds(pl.multiple_of(i * WIN, 8), WIN), :] = here(own, at, tail, zat, head, zat)
        return carry

    lax.fori_loop(0, 128, body, 0)
    lower = Window(before + 1, after + 1)
    upper = Window(before - 1, after - 1)
    j = here.row * LANES + here.lane
    for side, window, x, lost in (
        (0, lower, 7, jnp.logical_and(j == 0, before == HALF)),
        (1, upper, 0, jnp.logical_and(j == AVG - 1, after == -HALF)),
    ):
        beyond = spread(edges[side, 1:2, :])[64:]
        for plane in range(2):
            for z in range(8):
                i = (plane * 8 + x) * 8 + z
                at = PAD + i * OWN
                zat = PAD + i * ZONE
                value = window(own, at, tail, zat, head, zat)
                y = 56 * plane + z
                value = jnp.where(lost, beyond[y : y + 1], value)
                sides[pl.ds(((side * 2 + plane) * 8 + z) * WIN, WIN), :] = value
    half = 64 * WIN
    send_faces(faces.at[pl.ds(0, half)], faces.at[pl.ds(half, half)], even_out, odd_out, sem)


def each_x(run):
    run(0, 0)

    def mid(x, carry):
        run(x, 1)
        return carry

    lax.fori_loop(1, 7, mid, 0)
    run(7, 2)


def cell_rows(plane, x, z):
    at = ((plane * 8 + x) * 8 + z) * WIN
    return pl.ds(at if isinstance(at, int) else pl.multiple_of(at, 8), WIN)


def face_kernel(
    held_ref, before_ref, state, coef, even_in, odd_in, even_face, odd_face, faces, sides,
    even_out, odd_out, even_end, odd_end, new, below, inner,
    own, tail, head, near, q, ends, sem,
):
    before, after = drifts(held_ref, before_ref)
    even = is_even("curve")
    size = 6 * 64 * ZONE
    half = 64 * WIN
    run_copies(
        face_planes(own, state.at[0], (1, 6), (0, 5))
        + face_planes(own, coef, (0, 1, 6, 7), (1, 2, 3, 4))
        + face_planes(own, state.at[1], (0, 7), (6, 7)),
        sem,
    )
    zone = pl.ds(PAD, size)
    take_zones(even_in, odd_in, tail.at[zone], head.at[zone], sem, even)
    take_faces(even_face, odd_face, near.at[pl.ds(0, half)], near.at[pl.ds(half, half)], sem)
    for to, more in ((0, 6), (5, 7)):
        for x in range(8):
            a = pl.ds(PAD + (to * 8 + x) * SLAB, SLAB)
            b = pl.ds(PAD + (more * 8 + x) * SLAB, SLAB)
            own[a, :] = own[a, :] + own[b, :]
    here = Window(before, after)

    def body(i, carry):
        for plane, ref, to, add in (
            (0, q, 0, 0.0),
            (5, q, 1, 0.0),
            (1, below, 0, 6.0),
            (4, below, 1, 6.0),
            (2, inner, 0, 6.0),
            (3, inner, 1, 6.0),
        ):
            at = PAD + (plane * 64 + i) * OWN
            zat = PAD + (plane * 64 + i) * ZONE
            value = here(own, at, tail, zat, head, zat)
            ref[pl.ds(pl.multiple_of((to * 64 + i) * WIN, 8), WIN), :] = value + add
        return carry

    lax.fori_loop(0, 64, body, 0)

    def run(x, kind):
        for plane in range(2):
            for z in range(8):
                here = cell_rows(plane, x, z)
                total = q[here, :] + near[here, :]
                if kind == 0:
                    total += sides[pl.ds((plane * 8 + z) * WIN, WIN), :]
                else:
                    total += faces[cell_rows(plane, x - 1, z), :]
                if kind == 2:
                    total += sides[pl.ds(((2 + plane) * 8 + z) * WIN, WIN), :]
                else:
                    total += faces[cell_rows(plane, x + 1, z), :]
                if z > 0:
                    total += faces[cell_rows(plane, x, z - 1), :]
                if z < 7:
                    total += faces[cell_rows(plane, x, z + 1), :]
                new[here, :] = total / below[here, :]

    each_x(run)
    for plane in range(2):
        for z in range(8):
            i = plane * 8 + z
            ends[0, i : i + 1, :] = new[pl.ds(((plane * 8 + 7) * 8 + z) * WIN + WIN - 1, 1), :]
            ends[1, i : i + 1, :] = new[pl.ds((plane * 64 + z) * WIN, 1), :]
    send_faces(new.at[pl.ds(0, half)], new.at[pl.ds(half, half)], even_out, odd_out, sem)
    send_zones(ends.at[0], ends.at[1], even_end, odd_end, sem, even)


def last_kernel(
    held_ref, before_ref, pack, even_in, odd_in, even_face, odd_face, even_end, odd_end,
    new, below, inner,
    out,
    own, tail, head, near, ends, sem,
):
    before, after = drifts(held_ref, before_ref)
    even = is_even("curve")
    size = 8 * 64 * ZONE
    half = 64 * WIN
    fetch = pltpu.make_async_copy(pack, own.at[pl.ds(PAD, CELLS * OWN)], sem.at[7])
    fetch.start()
    zone = pl.ds(PAD, size)
    take_zones(even_in, odd_in, tail.at[zone], head.at[zone], sem, even)
    take_zones(even_end, odd_end, ends.at[0], ends.at[1], sem, even)
    take_faces(even_face, odd_face, near.at[pl.ds(0, half)], near.at[pl.ds(half, half)], sem)
    fetch.wait()
    here = Window(before, after)
    lane, row = here.lane, here.row

    def get(y, x, z):
        i = (y * 8 + x) * 8 + z
        return here(own, PAD + i * OWN, tail, PAD + i * ZONE, head, PAD + i * ZONE)

    def put(x, y, z, value):
        at = ((x * 8 + y) * 8 + z) * WIN
        out[pl.ds(at if isinstance(at, int) else pl.multiple_of(at, 8), WIN), :] = value

    def left(plane, z):
        v = pltpu.roll(new[cell_rows(plane, 7, z), :], 1, 1)
        i = plane * 8 + z
        edge = pltpu.roll(jnp.broadcast_to(ends[0, i : i + 1, :], (WIN, LANES)), 1, 1)
        return jnp.where(lane == 0, jnp.where(row == 0, edge, pltpu.roll(v, 1, 0)), v)

    def right(plane, z):
        v = pltpu.roll(new[cell_rows(plane, 0, z), :], LANES - 1, 1)
        i = plane * 8 + z
        edge = pltpu.roll(jnp.broadcast_to(ends[1, i : i + 1, :], (WIN, LANES)), LANES - 1, 1)
        next_row = jnp.where(row == WIN - 1, edge, pltpu.roll(v, WIN - 1, 0))
        return jnp.where(lane == LANES - 1, next_row, v)

    def run(x, kind):
        for plane, y in ((0, 0), (1, 7)):
            for z in range(8):
                cell = cell_rows(plane, x, z)
                total = get(y, x, z) + near[cell, :]
                total += left(plane, z) if kind == 0 else new[cell_rows(plane, x - 1, z), :]
                total += right(plane, z) if kind == 2 else new[cell_rows(plane, x + 1, z), :]
                if z > 0:
                    total += new[cell_rows(plane, x, z - 1), :]
                if z < 7:
                    total += new[cell_rows(plane, x, z + 1), :]
                put(x, y, z, total / below[cell, :])
        for plane, y in ((0, 1), (1, 6)):
            for z in range(8):
                cell = cell_rows(plane, x, z)
                put(x, y, z, (get(y, x, z) + new[cell, :]) / inner[cell, :])
        for y in range(2, 6):
            for z in range(8):
                put(x, y, z, get(y, x, z))

    each_x(run)


def swapped(value, axis, first):
    count = lax.axis_size(axis)
    pairs = [(i, i + 1) for i in range(first, count - 1, 2)]
    return lax.ppermute(value, axis, pairs + [(b, a) for a, b in pairs])


def swaps(values, axis):
    return tuple(swapped(value, axis, first) for first, value in enumerate(values))


def held_before(counts):
    rank, count = lax.axis_index("curve"), lax.axis_size("curve")
    total, before, bit = counts, jnp.zeros_like(counts), 1
    while bit < count:
        other = lax.ppermute(total, "curve", [(i, i ^ bit) for i in range(count) if i ^ bit < count])
        before += jnp.where(jnp.bitwise_and(rank, bit) != 0, other, 0)
        total += other
        bit *= 2
    return before


def array(*shape):
    return jax.ShapeDtypeStruct(shape, F32)


def call(kernel, outs, ins, scratch, sems=8, vmem_ins=(), vmem_outs=None, scalars=1, cost=4000):
    vmem = pl.BlockSpec(memory_space=pltpu.VMEM)
    specs = [SMEM] * scalars
    specs += [vmem if i in vmem_ins else ANY for i in range(scalars, len(ins))]
    return pl.pallas_call(
        kernel,
        out_shape=outs,
        in_specs=specs,
        out_specs=[vmem if vmem_outs and i in vmem_outs else ANY for i in range(len(outs))],
        scratch_shapes=[pltpu.VMEM(shape, F32) for shape in scratch] + [pltpu.SemaphoreType.DMA((sems,))],
        compiler_params=pltpu.CompilerParams(vmem_limit_bytes=40 * 2**20),
        cost_estimate=pl.CostEstimate(flops=cost * 4000, bytes_accessed=cost * 1000, transcendentals=0),
    )(*ins)


def local(state, coef, counts):
    state3 = state.reshape(2, CELLS * OWN, LANES)
    coef2 = coef.reshape(CELLS * OWN, LANES)
    state5 = state.reshape(2, 8, 8, SLAB, LANES)
    coef4 = coef.reshape(8, 8, SLAB, LANES)
    rows = CELLS * OWN
    step = 8 * SLAB
    zone = 64 * ZONE
    win = 64 * WIN

    before = held_before(counts)
    message = (2 * zone + 8, LANES)
    faces_out = call(
        faces_kernel,
        [array(*message)] * 2,
        (counts, state3, coef2),
        [(rows + 2 * PAD, LANES), (2, step, LANES), (2, step, LANES), message, message],
    )
    faces_in = swaps(faces_out, "curve")
    message = (6 * zone, LANES)
    rest_out = call(
        rest_kernel,
        [array(*message)] * 2,
        (counts, state5, coef4),
        [(2, 8, SLAB, LANES), (2, 8, SLAB, LANES), (4, 8, SLAB, LANES), message, message],
    )
    rest_in = swaps(rest_out, "curve")
    message = (8 * zone, LANES)
    pack, *sweep_out = call(
        sweep_kernel,
        [array(rows, LANES)] + [array(*message)] * 2,
        (counts, state3, coef2, *faces_in),
        [
            (rows + 2 * PAD, LANES), (rows, LANES), (rows, LANES), (rows + 2 * PAD, LANES),
            (rows, LANES), (2, 8, LANES), message, message,
        ],
    )
    sweep_in = swaps(sweep_out, "curve")
    *near_out, faces, sides = call(
        align_kernel,
        [array(win, LANES)] * 2 + [array(2 * win, LANES), array(32 * WIN, LANES)],
        (counts, before, state5, *faces_in),
        [
            (2 * step + 2 * PAD, LANES), (2 * zone + 2 * PAD, LANES), (2 * zone + 2 * PAD, LANES),
            (2, 8, LANES),
        ],
        vmem_outs=(2, 3),
        scalars=2,
    )
    near_in = swaps(near_out, "grp")
    near_a, near_b, end_a, end_b, new, below, inner = call(
        face_kernel,
        [array(win, LANES)] * 2 + [array(16, LANES)] * 2 + [array(2 * win, LANES)] * 3,
        (counts, before, state5, coef4, *rest_in, *near_in, faces, sides),
        [
            (8 * step + 2 * PAD, LANES), (6 * zone + 2 * PAD, LANES), (6 * zone + 2 * PAD, LANES),
            (2 * win, LANES), (2 * win, LANES), (2, 16, LANES),
        ],
        vmem_ins=(8, 9),
        vmem_outs=(4, 5, 6),
        scalars=2,
    )
    near_in = swaps((near_a, near_b), "grp")
    end_in = swaps((end_a, end_b), "curve")
    (out,) = call(
        last_kernel,
        [array(CELLS * WIN, LANES)],
        (counts, before, pack, *sweep_in, *near_in, *end_in, new, below, inner),
        [
            (rows + 2 * PAD, LANES), (8 * zone + 2 * PAD, LANES), (8 * zone + 2 * PAD, LANES),
            (2 * win, LANES), (2, 16, LANES),
        ],
        vmem_ins=(9, 10, 11),
        vmem_outs=(0,),
        scalars=2,
    )
    return out.reshape(CELLS, 1, AVG)


def solution(mesh):
    placed = (P(None, None, "grp", "curve"), P(None, "grp", "curve"), P("grp", "curve"))
    return jax.shard_map(
        local, mesh=mesh, in_specs=placed, out_specs=P(None, "grp", "curve"), check_vma=False
    )
```

time: 245 us -> 103 us (0.42)
  the two profiles are of different devices: /device:TPU:15 before, /device:TPU:12 now
where the time goes in v1:
time: 103 us; the launch traced here: 102 us
  Pallas kernels  34.1 us (33%)
  starting transfers between devices  30.7 us (30%)
  waiting for transfers between devices  25.8 us (25%)
  local copies, waits for them, and re-layouts  7.45 us (7%)
  between operations  4.08 us (4%)
    pallas_call x6, Pallas kernels, call(): pl.pallas_call(kernel, out_shape=outs, in_specs=specs, out_specs=[vmem if...  34.1 us
    ppermute x12, starting transfers between devices, swapped(): return lax.ppermute(value, axis, pairs + [(b, a) for a, b in pairs])  23.8 us
    ppermute x3, waiting for transfers between devices, held_before(): lax.ppermute(total, 'curve', [(i, i ^ bit) for i in range(count) if i ^ b...  14.8 us
    ppermute x12, waiting for transfers between devices, swapped(): return lax.ppermute(value, axis, pairs + [(b, a) for a, b in pairs])  11 us
    unnamed x8, local copies, waits for them, and re-layouts  7.45 us
    ppermute x3, starting transfers between devices, held_before(): lax.ppermute(total, 'curve', [(i, i ^ bit) for i in range(count) if i ^ b...  6.87 us
  transfers between devices with their start and end apart: 15, of which 4 were waited for; matrix products, arithmetic and copies ran while one was open for 0% of the time, Pallas kernels for 28%

profile of v1, /device:TPU:12, one launch (start us, length us, event | category | flops | bytes accessed | tf_op | source)
XLA Modules:
  0.0 102.1 jit_solution(8332017507255269195)
XLA Ops:
  0.7 2.8 %copy-done = f32[2,512,1,1536]{3,2,1,0:T(1,128)S(1)} copy-done((f32[2,512,1,1536]{3,2,1,0:T(1,128)S(1)}, f32[2,512,1,1536]{3,2,1,0:T(1,128)}, u32[]{:S(2)}) %copy-start) | copy-done | bytes 6291480
  3.4 1.9 %copy-done.2 = f32[512,1,1536]{2,1,0:T(1,128)S(1)} copy-done((f32[512,1,1536]{2,1,0:T(1,128)S(1)}, f32[512,1,1536]{2,1,0:T(1,128)}, u32[]{:S(2)}) %copy-start.2) | copy-done | bytes 3145752
  5.3 1.5 %shard_map.39 = (f32[768,128]{1,0:T(8,128)S(1)}, f32[768,128]{1,0:T(8,128)S(1)}) custom-call(s32[1,1]{1,0:T(1,128)S(6)} %copy.5.held_ref, f32[2,8,8,96,128]{4,3,2,1,0:T(8,128)S(1)} %bitcast.8, f32[8,8,96,128]{3,2,1,0:T(8,128)S(1)} %bitcast.13), custom_call_target="tpu_custom_call" | custom-call | flops 16000000 | bytes 4000000 | tf_op jit(solution)/shard_map/pallas_call | solution.py:597
  6.8 1.6 %collective-permute-start.7 = (f32[768,128]{1,0:T(8,128)S(1)}, f32[768,128]{1,0:T(8,128)S(1)}, u32[]{:S(2)}, u32[]{:S(2)}) collective-permute-start(f32[768,128]{1,0:T(8,128)S(1)} %get-tuple-element.28), channel_id=1, source_target_pairs={{0,4},{8,12},{16,20},{24,28},{4,0},{12,8},{20,16},{28,24},{1,5},{9... | collective-permute-start | bytes 1179656 | tf_op jit(solution)/shard_map/ppermute | solution.py:571
  8.4 1.6 %shard_map.37 = (f32[264,128]{1,0:T(8,128)S(1)}, f32[264,128]{1,0:T(8,128)S(1)}) custom-call(s32[1,1]{1,0:T(1,128)S(6)} %copy.5.held_ref, f32[2,6144,128]{2,1,0:T(8,128)S(1)} %bitcast.9, f32[6144,128]{1,0:T(8,128)S(1)} %bitcast.14), custom_call_target="tpu_custom_call" | custom-call | flops 16000000 | bytes 4000000 | tf_op jit(solution)/shard_map/pallas_call | solution.py:597
  10.6 3.3 %collective-permute-start.4 = (f32[264,128]{1,0:T(8,128)S(1)}, f32[264,128]{1,0:T(8,128)S(1)}, u32[]{:S(2)}, u32[]{:S(2)}) collective-permute-start(f32[264,128]{1,0:T(8,128)S(1)} %get-tuple-element.24), channel_id=1, source_target_pairs={{4,8},{12,16},{20,24},{8,4},{16,12},{24,20},{5,9},{13,17},{21,25},... | collective-permute-start | bytes 405512 | tf_op jit(solution)/shard_map/ppermute | solution.py:571
  13.8 3.5 %collective-permute-start.8 = (f32[768,128]{1,0:T(8,128)S(1)}, f32[768,128]{1,0:T(8,128)S(1)}, u32[]{:S(2)}, u32[]{:S(2)}) collective-permute-start(f32[768,128]{1,0:T(8,128)S(1)} %get-tuple-element.29), channel_id=1, source_target_pairs={{4,8},{12,16},{20,24},{8,4},{16,12},{24,20},{5,9},{13,17},{21,25},... | collective-permute-start | bytes 1179656 | tf_op jit(solution)/shard_map/ppermute | solution.py:571
  17.3 1.6 %collective-permute-start = (s32[1,1]{1,0:T(1,128)}, s32[1,1]{1,0:T(1,128)}, u32[]{:S(2)}, u32[]{:S(2)}) collective-permute-start(s32[1,1]{1,0:T(1,128)} %param.5), channel_id=1, source_target_pairs={{0,4},{4,0},{8,12},{12,8},{16,20},{20,16},{24,28},{28,24},{1,5},{5... | collective-permute-start | bytes 20 | tf_op jit(solution)/shard_map/ppermute | solution.py:582
  18.9 13.1 %collective-permute-done = s32[1,1]{1,0:T(1,128)} collective-permute-done((s32[1,1]{1,0:T(1,128)}, s32[1,1]{1,0:T(1,128)}, u32[]{:S(2)}, u32[]{:S(2)}) %collective-permute-start) | collective-permute-done | bytes 36 | tf_op jit(solution)/shard_map/ppermute | solution.py:582
  34.8 1.7 %collective-permute-done.1 = s32[1,1]{1,0:T(1,128)} collective-permute-done((s32[1,1]{1,0:T(1,128)}, s32[1,1]{1,0:T(1,128)}, u32[]{:S(2)}, u32[]{:S(2)}) %collective-permute-start.1) | collective-permute-done | bytes 36 | tf_op jit(solution)/shard_map/ppermute | solution.py:582
  37.0 4.0 %collective-permute-start.2 = (s32[1,1]{1,0:T(1,128)}, s32[1,1]{1,0:T(1,128)}, u32[]{:S(2)}, u32[]{:S(2)}) collective-permute-start(s32[1,1]{1,0:T(1,128)} %add.14), channel_id=1, source_target_pairs={{0,16},{4,20},{8,24},{12,28},{16,0},{20,4},{24,8},{28,12},{1,17},{... | collective-permute-start | bytes 20 | tf_op jit(solution)/shard_map/ppermute | solution.py:582
  42.3 2.8 %copy-done.1 = f32[2,512,1,1536]{3,2,1,0:T(1,128)S(1)} copy-done((f32[2,512,1,1536]{3,2,1,0:T(1,128)S(1)}, f32[2,512,1,1536]{3,2,1,0:T(1,128)}, u32[]{:S(2)}) %copy-start.1) | copy-done | bytes 6291480
  45.1 10.2 %shard_map.40 = (f32[512,128]{1,0:T(8,128)S(1)}, f32[512,128]{1,0:T(8,128)S(1)}, f32[1024,128]{1,0:T(8,128)S(1)}, f32[256,128]{1,0:T(8,128)S(1)}) custom-call(s32[1,1]{1,0:T(1,128)S(6)} %copy.5.held_ref, s32[1,1]{1,0:T(1,128)S(6)} %add.15.before_ref, f32[2,8,8,96,128]{4,3,2,1,0:T(8,128)S(1)} %bitcast.10, f32[264,128]{1,0:T(8,128)S(1)} %collective-permute-done.3.even_in, ...), custom_call_target="tpu_custom_call" | custom-call | flops 16000000 | bytes 4000000 | tf_op jit(solution)/shard_map/pallas_call | solution.py:597
  55.4 2.5 %collective-permute-start.10 = (f32[512,128]{1,0:T(8,128)S(1)}, f32[512,128]{1,0:T(8,128)S(1)}, u32[]{:S(2)}, u32[]{:S(2)}) collective-permute-start(f32[512,128]{1,0:T(8,128)S(1)} %get-tuple-element.31), channel_id=1, source_target_pairs={{1,2},{2,1},{5,6},{6,5},{9,10},{10,9},{13,14},{14,13},{17,18},{18,... | collective-permute-start | bytes 786440 | tf_op jit(solution)/shard_map/ppermute | solution.py:571
  57.9 9.5 %shard_map.38 = (f32[6144,128]{1,0:T(8,128)S(1)}, f32[1024,128]{1,0:T(8,128)S(1)}, f32[1024,128]{1,0:T(8,128)S(1)}) custom-call(s32[1,1]{1,0:T(1,128)S(6)} %copy.5.held_ref, f32[2,6144,128]{2,1,0:T(8,128)S(1)} %bitcast.11, f32[6144,128]{1,0:T(8,128)S(1)} %bitcast.15, f32[264,128]{1,0:T(8,128)S(1)} %collective-permute-done.3.even_in, ...), custom_call_target="tpu_custom_call" | custom-call | flops 16000000 | bytes 4000000 | tf_op jit(solution)/shard_map/pallas_call | solution.py:597
  67.5 1.5 %collective-permute-start.5 = (f32[1024,128]{1,0:T(8,128)S(1)}, f32[1024,128]{1,0:T(8,128)S(1)}, u32[]{:S(2)}, u32[]{:S(2)}) collective-permute-start(f32[1024,128]{1,0:T(8,128)S(1)} %get-tuple-element.26), channel_id=1, source_target_pairs={{0,4},{8,12},{16,20},{24,28},{4,0},{12,8},{20,16},{28,24},{1,5},{9... | collective-permute-start | bytes 1572872 | tf_op jit(solution)/shard_map/ppermute | solution.py:571
  69.0 2.4 %collective-permute-start.6 = (f32[1024,128]{1,0:T(8,128)S(1)}, f32[1024,128]{1,0:T(8,128)S(1)}, u32[]{:S(2)}, u32[]{:S(2)}) collective-permute-start(f32[1024,128]{1,0:T(8,128)S(1)} %get-tuple-element.27), channel_id=1, source_target_pairs={{4,8},{12,16},{20,24},{8,4},{16,12},{24,20},{5,9},{13,17},{21,25},... | collective-permute-start | bytes 1572872 | tf_op jit(solution)/shard_map/ppermute | solution.py:571
  71.4 7.0 %shard_map.41 = (f32[512,128]{1,0:T(8,128)S(1)}, f32[512,128]{1,0:T(8,128)S(1)}, f32[16,128]{1,0:T(8,128)S(1)}, f32[16,128]{1,0:T(8,128)S(1)}, f32[1024,128]{1,0...) custom-call(s32[1,1]{1,0:T(1,128)S(6)} %copy.5.held_ref, s32[1,1]{1,0:T(1,128)S(6)} %add.15.before_ref, ...), custom_call_target="tpu_custom_call" | custom-call | flops 16000000 | bytes 4000000 | tf_op jit(solution)/shard_map/pallas_call | solution.py:597
  78.5 2.5 %collective-permute-start.12 = (f32[512,128]{1,0:T(8,128)S(1)}, f32[512,128]{1,0:T(8,128)S(1)}, u32[]{:S(2)}, u32[]{:S(2)}) collective-permute-start(f32[512,128]{1,0:T(8,128)S(1)} %get-tuple-element.35), channel_id=1, source_target_pairs={{1,2},{2,1},{5,6},{6,5},{9,10},{10,9},{13,14},{14,13},{17,18},{18,... | collective-permute-start | bytes 786440 | tf_op jit(solution)/shard_map/ppermute | solution.py:571
  81.0 2.6 %collective-permute-start.13 = (f32[16,128]{1,0:T(8,128)S(1)}, f32[16,128]{1,0:T(8,128)S(1)}, u32[]{:S(2)}, u32[]{:S(2)}) collective-permute-start(f32[16,128]{1,0:T(8,128)S(1)} %get-tuple-element.36), channel_id=1, source_target_pairs={{0,4},{8,12},{16,20},{24,28},{4,0},{12,8},{20,16},{28,24},{1,5},{9... | collective-permute-start | bytes 24584 | tf_op jit(solution)/shard_map/ppermute | solution.py:571
  83.6 7.8 %collective-permute-done.13.even_end = f32[16,128]{1,0:T(8,128)S(1)} collective-permute-done((f32[16,128]{1,0:T(8,128)S(1)}, f32[16,128]{1,0:T(8,128)S(1)}, u32[]{:S(2)}, u32[]{:S(2)}) %collective-permute-start.13) | collective-permute-done | bytes 8224 | tf_op jit(solution)/shard_map/ppermute | solution.py:571
  91.4 3.3 %collective-permute-start.14 = (f32[16,128]{1,0:T(8,128)S(1)}, f32[16,128]{1,0:T(8,128)S(1)}, u32[]{:S(2)}, u32[]{:S(2)}) collective-permute-start(f32[16,128]{1,0:T(8,128)S(1)} %get-tuple-element.37), channel_id=1, source_target_pairs={{4,8},{12,16},{20,24},{8,4},{16,12},{24,20},{5,9},{13,17},{21,25},... | collective-permute-start | bytes 24584 | tf_op jit(solution)/shard_map/ppermute | solution.py:571
  94.7 3.1 %collective-permute-done.14.odd_end = f32[16,128]{1,0:T(8,128)S(1)} collective-permute-done((f32[16,128]{1,0:T(8,128)S(1)}, f32[16,128]{1,0:T(8,128)S(1)}, u32[]{:S(2)}, u32[]{:S(2)}) %collective-permute-start.14) | collective-permute-done | bytes 8224 | tf_op jit(solution)/shard_map/ppermute | solution.py:571
  97.9 4.3 %shard_map.42 = f32[4096,128]{1,0:T(8,128)} custom-call(s32[1,1]{1,0:T(1,128)S(6)} %copy.5.held_ref, s32[1,1]{1,0:T(1,128)S(6)} %add.15.before_ref, f32[6144,128]{1,0:T(8,128)S(1)} %get-tuple-element.25.pack, f32[1024,128]{1,0:T(8,128)S(1)} %collective-permute-done.5.even_in, f32[1024,128]{1,0:T(8,128)S(1)} %collective-permute-done.6.odd_in, ...), custom_call_target="tpu_custom_call" | custom-call | flops 16000000 | bytes 4000000 | tf_op jit(solution)/shard_map/pallas_call | solution.py:597
  (20 shorter events, 2.2 us)
Async XLA Ops:
  0.7 2.8 %copy-start = (f32[2,512,1,1536]{3,2,1,0:T(1,128)S(1)}, f32[2,512,1,1536]{3,2,1,0:T(1,128)}, u32[]{:S(2)}) copy-start(f32[2,512,1,1536]{3,2,1,0:T(1,128)} %param.3) | copy-start | bytes 18874372
  3.4 1.9 %copy-start.2 = (f32[512,1,1536]{2,1,0:T(1,128)S(1)}, f32[512,1,1536]{2,1,0:T(1,128)}, u32[]{:S(2)}) copy-start(f32[512,1,1536]{2,1,0:T(1,128)} %param.4) | copy-start | bytes 9437188
  6.8 62.1 %collective-permute-start.7 = (f32[768,128]{1,0:T(8,128)S(1)}, f32[768,128]{1,0:T(8,128)S(1)}, u32[]{:S(2)}, u32[]{:S(2)}) collective-permute-start(f32[768,128]{1,0:T(8,128)S(1)} %get-tuple-element.28), channel_id=1, source_target_pairs={{0,4},{8,12},{16,20},{24,28},{4,0},{12,8},{20,16},{28,24},{1,5},{9... | collective-permute-start | bytes 1179656 | tf_op jit(solution)/shard_map/ppermute | solution.py:571
  10.0 32.3 %collective-permute-start.3 = (f32[264,128]{1,0:T(8,128)S(1)}, f32[264,128]{1,0:T(8,128)S(1)}, u32[]{:S(2)}, u32[]{:S(2)}) collective-permute-start(f32[264,128]{1,0:T(8,128)S(1)} %get-tuple-element.23), channel_id=1, source_target_pairs={{0,4},{8,12},{16,20},{24,28},{4,0},{12,8},{20,16},{28,24},{1,5},{9... | collective-permute-start | bytes 405512 | tf_op jit(solution)/shard_map/ppermute | solution.py:571
  10.6 31.7 %collective-permute-start.4 = (f32[264,128]{1,0:T(8,128)S(1)}, f32[264,128]{1,0:T(8,128)S(1)}, u32[]{:S(2)}, u32[]{:S(2)}) collective-permute-start(f32[264,128]{1,0:T(8,128)S(1)} %get-tuple-element.24), channel_id=1, source_target_pairs={{4,8},{12,16},{20,24},{8,4},{16,12},{24,20},{5,9},{13,17},{21,25},... | collective-permute-start | bytes 405512 | tf_op jit(solution)/shard_map/ppermute | solution.py:571
  13.8 57.5 %collective-permute-start.8 = (f32[768,128]{1,0:T(8,128)S(1)}, f32[768,128]{1,0:T(8,128)S(1)}, u32[]{:S(2)}, u32[]{:S(2)}) collective-permute-start(f32[768,128]{1,0:T(8,128)S(1)} %get-tuple-element.29), channel_id=1, source_target_pairs={{4,8},{12,16},{20,24},{8,4},{16,12},{24,20},{5,9},{13,17},{21,25},... | collective-permute-start | bytes 1179656 | tf_op jit(solution)/shard_map/ppermute | solution.py:571
  17.3 14.7 %collective-permute-start = (s32[1,1]{1,0:T(1,128)}, s32[1,1]{1,0:T(1,128)}, u32[]{:S(2)}, u32[]{:S(2)}) collective-permute-start(s32[1,1]{1,0:T(1,128)} %param.5), channel_id=1, source_target_pairs={{0,4},{4,0},{8,12},{12,8},{16,20},{20,16},{24,28},{28,24},{1,5},{5... | collective-permute-start | bytes 20 | tf_op jit(solution)/shard_map/ppermute | solution.py:582
  32.7 3.7 %collective-permute-start.1 = (s32[1,1]{1,0:T(1,128)}, s32[1,1]{1,0:T(1,128)}, u32[]{:S(2)}, u32[]{:S(2)}) collective-permute-start(s32[1,1]{1,0:T(1,128)} %add.12), channel_id=1, source_target_pairs={{0,8},{4,12},{8,0},{12,4},{16,24},{20,28},{24,16},{28,20},{1,9},{5... | collective-permute-start | bytes 20 | tf_op jit(solution)/shard_map/ppermute | solution.py:582
  37.0 4.5 %collective-permute-start.2 = (s32[1,1]{1,0:T(1,128)}, s32[1,1]{1,0:T(1,128)}, u32[]{:S(2)}, u32[]{:S(2)}) collective-permute-start(s32[1,1]{1,0:T(1,128)} %add.14), channel_id=1, source_target_pairs={{0,16},{4,20},{8,24},{12,28},{16,0},{20,4},{24,8},{28,12},{1,17},{... | collective-permute-start | bytes 20 | tf_op jit(solution)/shard_map/ppermute | solution.py:582
  42.3 2.8 %copy-start.1 = (f32[2,512,1,1536]{3,2,1,0:T(1,128)S(1)}, f32[2,512,1,1536]{3,2,1,0:T(1,128)}, u32[]{:S(2)}) copy-start(f32[2,512,1,1536]{3,2,1,0:T(1,128)} %param.3) | copy-start | bytes 18874372
  45.1 12.9 %copy-start.3 = (f32[512,1,1536]{2,1,0:T(1,128)S(1)}, f32[512,1,1536]{2,1,0:T(1,128)}, u32[]{:S(2)}) copy-start(f32[512,1,1536]{2,1,0:T(1,128)} %param.4) | copy-start | bytes 9437188
  55.3 16.0 %collective-permute-start.9 = (f32[512,128]{1,0:T(8,128)S(1)}, f32[512,128]{1,0:T(8,128)S(1)}, u32[]{:S(2)}, u32[]{:S(2)}) collective-permute-start(f32[512,128]{1,0:T(8,128)S(1)} %get-tuple-element.30), channel_id=1, source_target_pairs={{0,1},{2,3},{1,0},{3,2},{4,5},{6,7},{5,4},{7,6},{8,9},{10,11},{9,8... | collective-permute-start | bytes 786440 | tf_op jit(solution)/shard_map/ppermute | solution.py:571
  55.4 16.0 %collective-permute-start.10 = (f32[512,128]{1,0:T(8,128)S(1)}, f32[512,128]{1,0:T(8,128)S(1)}, u32[]{:S(2)}, u32[]{:S(2)}) collective-permute-start(f32[512,128]{1,0:T(8,128)S(1)} %get-tuple-element.31), channel_id=1, source_target_pairs={{1,2},{2,1},{5,6},{6,5},{9,10},{10,9},{13,14},{14,13},{17,18},{18,... | collective-permute-start | bytes 786440 | tf_op jit(solution)/shard_map/ppermute | solution.py:571
  67.5 30.4 %collective-permute-start.5 = (f32[1024,128]{1,0:T(8,128)S(1)}, f32[1024,128]{1,0:T(8,128)S(1)}, u32[]{:S(2)}, u32[]{:S(2)}) collective-permute-start(f32[1024,128]{1,0:T(8,128)S(1)} %get-tuple-element.26), channel_id=1, source_target_pairs={{0,4},{8,12},{16,20},{24,28},{4,0},{12,8},{20,16},{28,24},{1,5},{9... | collective-permute-start | bytes 1572872 | tf_op jit(solution)/shard_map/ppermute | solution.py:571
  69.0 28.9 %collective-permute-start.6 = (f32[1024,128]{1,0:T(8,128)S(1)}, f32[1024,128]{1,0:T(8,128)S(1)}, u32[]{:S(2)}, u32[]{:S(2)}) collective-permute-start(f32[1024,128]{1,0:T(8,128)S(1)} %get-tuple-element.27), channel_id=1, source_target_pairs={{4,8},{12,16},{20,24},{8,4},{16,12},{24,20},{5,9},{13,17},{21,25},... | collective-permute-start | bytes 1572872 | tf_op jit(solution)/shard_map/ppermute | solution.py:571
  78.4 19.5 %collective-permute-start.11 = (f32[512,128]{1,0:T(8,128)S(1)}, f32[512,128]{1,0:T(8,128)S(1)}, u32[]{:S(2)}, u32[]{:S(2)}) collective-permute-start(f32[512,128]{1,0:T(8,128)S(1)} %get-tuple-element.34), channel_id=1, source_target_pairs={{0,1},{2,3},{1,0},{3,2},{4,5},{6,7},{5,4},{7,6},{8,9},{10,11},{9,8... | collective-permute-start | bytes 786440 | tf_op jit(solution)/shard_map/ppermute | solution.py:571
  78.5 19.4 %collective-permute-start.12 = (f32[512,128]{1,0:T(8,128)S(1)}, f32[512,128]{1,0:T(8,128)S(1)}, u32[]{:S(2)}, u32[]{:S(2)}) collective-permute-start(f32[512,128]{1,0:T(8,128)S(1)} %get-tuple-element.35), channel_id=1, source_target_pairs={{1,2},{2,1},{5,6},{6,5},{9,10},{10,9},{13,14},{14,13},{17,18},{18,... | collective-permute-start | bytes 786440 | tf_op jit(solution)/shard_map/ppermute | solution.py:571
  81.0 10.5 %collective-permute-start.13 = (f32[16,128]{1,0:T(8,128)S(1)}, f32[16,128]{1,0:T(8,128)S(1)}, u32[]{:S(2)}, u32[]{:S(2)}) collective-permute-start(f32[16,128]{1,0:T(8,128)S(1)} %get-tuple-element.36), channel_id=1, source_target_pairs={{0,4},{8,12},{16,20},{24,28},{4,0},{12,8},{20,16},{28,24},{1,5},{9... | collective-permute-start | bytes 24584 | tf_op jit(solution)/shard_map/ppermute | solution.py:571
  91.4 6.4 %collective-permute-start.14 = (f32[16,128]{1,0:T(8,128)S(1)}, f32[16,128]{1,0:T(8,128)S(1)}, u32[]{:S(2)}, u32[]{:S(2)}) collective-permute-start(f32[16,128]{1,0:T(8,128)S(1)} %get-tuple-element.37), channel_id=1, source_target_pairs={{4,8},{12,16},{20,24},{8,4},{16,12},{24,20},{5,9},{13,17},{21,25},... | collective-permute-start | bytes 24584 | tf_op jit(solution)/shard_map/ppermute | solution.py:571

commit v2 on v1

--- a/solution.py
+++ b/solution.py
@@ -5,10 +5,10 @@
 from jax.experimental.pallas import tpu as pltpu
 from jax.sharding import PartitionSpec as P
 
+
 AVG = 1024
 HALF = 256
 CAP = 1536
-SWEEPS = 2
 
 LANES = 128
 OWN = CAP // LANES
@@ -19,6 +19,7 @@
 PAD = 16
 F32 = jnp.float32
 ANY = pl.BlockSpec(memory_space=pl.ANY)
+HBM = pl.BlockSpec(memory_space=pltpu.HBM)
 SMEM = pl.BlockSpec(memory_space=pltpu.SMEM)
 
 
@@ -94,13 +95,13 @@
     inner = 6 if outer == 7 else 1
 
     def at(ref, x, r):
-        return ref[pl.ds(PAD + x * 8 * SLAB + r, 64, stride=OWN), :]
+        return ref[pl.ds(x * 8 * SLAB + r, 64, stride=OWN), :]
 
     u = at(u_ref, outer, row)
-    side = s_ref[pl.ds(row, 64, stride=OWN), :] + at(u_ref, inner, row) + up8(u) + down8(u)
+    side = at(s_ref, outer, row) + at(u_ref, inner, row) + up8(u) + down8(u)
     zero = jnp.zeros((8, LANES), F32)
     side += jnp.concatenate([zero, u[:-8]], 0) + jnp.concatenate([u[8:], zero], 0)
-    parts = [(u, side), (c_ref[pl.ds(row, 64, stride=OWN), :], at(u_ref, outer, extra_row))]
+    parts = [(u, side), (at(c_ref, outer, row), at(u_ref, outer, extra_row))]
     back = lax.rem(LANES - lane, LANES)
     rows = []
     for pair in parts:
@@ -113,78 +114,63 @@
     return jnp.transpose(jnp.broadcast_to(packed, (LANES, LANES)))
 
 
-def faces_kernel(held_ref, state, coef, even_out, odd_out, u, s, c, tail, head, sem):
+def front_kernel(
+    held_ref, _, state, coef,
+    even_out, odd_out, even_rest, odd_rest,
+    tail, head, tail_rest, head_rest, sem,
+):
     held = held_ref[0, 0]
-    rows = 8 * SLAB
-    run_copies(
-        [
-            (state.at[0], u.at[pl.ds(PAD, 8 * rows)]),
-            (state.at[1, pl.ds(0, rows)], s.at[0]),
-            (state.at[1, pl.ds(7 * rows, rows)], s.at[1]),
-            (coef.at[pl.ds(0, rows)], c.at[0]),
-            (coef.at[pl.ds(7 * rows, rows)], c.at[1]),
-        ],
-        sem,
-    )
+    rows = CELLS * OWN
+    u, c = state, coef
+    s = state.at[pl.ds(rows, rows)]
     place = tail_place(held)
+    even = is_even("curve")
+
+    def at(ref, x, y):
+        start = (x * 8 + y) * SLAB
+        return lambda r: ref[pl.ds(start + r, 8, stride=OWN), :]
+
+    def both(x, y, inner):
+        return lambda r: at(u, x, inner)(r) + at(s, x, y)(r)
+
     for plane in range(2):
         for x in range(8):
-            start = PAD + (x * 8 + 7 * plane) * SLAB
-            load = lambda r, start=start: u[pl.ds(start + r, 8, stride=OWN), :]
-            put_zones(load, tail, head, (plane * 8 + x) * 8 * ZONE, place)
+            put_zones(at(u, x, 7 * plane), tail, head, (plane * 8 + x) * 8 * ZONE, place)
     end = held - 1
     row, lane = lax.div(end, LANES), lax.rem(end, LANES)
     edge = 2 * 64 * ZONE
     blank = jnp.zeros((6, LANES), F32)
-    first = edge_rows(u, s.at[0], c.at[0], 0, 0, 0, ZONE)
+    first = edge_rows(u, s, c, 0, 0, 0, ZONE)
     head[pl.ds(edge, 8), :] = jnp.concatenate(first + [blank], 0)
-    last = edge_rows(u, s.at[1], c.at[1], 7, row, lane, row - ZONE)
+    last = edge_rows(u, s, c, 7, row, lane, row - ZONE)
     tail[pl.ds(edge, 8), :] = jnp.concatenate(last + [blank], 0)
-    send_zones(tail, head, even_out, odd_out, sem, is_even("curve"))
-
-
-def rest_kernel(held_ref, state, coef, even_out, odd_out, u, s, c, tail, head, sem):
-    run_copies(
-        [(state.at[0, :, y], u.at[i]) for i, y in enumerate((1, 6))]
-        + [(state.at[1, :, y], s.at[i]) for i, y in enumerate((0, 7))]
-        + [(coef.at[:, y], c.at[i]) for i, y in enumerate((0, 1, 6, 7))],
-        sem,
-    )
-    place = tail_place(held_ref[0, 0])
-
-    def at(ref, i, x):
-        return lambda r: ref[i, x, pl.ds(r, 8, stride=OWN), :]
-
-    def both(i, x):
-        return lambda r: at(u, i, x)(r) + at(s, i, x)(r)
-
-    def body(x, carry):
-        loads = [both(0, x)] + [at(c, i, x) for i in range(4)] + [both(1, x)]
+    for x in range(8):
+        loads = [both(x, 0, 1)] + [at(c, x, y) for y in (0, 1, 6, 7)] + [both(x, 7, 6)]
         for plane, load in enumerate(loads):
-            put_zones(load, tail, head, (plane * 8 + x) * 8 * ZONE, place)
-        return carry
-
-    lax.fori_loop(0, 8, body, 0)
-    send_zones(tail, head, even_out, odd_out, sem, is_even("curve"))
-
-
-def sweep_kernel(held_ref, state, coef, even_in, odd_in, pack, even_out, odd_out, u, s, c, v, w, edges, tail, head, sem):
+            put_zones(load, tail_rest, head_rest, (plane * 8 + x) * 8 * ZONE, place)
+    for flag, a, b, ra, rb in (
+        (even, tail, head, tail_rest, head_rest),
+        (jnp.logical_not(even), head, tail, head_rest, tail_rest),
+    ):
+        @pl.when(flag)
+        def _():
+            run_copies([(a, even_out), (b, odd_out), (ra, even_rest), (rb, odd_rest)], sem)
+
+
+def sweep_kernel(
+    held_ref, _, state, coef, even_in, odd_in,
+    front, pack, even_out, odd_out,
+    v, edges, tail, head, sem,
+):
     held = held_ref[0, 0]
     even = is_even("curve")
     rank, ranks = lax.axis_index("curve"), lax.axis_size("curve")
-    rows = CELLS * OWN
     edge = 2 * 64 * ZONE
-    run_copies(
-        [
-            (state.at[0], u.at[pl.ds(PAD, rows)]),
-            (state.at[1], s),
-            (coef, c),
-        ],
-        sem,
-    )
-    take_zones(
-        even_in.at[pl.ds(edge, 8)], odd_in.at[pl.ds(edge, 8)], edges.at[0], edges.at[1], sem, even
-    )
+    packed = pl.ds(edge, 8)
+    u, c = state, coef
+    s = state.at[pl.ds(CELLS * OWN, CELLS * OWN)]
+    w = pack.at[pl.ds(PAD, CELLS * OWN)]
+    take_zones(even_in.at[packed], odd_in.at[packed], edges.at[0], edges.at[1], sem, even)
     row96 = iota((SLAB, LANES), 0)
     lane96 = iota((SLAB, LANES), 1)
     slot = lax.rem(row96, OWN) * LANES + lane96
@@ -220,10 +206,9 @@
             b = (x * 8 + y) * SLAB
             if not isinstance(b, int):
                 b = pl.multiple_of(b, 8)
-            p = b + PAD
-            total = s[pl.ds(b, SLAB), :] + zsum(u, p) + xsum(u, p, kind)
-            total += u[pl.ds(p - SLAB, SLAB), :] + u[pl.ds(p + SLAB, SLAB), :]
-            v[pl.ds(p, SLAB), :] = total / (6.0 + c[pl.ds(b, SLAB), :])
+            total = s[pl.ds(b, SLAB), :] + zsum(u, b) + xsum(u, b, kind)
+            total += u[pl.ds(b - SLAB, SLAB), :] + u[pl.ds(b + SLAB, SLAB), :]
+            v[pl.ds(b + PAD, SLAB), :] = total / (6.0 + c[pl.ds(b, SLAB), :])
             return carry
 
         lax.fori_loop(1, 7, body, 0)
@@ -244,7 +229,7 @@
         hit = lane == at_lane
         cell = c[plain, :]
         v[place, :] = v[place, :] + jnp.where(hit, a[:64] / (6.0 + cell), 0.0)
-        beyond = (a[64:] + u[place, :]) / (6.0 + b[:64])
+        beyond = (a[64:] + u[plain, :]) / (6.0 + b[:64])
         mine.append(jnp.where(jnp.logical_and(hit, there), beyond, 0.0))
 
     def second(x, kind):
@@ -292,15 +277,29 @@
     place = tail_place(held)
 
     def body(i, carry):
-        load = lambda r: w[pl.ds(i * SLAB + r, 8, stride=OWN), :]
-        put_zones(load, tail, head, pl.multiple_of(i * 8 * ZONE, 8), place)
+        for k in range(8):
+            at = pl.multiple_of((i * 8 + k) * SLAB, 8)
+            load = lambda r, at=at: w[pl.ds(at + r, 8, stride=OWN), :]
+            put_zones(load, tail, head, pl.multiple_of((i * 8 + k) * 8 * ZONE, 8), place)
         return carry
 
-    lax.fori_loop(0, 64, body, 0)
-    save = pltpu.make_async_copy(w, pack, sem.at[7])
-    save.start()
+    lax.fori_loop(0, 8, body, 0)
+
+    def keep(x, carry):
+        def slab(ref, y):
+            return ref[pl.ds(pl.multiple_of((x * 8 + y) * SLAB, 8), SLAB), :]
+
+        for plane, value in enumerate(
+            (
+                slab(u, 0), slab(u, 7), slab(s, 0) + slab(u, 1), slab(c, 0),
+                slab(c, 1), slab(c, 6), slab(c, 7), slab(s, 7) + slab(u, 6),
+            )
+        ):
+            front[pl.ds(pl.multiple_of(PAD + (plane * 8 + x) * SLAB, 8), SLAB), :] = value
+        return carry
+
+    lax.fori_loop(0, 8, keep, 0)
     send_zones(tail, head, even_out, odd_out, sem, even)
-    save.wait()
 
 
 class Window:
@@ -331,18 +330,9 @@
         return jnp.where(self.from_tail, prev, jnp.where(self.from_head, after, mine))
 
 
-def drifts(held_ref, before_ref):
-    rank = lax.axis_index("curve")
-    before = before_ref[0, 0] - rank * AVG
+def drifts(held_ref, before_refs):
+    before = before_refs[0][0, 0] - lax.axis_index("curve") * AVG
     return before, before + held_ref[0, 0] - AVG
-
-
-def face_planes(ref, state_or_coef, planes, where):
-    size = 8 * SLAB
-    return [
-        (state_or_coef.at[:, y], ref.at[pl.ds(PAD + i * size, size)].reshape(8, SLAB, LANES))
-        for y, i in zip(planes, where)
-    ]
 
 
 def send_faces(low, high, even_out, odd_out, sem):
@@ -370,14 +360,13 @@
 
 
 def align_kernel(
-    held_ref, before_ref, state, even_in, odd_in,
+    held_ref, before_refs, own, even_in, odd_in,
     even_out, odd_out, faces, sides,
-    own, tail, head, edges, sem,
+    tail, head, edges, sem,
 ):
-    before, after = drifts(held_ref, before_ref)
+    before, after = drifts(held_ref, before_refs)
     even = is_even("curve")
     edge = 2 * 64 * ZONE
-    run_copies(face_planes(own, state.at[0], (0, 7), (0, 1)), sem)
     zone = pl.ds(PAD, edge)
     take_zones(
         even_in.at[pl.ds(0, edge)], odd_in.at[pl.ds(0, edge)], tail.at[zone], head.at[zone], sem, even
@@ -386,13 +375,15 @@
     take_zones(even_in.at[packed], odd_in.at[packed], edges.at[0], edges.at[1], sem, even)
     here = Window(before, after)
 
-    def body(i, carry):
-        at = PAD + i * OWN
-        zat = PAD + i * ZONE
-        faces[pl.ds(pl.multiple_of(i * WIN, 8), WIN), :] = here(own, at, tail, zat, head, zat)
+    def body(k, carry):
+        for z in range(8):
+            i = k * 8 + z
+            at = PAD + i * OWN
+            zat = PAD + i * ZONE
+            faces[pl.ds(pl.multiple_of(i * WIN, 8), WIN), :] = here(own, at, tail, zat, head, zat)
         return carry
 
-    lax.fori_loop(0, 128, body, 0)
+    lax.fori_loop(0, 16, body, 0)
     lower = Window(before + 1, after + 1)
     upper = Window(before - 1, after - 1)
     j = here.row * LANES + here.lane
@@ -431,31 +422,20 @@
 
 
 def face_kernel(
-    held_ref, before_ref, state, coef, even_in, odd_in, even_face, odd_face, faces, sides,
+    held_ref, before_refs, own, even_in, odd_in, even_face, odd_face, faces, sides,
     even_out, odd_out, even_end, odd_end, new, below, inner,
-    own, tail, head, near, q, ends, sem,
+    tail, head, near, q, ends, sem,
 ):
-    before, after = drifts(held_ref, before_ref)
+    before, after = drifts(held_ref, before_refs)
     even = is_even("curve")
     size = 6 * 64 * ZONE
     half = 64 * WIN
-    run_copies(
-        face_planes(own, state.at[0], (1, 6), (0, 5))
-        + face_planes(own, coef, (0, 1, 6, 7), (1, 2, 3, 4))
-        + face_planes(own, state.at[1], (0, 7), (6, 7)),
-        sem,
-    )
     zone = pl.ds(PAD, size)
     take_zones(even_in, odd_in, tail.at[zone], head.at[zone], sem, even)
     take_faces(even_face, odd_face, near.at[pl.ds(0, half)], near.at[pl.ds(half, half)], sem)
-    for to, more in ((0, 6), (5, 7)):
-        for x in range(8):
-            a = pl.ds(PAD + (to * 8 + x) * SLAB, SLAB)
-            b = pl.ds(PAD + (more * 8 + x) * SLAB, SLAB)
-            own[a, :] = own[a, :] + own[b, :]
     here = Window(before, after)
 
-    def body(i, carry):
+    def body(k, carry):
         for plane, ref, to, add in (
             (0, q, 0, 0.0),
             (5, q, 1, 0.0),
@@ -464,13 +444,15 @@
             (2, inner, 0, 6.0),
             (3, inner, 1, 6.0),
         ):
-            at = PAD + (plane * 64 + i) * OWN
-            zat = PAD + (plane * 64 + i) * ZONE
-            value = here(own, at, tail, zat, head, zat)
-            ref[pl.ds(pl.multiple_of((to * 64 + i) * WIN, 8), WIN), :] = value + add
+            for z in range(8):
+                i = k * 8 + z
+                at = PAD + ((plane + 2) * 64 + i) * OWN
+                zat = PAD + (plane * 64 + i) * ZONE
+                value = here(own, at, tail, zat, head, zat)
+                ref[pl.ds(pl.multiple_of((to * 64 + i) * WIN, 8), WIN), :] = value + add
         return carry
 
-    lax.fori_loop(0, 64, body, 0)
+    lax.fori_loop(0, 8, body, 0)
 
     def run(x, kind):
         for plane in range(2):
@@ -502,22 +484,19 @@
 
 
 def last_kernel(
-    held_ref, before_ref, pack, even_in, odd_in, even_face, odd_face, even_end, odd_end,
+    held_ref, before_refs, own, even_in, odd_in, even_face, odd_face, even_end, odd_end,
     new, below, inner,
     out,
-    own, tail, head, near, ends, sem,
+    tail, head, near, ends, sem,
 ):
-    before, after = drifts(held_ref, before_ref)
+    before, after = drifts(held_ref, before_refs)
     even = is_even("curve")
     size = 8 * 64 * ZONE
     half = 64 * WIN
-    fetch = pltpu.make_async_copy(pack, own.at[pl.ds(PAD, CELLS * OWN)], sem.at[7])
-    fetch.start()
     zone = pl.ds(PAD, size)
     take_zones(even_in, odd_in, tail.at[zone], head.at[zone], sem, even)
     take_zones(even_end, odd_end, ends.at[0], ends.at[1], sem, even)
     take_faces(even_face, odd_face, near.at[pl.ds(0, half)], near.at[pl.ds(half, half)], sem)
-    fetch.wait()
     here = Window(before, after)
     lane, row = here.lane, here.row
 
@@ -572,17 +551,23 @@
 
 
 def swaps(values, axis):
-    return tuple(swapped(value, axis, first) for first, value in enumerate(values))
+    got = []
+    for first, value in enumerate(values):
+        got.append(swapped(value, axis, first))
+    return got
 
 
 def held_before(counts):
     rank, count = lax.axis_index("curve"), lax.axis_size("curve")
-    total, before, bit = counts, jnp.zeros_like(counts), 1
-    while bit < count:
-        other = lax.ppermute(total, "curve", [(i, i ^ bit) for i in range(count) if i ^ bit < count])
-        before += jnp.where(jnp.bitwise_and(rank, bit) != 0, other, 0)
+    places = [i for i in range(count) if 1 << i < count]
+    above = [jnp.bitwise_and(rank >> i, 1).reshape(1, 1) for i in places]
+    total, *above = lax.optimization_barrier((counts, *above))
+    before = jnp.zeros_like(counts)
+    for i in places:
+        pairs = [(a, a ^ 1 << i) for a in range(count) if a ^ 1 << i < count]
+        other = lax.ppermute(total, "curve", pairs)
+        before += above[i] * other
         total += other
-        bit *= 2
     return before
 
 
@@ -590,102 +575,103 @@
     return jax.ShapeDtypeStruct(shape, F32)
 
 
-def call(kernel, outs, ins, scratch, sems=8, vmem_ins=(), vmem_outs=None, scalars=1, cost=4000):
+def call(kernel, outs, ins, scratch, limit, vmem_ins=(), vmem_outs=(), hbm_ins=(), us=2):
+    (held,), others, *arrays = ins
     vmem = pl.BlockSpec(memory_space=pltpu.VMEM)
-    specs = [SMEM] * scalars
-    specs += [vmem if i in vmem_ins else ANY for i in range(scalars, len(ins))]
+    specs = [SMEM] * (1 + len(others))
+    specs += [
+        vmem if i in vmem_ins else HBM if i in hbm_ins else ANY for i in range(len(arrays))
+    ]
+
+    def body(held_ref, *refs):
+        kernel(held_ref, refs[: len(others)], *refs[len(others) :])
+
     return pl.pallas_call(
-        kernel,
+        body,
         out_shape=outs,
         in_specs=specs,
-        out_specs=[vmem if vmem_outs and i in vmem_outs else ANY for i in range(len(outs))],
-        scratch_shapes=[pltpu.VMEM(shape, F32) for shape in scratch] + [pltpu.SemaphoreType.DMA((sems,))],
-        compiler_params=pltpu.CompilerParams(vmem_limit_bytes=40 * 2**20),
-        cost_estimate=pl.CostEstimate(flops=cost * 4000, bytes_accessed=cost * 1000, transcendentals=0),
-    )(*ins)
+        out_specs=[vmem if i in vmem_outs else ANY for i in range(len(outs))],
+        scratch_shapes=[pltpu.VMEM(shape, F32) for shape in scratch] + [pltpu.SemaphoreType.DMA((8,))],
+        compiler_params=pltpu.CompilerParams(vmem_limit_bytes=limit * 2**20),
+        cost_estimate=pl.CostEstimate(flops=us * 4_000_000, bytes_accessed=us * 10**6, transcendentals=0),
+    )(held, *others, *arrays)
 
 
 def local(state, coef, counts):
-    state3 = state.reshape(2, CELLS * OWN, LANES)
+    state2 = state.reshape(2 * CELLS * OWN, LANES)
     coef2 = coef.reshape(CELLS * OWN, LANES)
-    state5 = state.reshape(2, 8, 8, SLAB, LANES)
-    coef4 = coef.reshape(8, 8, SLAB, LANES)
     rows = CELLS * OWN
-    step = 8 * SLAB
     zone = 64 * ZONE
     win = 64 * WIN
 
-    before = held_before(counts)
-    message = (2 * zone + 8, LANES)
-    faces_out = call(
-        faces_kernel,
-        [array(*message)] * 2,
-        (counts, state3, coef2),
-        [(rows + 2 * PAD, LANES), (2, step, LANES), (2, step, LANES), message, message],
+    others = (held_before(counts),)
+    message, rest = (2 * zone + 8, LANES), (6 * zone, LANES)
+    *faces_out, rest_a, rest_b = call(
+        front_kernel,
+        [array(*message)] * 2 + [array(*rest)] * 2,
+        ((counts,), (), state2, coef2),
+        [message, message, rest, rest],
+        limit=4,
+        vmem_ins=(0, 1),
     )
     faces_in = swaps(faces_out, "curve")
-    message = (6 * zone, LANES)
-    rest_out = call(
-        rest_kernel,
-        [array(*message)] * 2,
-        (counts, state5, coef4),
-        [(2, 8, SLAB, LANES), (2, 8, SLAB, LANES), (4, 8, SLAB, LANES), message, message],
-    )
-    rest_in = swaps(rest_out, "curve")
+    rest_in = swaps((rest_a, rest_b), "curve")
     message = (8 * zone, LANES)
-    pack, *sweep_out = call(
+    front, pack, *sweep_out = call(
         sweep_kernel,
-        [array(rows, LANES)] + [array(*message)] * 2,
-        (counts, state3, coef2, *faces_in),
-        [
-            (rows + 2 * PAD, LANES), (rows, LANES), (rows, LANES), (rows + 2 * PAD, LANES),
-            (rows, LANES), (2, 8, LANES), message, message,
-        ],
+        [array(rows + 2 * PAD, LANES)] * 2 + [array(*message)] * 2,
+        ((counts,), (), state2, coef2, *faces_in),
+        [(rows + 2 * PAD, LANES), (2, 8, LANES), message, message],
+        limit=24,
+        vmem_ins=(0, 1),
+        vmem_outs=(0, 1),
+        us=6,
     )
     sweep_in = swaps(sweep_out, "curve")
     *near_out, faces, sides = call(
         align_kernel,
         [array(win, LANES)] * 2 + [array(2 * win, LANES), array(32 * WIN, LANES)],
-        (counts, before, state5, *faces_in),
-        [
-            (2 * step + 2 * PAD, LANES), (2 * zone + 2 * PAD, LANES), (2 * zone + 2 * PAD, LANES),
-            (2, 8, LANES),
-        ],
+        ((counts,), others, front, *faces_in),
+        [(2 * zone + 2 * PAD, LANES), (2 * zone + 2 * PAD, LANES), (2, 8, LANES)],
+        limit=8,
+        vmem_ins=(0,),
         vmem_outs=(2, 3),
-        scalars=2,
     )
     near_in = swaps(near_out, "grp")
     near_a, near_b, end_a, end_b, new, below, inner = call(
         face_kernel,
         [array(win, LANES)] * 2 + [array(16, LANES)] * 2 + [array(2 * win, LANES)] * 3,
-        (counts, before, state5, coef4, *rest_in, *near_in, faces, sides),
+        ((counts,), others, front, *rest_in, *near_in, faces, sides),
         [
-            (8 * step + 2 * PAD, LANES), (6 * zone + 2 * PAD, LANES), (6 * zone + 2 * PAD, LANES),
+            (6 * zone + 2 * PAD, LANES), (6 * zone + 2 * PAD, LANES),
             (2 * win, LANES), (2 * win, LANES), (2, 16, LANES),
         ],
-        vmem_ins=(8, 9),
+        limit=8,
+        vmem_ins=(0, 5, 6),
         vmem_outs=(4, 5, 6),
-        scalars=2,
+        us=3,
     )
     near_in = swaps((near_a, near_b), "grp")
     end_in = swaps((end_a, end_b), "curve")
     (out,) = call(
         last_kernel,
         [array(CELLS * WIN, LANES)],
-        (counts, before, pack, *sweep_in, *near_in, *end_in, new, below, inner),
+        ((counts,), others, pack, *sweep_in, *near_in, *end_in, new, below, inner),
         [
-            (rows + 2 * PAD, LANES), (8 * zone + 2 * PAD, LANES), (8 * zone + 2 * PAD, LANES),
+            (8 * zone + 2 * PAD, LANES), (8 * zone + 2 * PAD, LANES),
             (2 * win, LANES), (2, 16, LANES),
         ],
-        vmem_ins=(9, 10, 11),
+        limit=12,
+        vmem_ins=(0, 7, 8, 9),
         vmem_outs=(0,),
-        scalars=2,
+        us=3,
     )
     return out.reshape(CELLS, 1, AVG)
 
 
 def solution(mesh):
     placed = (P(None, None, "grp", "curve"), P(None, "grp", "curve"), P("grp", "curve"))
+
     return jax.shard_map(
         local, mesh=mesh, in_specs=placed, out_specs=P(None, "grp", "curve"), check_vma=False
     )

time: 103 us -> 90.2 us (0.88)
  the two profiles are of different devices: /device:TPU:12 before, /device:TPU:6 now
where the time goes in v2:
time: 90.2 us; the launch traced here: 89.8 us
  waiting for transfers between devices  31.6 us (35%)
  starting transfers between devices  30.3 us (34%)
  Pallas kernels  16.5 us (18%)
  local copies, waits for them, and re-layouts  7.45 us (8%)
  between operations  4.04 us (4%)
    ppermute x12, starting transfers between devices, swapped(): return lax.ppermute(value, axis, pairs + [(b, a) for a, b in pairs])  23.3 us
    ppermute x3, waiting for transfers between devices, held_before(): other = lax.ppermute(total, 'curve', pairs)  16.6 us
    pallas_call x5, Pallas kernels, call(): pl.pallas_call(body, out_shape=outs, in_specs=specs, out_specs=[vmem if i...  16.5 us
    ppermute x12, waiting for transfers between devices, swapped(): return lax.ppermute(value, axis, pairs + [(b, a) for a, b in pairs])  15 us
    unnamed x8, local copies, waits for them, and re-layouts  7.45 us
    ppermute x3, starting transfers between devices, held_before(): other = lax.ppermute(total, 'curve', pairs)  6.96 us
  transfers between devices with their start and end apart: 15, of which 4 were waited for; matrix products, arithmetic and copies ran while one was open for 0% of the time, Pallas kernels for 12%

profile of v2, /device:TPU:6, one launch (start us, length us, event | category | flops | bytes accessed | tf_op | source)
XLA Modules:
  0.0 89.8 jit_solution(17206744785018599767)
XLA Ops:
  0.7 2.8 %copy-done = f32[2,512,1,1536]{3,2,1,0:T(1,128)S(1)} copy-done((f32[2,512,1,1536]{3,2,1,0:T(1,128)S(1)}, f32[2,512,1,1536]{3,2,1,0:T(1,128)}, u32[]{:S(2)}) %copy-start) | copy-done | bytes 6291480
  3.4 1.9 %copy-done.2 = f32[512,1,1536]{2,1,0:T(1,128)S(1)} copy-done((f32[512,1,1536]{2,1,0:T(1,128)S(1)}, f32[512,1,1536]{2,1,0:T(1,128)}, u32[]{:S(2)}) %copy-start.2) | copy-done | bytes 3145752
  5.3 1.5 %shard_map.37 = (f32[264,128]{1,0:T(8,128)}, f32[264,128]{1,0:T(8,128)S(1)}, f32[768,128]{1,0:T(8,128)}, f32[768,128]{1,0:T(8,128)}) custom-call(s32[1,1]{1,0:T(1,128)S(6)} %copy.5.held_ref, f32[12288,128]{1,0:T(8,128)S(1)} %bitcast.6, f32[6144,128]{1,0:T(8,128)S(1)} %bitcast.8), custom_call_target="tpu_custom_call" | custom-call | flops 8000000 | bytes 2000000 | tf_op jit(solution)/shard_map/pallas_call | solution.py:589
  6.8 0.6 collective-permute-start.7
  7.4 1.5 %collective-permute-start.3 = (f32[264,128]{1,0:T(8,128)}, f32[264,128]{1,0:T(8,128)S(1)}, u32[]{:S(2)}, u32[]{:S(2)}) collective-permute-start(f32[264,128]{1,0:T(8,128)} %get-tuple-element.32), channel_id=1, source_target_pairs={{0,4},{8,12},{16,20},{24,28},{4,0},{12,8},{20,16},{28,24},{1,5},{9... | collective-permute-start | bytes 405512 | tf_op jit(solution)/shard_map/ppermute | solution.py:550
  8.9 3.4 %collective-permute-start.4 = (f32[264,128]{1,0:T(8,128)S(1)}, f32[264,128]{1,0:T(8,128)S(1)}, u32[]{:S(2)}, u32[]{:S(2)}) collective-permute-start(f32[264,128]{1,0:T(8,128)S(1)} %get-tuple-element.33), channel_id=1, source_target_pairs={{4,8},{12,16},{20,24},{8,4},{16,12},{24,20},{5,9},{13,17},{21,25},... | collective-permute-start | bytes 405512 | tf_op jit(solution)/shard_map/ppermute | solution.py:550
  12.4 3.3 %collective-permute-start.8 = (f32[768,128]{1,0:T(8,128)}, f32[768,128]{1,0:T(8,128)}, u32[]{:S(2)}, u32[]{:S(2)}) collective-permute-start(f32[768,128]{1,0:T(8,128)} %get-tuple-element.39), channel_id=1, source_target_pairs={{4,8},{12,16},{20,24},{8,4},{16,12},{24,20},{5,9},{13,17},{21,25},... | collective-permute-start | bytes 1179656 | tf_op jit(solution)/shard_map/ppermute | solution.py:550
  15.8 16.5 %collective-permute-done = s32[1,1]{1,0:T(1,128)} collective-permute-done((s32[1,1]{1,0:T(1,128)}, s32[1,1]{1,0:T(1,128)}, u32[]{:S(2)}, u32[]{:S(2)}) %collective-permute-start) | collective-permute-done | bytes 36 | tf_op jit(solution)/shard_map/ppermute | solution.py:568
  32.9 2.9 %collective-permute-start.1 = (s32[1,1]{1,0:T(1,128)}, s32[1,1]{1,0:T(1,128)}, u32[]{:S(2)}, u32[]{:S(2)}) collective-permute-start(s32[1,1]{1,0:T(1,128)} %add.12), channel_id=1, source_target_pairs={{0,8},{4,12},{8,0},{12,4},{16,24},{20,28},{24,16},{28,20},{1,9},{5... | collective-permute-start | bytes 20 | tf_op jit(solution)/shard_map/ppermute | solution.py:568
  37.2 4.0 %collective-permute-start.2 = (s32[1,1]{1,0:T(1,128)}, s32[1,1]{1,0:T(1,128)}, u32[]{:S(2)}, u32[]{:S(2)}) collective-permute-start(s32[1,1]{1,0:T(1,128)} %add.14), channel_id=1, source_target_pairs={{0,16},{4,20},{8,24},{12,28},{16,0},{20,4},{24,8},{28,12},{1,17},{... | collective-permute-start | bytes 20 | tf_op jit(solution)/shard_map/ppermute | solution.py:568
  42.4 2.8 %copy-done.1 = f32[2,512,1,1536]{3,2,1,0:T(1,128)S(1)} copy-done((f32[2,512,1,1536]{3,2,1,0:T(1,128)S(1)}, f32[2,512,1,1536]{3,2,1,0:T(1,128)}, u32[]{:S(2)}) %copy-start.1) | copy-done | bytes 6291480
  45.2 5.2 %shard_map.38 = (f32[6176,128]{1,0:T(8,128)S(1)}, f32[6176,128]{1,0:T(8,128)S(1)}, f32[1024,128]{1,0:T(8,128)S(1)}, f32[1024,128]{1,0:T(8,128)S(1)}) custom-call(s32[1,1]{1,0:T(1,128)S(6)} %copy.5.held_ref, f32[12288,128]{1,0:T(8,128)S(1)} %bitcast.7, f32[6144,128]{1,0:T(8,128)S(1)} %bitcast.9, f32[264,128]{1,0:T(8,128)S(1)} %collective-permute-done.3.refs_2_, ...), custom_call_target="tpu_custom_call" | custom-call | flops 24000000 | bytes 6000000 | tf_op jit(solution)/shard_map/pallas_call | solution.py:589
  50.4 2.3 %shard_map.39 = (f32[512,128]{1,0:T(8,128)S(1)}, f32[512,128]{1,0:T(8,128)S(1)}, f32[1024,128]{1,0:T(8,128)S(1)}, f32[256,128]{1,0:T(8,128)S(1)}) custom-call(s32[1,1]{1,0:T(1,128)S(6)} %copy.5.held_ref, s32[1,1]{1,0:T(1,128)S(6)} %add.15.refs_0_, f32[6176,128]{1,0:T(8,128)S(1)} %get-tuple-element.37.refs_1_, f32[264,128]{1,0:T(8,128)S(1)} %collective-permute-done.3.refs_2_, ...), custom_call_target="tpu_custom_call" | custom-call | flops 8000000 | bytes 2000000 | tf_op jit(solution)/shard_map/pallas_call | solution.py:589
  52.8 2.5 %collective-permute-start.10 = (f32[512,128]{1,0:T(8,128)S(1)}, f32[512,128]{1,0:T(8,128)S(1)}, u32[]{:S(2)}, u32[]{:S(2)}) collective-permute-start(f32[512,128]{1,0:T(8,128)S(1)} %get-tuple-element.41), channel_id=1, source_target_pairs={{1,2},{2,1},{5,6},{6,5},{9,10},{10,9},{13,14},{14,13},{17,18},{18,... | collective-permute-start | bytes 786440 | tf_op jit(solution)/shard_map/ppermute | solution.py:550
  55.3 0.6 collective-permute-start.5
  55.9 4.4 %collective-permute-start.6 = (f32[1024,128]{1,0:T(8,128)S(1)}, f32[1024,128]{1,0:T(8,128)S(1)}, u32[]{:S(2)}, u32[]{:S(2)}) collective-permute-start(f32[1024,128]{1,0:T(8,128)S(1)} %get-tuple-element.36), channel_id=1, source_target_pairs={{4,8},{12,16},{20,24},{8,4},{16,12},{24,20},{5,9},{13,17},{21,25},... | collective-permute-start | bytes 1572872 | tf_op jit(solution)/shard_map/ppermute | solution.py:550
  60.3 0.1 collective-permute-done.10.refs_5_
  60.5 3.5 %shard_map.40 = (f32[512,128]{1,0:T(8,128)S(1)}, f32[512,128]{1,0:T(8,128)S(1)}, f32[16,128]{1,0:T(8,128)S(1)}, f32[16,128]{1,0:T(8,128)S(1)}, f32[1024,128]{1,0...) custom-call(s32[1,1]{1,0:T(1,128)S(6)} %copy.5.held_ref, s32[1,1]{1,0:T(1,128)S(6)} %add.15.refs_0_, ...), custom_call_target="tpu_custom_call" | custom-call | flops 12000000 | bytes 3000000 | tf_op jit(solution)/shard_map/pallas_call | solution.py:589
  64.0 2.8 %collective-permute-start.12 = (f32[512,128]{1,0:T(8,128)S(1)}, f32[512,128]{1,0:T(8,128)S(1)}, u32[]{:S(2)}, u32[]{:S(2)}) collective-permute-start(f32[512,128]{1,0:T(8,128)S(1)} %get-tuple-element.45), channel_id=1, source_target_pairs={{1,2},{2,1},{5,6},{6,5},{9,10},{10,9},{13,14},{14,13},{17,18},{18,... | collective-permute-start | bytes 786440 | tf_op jit(solution)/shard_map/ppermute | solution.py:550
  66.8 0.6 collective-permute-start.13
  67.4 11.8 %collective-permute-done.13.refs_6_ = f32[16,128]{1,0:T(8,128)S(1)} collective-permute-done((f32[16,128]{1,0:T(8,128)S(1)}, f32[16,128]{1,0:T(8,128)S(1)}, u32[]{:S(2)}, u32[]{:S(2)}) %collective-permute-start.13) | collective-permute-done | bytes 8224 | tf_op jit(solution)/shard_map/ppermute | solution.py:550
  79.3 3.4 %collective-permute-start.14 = (f32[16,128]{1,0:T(8,128)S(1)}, f32[16,128]{1,0:T(8,128)S(1)}, u32[]{:S(2)}, u32[]{:S(2)}) collective-permute-start(f32[16,128]{1,0:T(8,128)S(1)} %get-tuple-element.47), channel_id=1, source_target_pairs={{4,8},{12,16},{20,24},{8,4},{16,12},{24,20},{5,9},{13,17},{21,25},... | collective-permute-start | bytes 24584 | tf_op jit(solution)/shard_map/ppermute | solution.py:550
  82.7 3.0 %collective-permute-done.14.refs_7_ = f32[16,128]{1,0:T(8,128)S(1)} collective-permute-done((f32[16,128]{1,0:T(8,128)S(1)}, f32[16,128]{1,0:T(8,128)S(1)}, u32[]{:S(2)}, u32[]{:S(2)}) %collective-permute-start.14) | collective-permute-done | bytes 8224 | tf_op jit(solution)/shard_map/ppermute | solution.py:550
  85.7 4.1 %shard_map.41 = f32[4096,128]{1,0:T(8,128)} custom-call(s32[1,1]{1,0:T(1,128)S(6)} %copy.5.held_ref, s32[1,1]{1,0:T(1,128)S(6)} %add.15.refs_0_, f32[6176,128]{1,0:T(8,128)S(1)} %get-tuple-element.34.refs_1_, f32[1024,128]{1,0:T(8,128)S(1)} %collective-permute-done.5.refs_2_, f32[1024,128]{1,0:T(8,128)S(1)} %collective-permute-done.6.refs_3_, ...), custom_call_target="tpu_custom_call" | custom-call | flops 12000000 | bytes 3000000 | tf_op jit(solution)/shard_map/pallas_call | solution.py:589
  (19 shorter events, 0.3 us)
Async XLA Ops:
  0.7 2.8 %copy-start = (f32[2,512,1,1536]{3,2,1,0:T(1,128)S(1)}, f32[2,512,1,1536]{3,2,1,0:T(1,128)}, u32[]{:S(2)}) copy-start(f32[2,512,1,1536]{3,2,1,0:T(1,128)} %param.3) | copy-start | bytes 18874372
  3.4 1.9 %copy-start.2 = (f32[512,1,1536]{2,1,0:T(1,128)S(1)}, f32[512,1,1536]{2,1,0:T(1,128)}, u32[]{:S(2)}) copy-start(f32[512,1,1536]{2,1,0:T(1,128)} %param.4) | copy-start | bytes 9437188
  5.3 37.1 %copy-start.3 = (f32[512,1,1536]{2,1,0:T(1,128)S(1)}, f32[512,1,1536]{2,1,0:T(1,128)}, u32[]{:S(2)}) copy-start(f32[512,1,1536]{2,1,0:T(1,128)} %param.4) | copy-start | bytes 9437188
  6.8 49.1 %collective-permute-start.7 = (f32[768,128]{1,0:T(8,128)}, f32[768,128]{1,0:T(8,128)}, u32[]{:S(2)}, u32[]{:S(2)}) collective-permute-start(f32[768,128]{1,0:T(8,128)} %get-tuple-element.38), channel_id=1, source_target_pairs={{0,4},{8,12},{16,20},{24,28},{4,0},{12,8},{20,16},{28,24},{1,5},{9... | collective-permute-start | bytes 1179656 | tf_op jit(solution)/shard_map/ppermute | solution.py:550
  7.4 35.0 %collective-permute-start.3 = (f32[264,128]{1,0:T(8,128)}, f32[264,128]{1,0:T(8,128)S(1)}, u32[]{:S(2)}, u32[]{:S(2)}) collective-permute-start(f32[264,128]{1,0:T(8,128)} %get-tuple-element.32), channel_id=1, source_target_pairs={{0,4},{8,12},{16,20},{24,28},{4,0},{12,8},{20,16},{28,24},{1,5},{9... | collective-permute-start | bytes 405512 | tf_op jit(solution)/shard_map/ppermute | solution.py:550
  8.9 33.5 %collective-permute-start.4 = (f32[264,128]{1,0:T(8,128)S(1)}, f32[264,128]{1,0:T(8,128)S(1)}, u32[]{:S(2)}, u32[]{:S(2)}) collective-permute-start(f32[264,128]{1,0:T(8,128)S(1)} %get-tuple-element.33), channel_id=1, source_target_pairs={{4,8},{12,16},{20,24},{8,4},{16,12},{24,20},{5,9},{13,17},{21,25},... | collective-permute-start | bytes 405512 | tf_op jit(solution)/shard_map/ppermute | solution.py:550
  12.4 47.9 %collective-permute-start.8 = (f32[768,128]{1,0:T(8,128)}, f32[768,128]{1,0:T(8,128)}, u32[]{:S(2)}, u32[]{:S(2)}) collective-permute-start(f32[768,128]{1,0:T(8,128)} %get-tuple-element.39), channel_id=1, source_target_pairs={{4,8},{12,16},{20,24},{8,4},{16,12},{24,20},{5,9},{13,17},{21,25},... | collective-permute-start | bytes 1179656 | tf_op jit(solution)/shard_map/ppermute | solution.py:550
  15.7 16.6 %collective-permute-start = (s32[1,1]{1,0:T(1,128)}, s32[1,1]{1,0:T(1,128)}, u32[]{:S(2)}, u32[]{:S(2)}) collective-permute-start(s32[1,1]{1,0:T(1,128)} %param.5), channel_id=1, source_target_pairs={{0,4},{4,0},{8,12},{12,8},{16,20},{20,16},{24,28},{28,24},{1,5},{5... | collective-permute-start | bytes 20 | tf_op jit(solution)/shard_map/ppermute | solution.py:568
  32.9 3.6 %collective-permute-start.1 = (s32[1,1]{1,0:T(1,128)}, s32[1,1]{1,0:T(1,128)}, u32[]{:S(2)}, u32[]{:S(2)}) collective-permute-start(s32[1,1]{1,0:T(1,128)} %add.12), channel_id=1, source_target_pairs={{0,8},{4,12},{8,0},{12,4},{16,24},{20,28},{24,16},{28,20},{1,9},{5... | collective-permute-start | bytes 20 | tf_op jit(solution)/shard_map/ppermute | solution.py:568
  37.2 4.6 %collective-permute-start.2 = (s32[1,1]{1,0:T(1,128)}, s32[1,1]{1,0:T(1,128)}, u32[]{:S(2)}, u32[]{:S(2)}) collective-permute-start(s32[1,1]{1,0:T(1,128)} %add.14), channel_id=1, source_target_pairs={{0,16},{4,20},{8,24},{12,28},{16,0},{20,4},{24,8},{28,12},{1,17},{... | collective-permute-start | bytes 20 | tf_op jit(solution)/shard_map/ppermute | solution.py:568
  42.4 2.8 %copy-start.1 = (f32[2,512,1,1536]{3,2,1,0:T(1,128)S(1)}, f32[2,512,1,1536]{3,2,1,0:T(1,128)}, u32[]{:S(2)}) copy-start(f32[2,512,1,1536]{3,2,1,0:T(1,128)} %param.3) | copy-start | bytes 18874372
  52.7 7.6 %collective-permute-start.9 = (f32[512,128]{1,0:T(8,128)S(1)}, f32[512,128]{1,0:T(8,128)S(1)}, u32[]{:S(2)}, u32[]{:S(2)}) collective-permute-start(f32[512,128]{1,0:T(8,128)S(1)} %get-tuple-element.40), channel_id=1, source_target_pairs={{0,1},{2,3},{1,0},{3,2},{4,5},{6,7},{5,4},{7,6},{8,9},{10,11},{9,8... | collective-permute-start | bytes 786440 | tf_op jit(solution)/shard_map/ppermute | solution.py:550
  52.8 7.7 %collective-permute-start.10 = (f32[512,128]{1,0:T(8,128)S(1)}, f32[512,128]{1,0:T(8,128)S(1)}, u32[]{:S(2)}, u32[]{:S(2)}) collective-permute-start(f32[512,128]{1,0:T(8,128)S(1)} %get-tuple-element.41), channel_id=1, source_target_pairs={{1,2},{2,1},{5,6},{6,5},{9,10},{10,9},{13,14},{14,13},{17,18},{18,... | collective-permute-start | bytes 786440 | tf_op jit(solution)/shard_map/ppermute | solution.py:550
  55.3 30.4 %collective-permute-start.5 = (f32[1024,128]{1,0:T(8,128)S(1)}, f32[1024,128]{1,0:T(8,128)S(1)}, u32[]{:S(2)}, u32[]{:S(2)}) collective-permute-start(f32[1024,128]{1,0:T(8,128)S(1)} %get-tuple-element.35), channel_id=1, source_target_pairs={{0,4},{8,12},{16,20},{24,28},{4,0},{12,8},{20,16},{28,24},{1,5},{9... | collective-permute-start | bytes 1572872 | tf_op jit(solution)/shard_map/ppermute | solution.py:550
  55.9 29.8 %collective-permute-start.6 = (f32[1024,128]{1,0:T(8,128)S(1)}, f32[1024,128]{1,0:T(8,128)S(1)}, u32[]{:S(2)}, u32[]{:S(2)}) collective-permute-start(f32[1024,128]{1,0:T(8,128)S(1)} %get-tuple-element.36), channel_id=1, source_target_pairs={{4,8},{12,16},{20,24},{8,4},{16,12},{24,20},{5,9},{13,17},{21,25},... | collective-permute-start | bytes 1572872 | tf_op jit(solution)/shard_map/ppermute | solution.py:550
  63.9 21.8 %collective-permute-start.11 = (f32[512,128]{1,0:T(8,128)S(1)}, f32[512,128]{1,0:T(8,128)S(1)}, u32[]{:S(2)}, u32[]{:S(2)}) collective-permute-start(f32[512,128]{1,0:T(8,128)S(1)} %get-tuple-element.44), channel_id=1, source_target_pairs={{0,1},{2,3},{1,0},{3,2},{4,5},{6,7},{5,4},{7,6},{8,9},{10,11},{9,8... | collective-permute-start | bytes 786440 | tf_op jit(solution)/shard_map/ppermute | solution.py:550
  64.0 21.7 %collective-permute-start.12 = (f32[512,128]{1,0:T(8,128)S(1)}, f32[512,128]{1,0:T(8,128)S(1)}, u32[]{:S(2)}, u32[]{:S(2)}) collective-permute-start(f32[512,128]{1,0:T(8,128)S(1)} %get-tuple-element.45), channel_id=1, source_target_pairs={{1,2},{2,1},{5,6},{6,5},{9,10},{10,9},{13,14},{14,13},{17,18},{18,... | collective-permute-start | bytes 786440 | tf_op jit(solution)/shard_map/ppermute | solution.py:550
  66.8 12.4 %collective-permute-start.13 = (f32[16,128]{1,0:T(8,128)S(1)}, f32[16,128]{1,0:T(8,128)S(1)}, u32[]{:S(2)}, u32[]{:S(2)}) collective-permute-start(f32[16,128]{1,0:T(8,128)S(1)} %get-tuple-element.46), channel_id=1, source_target_pairs={{0,4},{8,12},{16,20},{24,28},{4,0},{12,8},{20,16},{28,24},{1,5},{9... | collective-permute-start | bytes 24584 | tf_op jit(solution)/shard_map/ppermute | solution.py:550
  79.3 6.4 %collective-permute-start.14 = (f32[16,128]{1,0:T(8,128)S(1)}, f32[16,128]{1,0:T(8,128)S(1)}, u32[]{:S(2)}, u32[]{:S(2)}) collective-permute-start(f32[16,128]{1,0:T(8,128)S(1)} %get-tuple-element.47), channel_id=1, source_target_pairs={{4,8},{12,16},{20,24},{8,4},{16,12},{24,20},{5,9},{13,17},{21,25},... | collective-permute-start | bytes 24584 | tf_op jit(solution)/shard_map/ppermute | solution.py:550

commit v3 on v2

--- a/solution.py
+++ b/solution.py
@@ -17,6 +17,7 @@
 SLAB = 8 * OWN
 CELLS = 512
 PAD = 16
+PLANE = 64 * ZONE
 F32 = jnp.float32
 ANY = pl.BlockSpec(memory_space=pl.ANY)
 HBM = pl.BlockSpec(memory_space=pltpu.HBM)
@@ -114,10 +115,21 @@
     return jnp.transpose(jnp.broadcast_to(packed, (LANES, LANES)))
 
 
+def end_curves():
+    curve = lax.axis_index("grp")
+    return curve == 0, curve == lax.axis_size("grp") - 1
+
+
+def plane_of(inner, low, high):
+    first, last = end_curves()
+    plane = jnp.where(first, high, jnp.where(last, low, inner))
+    return pl.multiple_of(plane * PLANE, 8)
+
+
 def front_kernel(
     held_ref, _, state, coef,
-    even_out, odd_out, even_rest, odd_rest,
-    tail, head, tail_rest, head_rest, sem,
+    even_1, odd_1, even_3, odd_3,
+    tail, head, tail_edge, head_edge, sem,
 ):
     held = held_ref[0, 0]
     rows = CELLS * OWN
@@ -125,6 +137,13 @@
     s = state.at[pl.ds(rows, rows)]
     place = tail_place(held)
     even = is_even("curve")
+    end = held - 1
+    row, lane = lax.div(end, LANES), lax.rem(end, LANES)
+    blank = jnp.zeros((6, LANES), F32)
+    first = edge_rows(u, s, c, 0, 0, 0, ZONE)
+    head_edge[...] = jnp.concatenate(first + [blank], 0)
+    last = edge_rows(u, s, c, 7, row, lane, row - ZONE)
+    tail_edge[...] = jnp.concatenate(last + [blank], 0)
 
     def at(ref, x, y):
         start = (x * 8 + y) * SLAB
@@ -133,51 +152,65 @@
     def both(x, y, inner):
         return lambda r: at(u, x, inner)(r) + at(s, x, y)(r)
 
-    for plane in range(2):
-        for x in range(8):
-            put_zones(at(u, x, 7 * plane), tail, head, (plane * 8 + x) * 8 * ZONE, place)
-    end = held - 1
-    row, lane = lax.div(end, LANES), lax.rem(end, LANES)
-    edge = 2 * 64 * ZONE
-    blank = jnp.zeros((6, LANES), F32)
-    first = edge_rows(u, s, c, 0, 0, 0, ZONE)
-    head[pl.ds(edge, 8), :] = jnp.concatenate(first + [blank], 0)
-    last = edge_rows(u, s, c, 7, row, lane, row - ZONE)
-    tail[pl.ds(edge, 8), :] = jnp.concatenate(last + [blank], 0)
     for x in range(8):
-        loads = [both(x, 0, 1)] + [at(c, x, y) for y in (0, 1, 6, 7)] + [both(x, 7, 6)]
+        loads = [at(u, x, 0), at(u, x, 7), both(x, 0, 1), both(x, 7, 6)]
+        loads += [at(c, x, y) for y in (0, 1, 7, 6)]
         for plane, load in enumerate(loads):
-            put_zones(load, tail_rest, head_rest, (plane * 8 + x) * 8 * ZONE, place)
-    for flag, a, b, ra, rb in (
-        (even, tail, head, tail_rest, head_rest),
-        (jnp.logical_not(even), head, tail, head_rest, tail_rest),
+            put_zones(load, tail, head, (plane * 8 + x) * 8 * ZONE, place)
+
+    def out(zone, edge, message_1, message_3):
+        return [
+            (zone.at[pl.ds(plane_of(0, 0, 1), PLANE)], message_1.at[pl.ds(0, PLANE)]),
+            (zone.at[pl.ds(plane_of(1, 2, 3), PLANE)], message_1.at[pl.ds(PLANE, PLANE)]),
+            (zone.at[pl.ds(plane_of(2, 4, 6), 2 * PLANE)], message_1.at[pl.ds(2 * PLANE, 2 * PLANE)]),
+            (edge, message_1.at[pl.ds(4 * PLANE, 8)]),
+            (zone.at[pl.ds(4 * PLANE, 4 * PLANE)], message_3),
+        ]
+
+    for flag, t, h in (
+        (even, (even_1, even_3), (odd_1, odd_3)),
+        (jnp.logical_not(even), (odd_1, odd_3), (even_1, even_3)),
     ):
         @pl.when(flag)
         def _():
-            run_copies([(a, even_out), (b, odd_out), (ra, even_rest), (rb, odd_rest)], sem)
+            run_copies(out(tail, tail_edge, *t) + out(head, head_edge, *h), sem)
+
+
+def take_edges(even_1, odd_1, edges, sem):
+    rows = pl.ds(4 * PLANE, 8)
+    take_zones(even_1.at[rows], odd_1.at[rows], edges.at[0], edges.at[1], sem, is_even("curve"))
+
+
+def by_parity(evens, odds, tail, head, copies_in, sem):
+    even = is_even("curve")
+    for flag, t, h in ((even, odds, evens), (jnp.logical_not(even), evens, odds)):
+        @pl.when(flag)
+        def _():
+            run_copies(copies_in(tail, *t) + copies_in(head, *h), sem)
+
+
+def to_plane(zone, start, count=1):
+    return zone.at[pl.ds(pl.multiple_of(PAD + start, 8), count * PLANE)]
 
 
 def sweep_kernel(
-    held_ref, _, state, coef, even_in, odd_in,
-    front, pack, even_out, odd_out,
-    v, edges, tail, head, sem,
+    held_ref, _, state, coef,
+    front, pack, ends,
+    v, sem,
 ):
     held = held_ref[0, 0]
-    even = is_even("curve")
-    rank, ranks = lax.axis_index("curve"), lax.axis_size("curve")
-    edge = 2 * 64 * ZONE
-    packed = pl.ds(edge, 8)
+    first_curve, last_curve = end_curves()
+    outer_sides = ((first_curve, 0, 1), (last_curve, 7, 6))
     u, c = state, coef
     s = state.at[pl.ds(CELLS * OWN, CELLS * OWN)]
     w = pack.at[pl.ds(PAD, CELLS * OWN)]
-    take_zones(even_in.at[packed], odd_in.at[packed], edges.at[0], edges.at[1], sem, even)
     row96 = iota((SLAB, LANES), 0)
     lane96 = iota((SLAB, LANES), 1)
     slot = lax.rem(row96, OWN) * LANES + lane96
     zlast, zfirst = row96 >= SLAB - OWN, row96 < OWN
     last_lane, first_lane = lane96 == LANES - 1, lane96 == 0
     starts = slot == 0
-    ends = slot == held - 1
+    finish = slot == held - 1
 
     def zsum(ref, b):
         up = jnp.where(zlast, 0.0, ref[pl.ds(b + OWN, SLAB), :])
@@ -192,7 +225,7 @@
 
     def right(ref, b):
         both = jnp.where(first_lane, ref[pl.ds(b + 1, SLAB), :], ref[pl.ds(b, SLAB), :])
-        return jnp.where(ends, 0.0, pltpu.roll(both, LANES - 1, 1))
+        return jnp.where(finish, 0.0, pltpu.roll(both, LANES - 1, 1))
 
     def xsum(ref, b, kind):
         if kind == 0:
@@ -215,22 +248,24 @@
 
     each_x(first)
 
-    end_row, end_lane = lax.div(held - 1, LANES), lax.rem(held - 1, LANES)
-    lane = iota((64, LANES), 1)
-    mine = []
-    for side, x, at_row, at_lane, there in (
-        (0, 0, 0, 0, rank > 0),
-        (1, 7, end_row, end_lane, rank < ranks - 1),
-    ):
-        a = spread(edges[side, 0:1, :])
-        b = spread(edges[side, 1:2, :])
-        place = pl.ds(PAD + x * step + at_row, 64, stride=OWN)
-        plain = pl.ds(x * step + at_row, 64, stride=OWN)
-        hit = lane == at_lane
-        cell = c[plain, :]
-        v[place, :] = v[place, :] + jnp.where(hit, a[:64] / (6.0 + cell), 0.0)
-        beyond = (a[64:] + u[plain, :]) / (6.0 + b[:64])
-        mine.append(jnp.where(jnp.logical_and(hit, there), beyond, 0.0))
+    def slab(ref, x, y, off=0):
+        b = off + (x * 8 + y) * SLAB
+        return ref[pl.ds(b if isinstance(b, int) else pl.multiple_of(b, 8), SLAB), :]
+
+    def zroll(value):
+        up = jnp.where(zlast, 0.0, pltpu.roll(value, SLAB - OWN, 0))
+        return up + jnp.where(zfirst, 0.0, pltpu.roll(value, OWN, 0))
+
+    for outer, y, inner in outer_sides:
+        @pl.when(outer)
+        def _():
+            def run(x, kind):
+                b = (x * 8 + y) * SLAB
+                b = b if isinstance(b, int) else pl.multiple_of(b, 8)
+                total = slab(s, x, y) + zroll(slab(u, x, y)) + slab(u, x, inner) + xsum(u, b, kind)
+                v[pl.ds(b + PAD, SLAB), :] = total / (6.0 + slab(c, x, y))
+
+            each_x(run)
 
     def second(x, kind):
         def at(y):
@@ -266,13 +301,82 @@
 
     each_x(second)
 
-    for side, x, at_row in ((0, 0, 0), (1, 7, end_row)):
-        for y in range(1, 7):
-            o = pl.ds((y * 8 + x) * SLAB + at_row, 8, stride=OWN)
-            more = mine[side][8 * y : 8 * y + 8]
-            if 2 <= y <= 5:
-                more = more / (6.0 + c[pl.ds((x * 8 + y) * SLAB + at_row, 8, stride=OWN), :])
-            w[o, :] = w[o, :] + more
+    for outer, y, inner in outer_sides:
+        @pl.when(outer)
+        def _():
+            def run(x, kind):
+                b = (x * 8 + y) * SLAB
+                b = b if isinstance(b, int) else pl.multiple_of(b, 8)
+                o = pl.ds((y * 8 + x) * SLAB, SLAB)
+                total = slab(s, x, y) + zroll(slab(v, x, y, PAD)) + xsum(v, b + PAD, kind)
+                total += slab(v, x, inner, PAD)
+                w[o, :] = total / (6.0 + slab(c, x, y))
+                o = pl.ds((inner * 8 + x) * SLAB, SLAB)
+                w[o, :] = (w[o, :] + slab(v, x, y, PAD)) / (6.0 + slab(c, x, inner))
+
+            each_x(run)
+
+    end_row = lax.div(held - 1, LANES)
+    for side, x, inner, at_row in ((0, 0, 1, 0), (1, 7, 6, end_row)):
+        for i, (ref, at_x) in enumerate(((c, x), (c, inner), (u, x))):
+            rows = pl.ds(at_x * step + at_row, 64, stride=OWN)
+            ends[pl.ds((side * 3 + i) * 64, 64), :] = ref[rows, :]
+
+    def keep(x, carry):
+        def slab(ref, y):
+            return ref[pl.ds(pl.multiple_of((x * 8 + y) * SLAB, 8), SLAB), :]
+
+        for plane, value in enumerate(
+            (
+                slab(u, 0), slab(u, 7), slab(s, 0) + slab(u, 1), slab(s, 7) + slab(u, 6),
+                slab(c, 0), slab(c, 1), slab(c, 7), slab(c, 6),
+            )
+        ):
+            front[pl.ds(pl.multiple_of(PAD + (plane * 8 + x) * SLAB, 8), SLAB), :] = value
+        return carry
+
+    lax.fori_loop(0, 8, keep, 0)
+
+
+def edge_kernel(
+    held_ref, _, pack, ends, even_1, odd_1,
+    new_pack, even_out, odd_out,
+    edges, tail, head, sem,
+):
+    held = held_ref[0, 0]
+    rank, ranks = lax.axis_index("curve"), lax.axis_size("curve")
+    first_curve, last_curve = end_curves()
+    take_edges(even_1, odd_1, edges, sem)
+    w = new_pack.at[pl.ds(PAD, CELLS * OWN)]
+    lane, row = iota((64, LANES), 1), iota((64, LANES), 0)
+    lone = jnp.logical_or(
+        jnp.logical_and(row < 8, jnp.logical_not(first_curve)),
+        jnp.logical_and(row >= 56, jnp.logical_not(last_curve)),
+    )
+    plain = jnp.logical_or(
+        jnp.logical_and(row < 16, jnp.logical_not(first_curve)),
+        jnp.logical_and(row >= 48, jnp.logical_not(last_curve)),
+    )
+    end_row, end_lane = lax.div(held - 1, LANES), lax.rem(held - 1, LANES)
+    zero = jnp.zeros((8, LANES), F32)
+    for side, x, inner, at_row, at_lane, there in (
+        (0, 0, 1, 0, 0, rank > 0),
+        (1, 7, 6, end_row, end_lane, rank < ranks - 1),
+    ):
+        a = spread(edges[side, 0:1, :])
+        b = spread(edges[side, 1:2, :])
+        coef, coef_inner, field = [ends[pl.ds((side * 3 + i) * 64, 64), :] for i in range(3)]
+        hit = jnp.logical_and(lane == at_lane, jnp.logical_not(lone))
+        more = jnp.where(hit, a[:64] / (6.0 + coef), 0.0)
+        beyond = (a[64:] + field) / (6.0 + b[:64])
+        total = jnp.where(jnp.logical_and(hit, there), beyond, 0.0) + up8(more) + down8(more)
+        total += jnp.concatenate([zero, more[:-8]], 0) + jnp.concatenate([more[8:], zero], 0)
+        total = total / jnp.where(plain, 1.0, 6.0 + coef)
+        more = more / jnp.where(plain, 1.0, 6.0 + coef_inner)
+        for at_x, value in ((x, total), (inner, more)):
+            for y in range(8):
+                o = pl.ds((y * 8 + at_x) * SLAB + at_row, 8, stride=OWN)
+                w[o, :] = w[o, :] + value[8 * y : 8 * y + 8]
 
     place = tail_place(held)
 
@@ -284,22 +388,7 @@
         return carry
 
     lax.fori_loop(0, 8, body, 0)
-
-    def keep(x, carry):
-        def slab(ref, y):
-            return ref[pl.ds(pl.multiple_of((x * 8 + y) * SLAB, 8), SLAB), :]
-
-        for plane, value in enumerate(
-            (
-                slab(u, 0), slab(u, 7), slab(s, 0) + slab(u, 1), slab(c, 0),
-                slab(c, 1), slab(c, 6), slab(c, 7), slab(s, 7) + slab(u, 6),
-            )
-        ):
-            front[pl.ds(pl.multiple_of(PAD + (plane * 8 + x) * SLAB, 8), SLAB), :] = value
-        return carry
-
-    lax.fori_loop(0, 8, keep, 0)
-    send_zones(tail, head, even_out, odd_out, sem, even)
+    send_zones(tail, head, even_out, odd_out, sem, is_even("curve"))
 
 
 class Window:
@@ -360,19 +449,23 @@
 
 
 def align_kernel(
-    held_ref, before_refs, own, even_in, odd_in,
+    held_ref, before_refs, own, even_1, odd_1,
     even_out, odd_out, faces, sides,
     tail, head, edges, sem,
 ):
     before, after = drifts(held_ref, before_refs)
     even = is_even("curve")
-    edge = 2 * 64 * ZONE
-    zone = pl.ds(PAD, edge)
-    take_zones(
-        even_in.at[pl.ds(0, edge)], odd_in.at[pl.ds(0, edge)], tail.at[zone], head.at[zone], sem, even
-    )
-    packed = pl.ds(edge, 8)
-    take_zones(even_in.at[packed], odd_in.at[packed], edges.at[0], edges.at[1], sem, even)
+
+    def copies_in(zone, message):
+        first, last = end_curves()
+        other = pl.multiple_of(jnp.where(jnp.logical_or(first, last), 2 * PLANE, PLANE), 8)
+        return [
+            (message.at[pl.ds(0, PLANE)], to_plane(zone, plane_of(0, 0, 1))),
+            (message.at[pl.ds(PLANE, PLANE)], to_plane(zone, other)),
+        ]
+
+    by_parity((even_1,), (odd_1,), tail, head, copies_in, sem)
+    take_edges(even_1, odd_1, edges, sem)
     here = Window(before, after)
 
     def body(k, carry):
@@ -422,31 +515,40 @@
 
 
 def face_kernel(
-    held_ref, before_refs, own, even_in, odd_in, even_face, odd_face, faces, sides,
+    held_ref, before_refs, own, even_1, odd_1, even_3, odd_3,
+    even_face, odd_face, faces, sides,
     even_out, odd_out, even_end, odd_end, new, below, inner,
     tail, head, near, q, ends, sem,
 ):
     before, after = drifts(held_ref, before_refs)
     even = is_even("curve")
-    size = 6 * 64 * ZONE
     half = 64 * WIN
-    zone = pl.ds(PAD, size)
-    take_zones(even_in, odd_in, tail.at[zone], head.at[zone], sem, even)
+
+    def copies_in(zone, message_1, message_3):
+        first, last = end_curves()
+        rest = jnp.where(jnp.logical_or(first, last), 8 * PLANE, 4 * PLANE)
+        return [
+            (message_1.at[pl.ds(PLANE, PLANE)], to_plane(zone, plane_of(1, 2, 3))),
+            (message_1.at[pl.ds(2 * PLANE, 2 * PLANE)], to_plane(zone, plane_of(2, 4, 6), 2)),
+            (message_3, to_plane(zone, rest, 4)),
+        ]
+
+    by_parity((even_1, even_3), (odd_1, odd_3), tail, head, copies_in, sem)
     take_faces(even_face, odd_face, near.at[pl.ds(0, half)], near.at[pl.ds(half, half)], sem)
     here = Window(before, after)
 
     def body(k, carry):
         for plane, ref, to, add in (
-            (0, q, 0, 0.0),
-            (5, q, 1, 0.0),
-            (1, below, 0, 6.0),
-            (4, below, 1, 6.0),
-            (2, inner, 0, 6.0),
-            (3, inner, 1, 6.0),
+            (2, q, 0, 0.0),
+            (3, q, 1, 0.0),
+            (4, below, 0, 6.0),
+            (6, below, 1, 6.0),
+            (5, inner, 0, 6.0),
+            (7, inner, 1, 6.0),
         ):
             for z in range(8):
                 i = k * 8 + z
-                at = PAD + ((plane + 2) * 64 + i) * OWN
+                at = PAD + (plane * 64 + i) * OWN
                 zat = PAD + (plane * 64 + i) * ZONE
                 value = here(own, at, tail, zat, head, zat)
                 ref[pl.ds(pl.multiple_of((to * 64 + i) * WIN, 8), WIN), :] = value + add
@@ -499,6 +601,7 @@
     take_faces(even_face, odd_face, near.at[pl.ds(0, half)], near.at[pl.ds(half, half)], sem)
     here = Window(before, after)
     lane, row = here.lane, here.row
+    outer = end_curves()
 
     def get(y, x, z):
         i = (y * 8 + x) * 8 + z
@@ -525,18 +628,21 @@
         for plane, y in ((0, 0), (1, 7)):
             for z in range(8):
                 cell = cell_rows(plane, x, z)
-                total = get(y, x, z) + near[cell, :]
+                held = get(y, x, z)
+                total = held + near[cell, :]
                 total += left(plane, z) if kind == 0 else new[cell_rows(plane, x - 1, z), :]
                 total += right(plane, z) if kind == 2 else new[cell_rows(plane, x + 1, z), :]
                 if z > 0:
                     total += new[cell_rows(plane, x, z - 1), :]
                 if z < 7:
                     total += new[cell_rows(plane, x, z + 1), :]
-                put(x, y, z, total / below[cell, :])
+                put(x, y, z, jnp.where(outer[plane], held, total / below[cell, :]))
         for plane, y in ((0, 1), (1, 6)):
             for z in range(8):
                 cell = cell_rows(plane, x, z)
-                put(x, y, z, (get(y, x, z) + new[cell, :]) / inner[cell, :])
+                held = get(y, x, z)
+                total = (held + new[cell, :]) / inner[cell, :]
+                put(x, y, z, jnp.where(outer[plane], held, total))
         for y in range(2, 6):
             for z in range(8):
                 put(x, y, z, get(y, x, z))
@@ -544,16 +650,21 @@
     each_x(run)
 
 
-def swapped(value, axis, first):
+def swapped(value, axis, first, inner):
     count = lax.axis_size(axis)
     pairs = [(i, i + 1) for i in range(first, count - 1, 2)]
-    return lax.ppermute(value, axis, pairs + [(b, a) for a, b in pairs])
-
-
-def swaps(values, axis):
+    pairs += [(b, a) for a, b in pairs]
+    if inner:
+        curves = lax.axis_size("grp")
+        pairs = [(a * curves + g, b * curves + g) for a, b in pairs for g in range(1, curves - 1)]
+        axis = (axis, "grp")
+    return lax.ppermute(value, axis, pairs)
+
+
+def swaps(values, axis, inner=False):
     got = []
     for first, value in enumerate(values):
-        got.append(swapped(value, axis, first))
+        got.append(swapped(value, axis, first, inner))
     return got
 
 
@@ -563,11 +674,13 @@
     above = [jnp.bitwise_and(rank >> i, 1).reshape(1, 1) for i in places]
     total, *above = lax.optimization_barrier((counts, *above))
     before = jnp.zeros_like(counts)
-    for i in places:
+    for i in places[:-1]:
         pairs = [(a, a ^ 1 << i) for a in range(count) if a ^ 1 << i < count]
         other = lax.ppermute(total, "curve", pairs)
         before += above[i] * other
         total += other
+    for top in above[len(places) - 1 :]:
+        before += top * (count * AVG - total)
     return before
 
 
@@ -575,7 +688,7 @@
     return jax.ShapeDtypeStruct(shape, F32)
 
 
-def call(kernel, outs, ins, scratch, limit, vmem_ins=(), vmem_outs=(), hbm_ins=(), us=2):
+def call(kernel, outs, ins, scratch, limit, vmem_ins=(), vmem_outs=(), hbm_ins=(), us=2, aliases={}):
     (held,), others, *arrays = ins
     vmem = pl.BlockSpec(memory_space=pltpu.VMEM)
     specs = [SMEM] * (1 + len(others))
@@ -591,9 +704,10 @@
         out_shape=outs,
         in_specs=specs,
         out_specs=[vmem if i in vmem_outs else ANY for i in range(len(outs))],
-        scratch_shapes=[pltpu.VMEM(shape, F32) for shape in scratch] + [pltpu.SemaphoreType.DMA((8,))],
+        scratch_shapes=[pltpu.VMEM(shape, F32) for shape in scratch] + [pltpu.SemaphoreType.DMA((10,))],
         compiler_params=pltpu.CompilerParams(vmem_limit_bytes=limit * 2**20),
         cost_estimate=pl.CostEstimate(flops=us * 4_000_000, bytes_accessed=us * 10**6, transcendentals=0),
+        input_output_aliases=aliases,
     )(held, *others, *arrays)
 
 
@@ -605,34 +719,43 @@
     win = 64 * WIN
 
     others = (held_before(counts),)
-    message, rest = (2 * zone + 8, LANES), (6 * zone, LANES)
-    *faces_out, rest_a, rest_b = call(
+    message, edge = (8 * zone, LANES), (8, LANES)
+    outs = call(
         front_kernel,
-        [array(*message)] * 2 + [array(*rest)] * 2,
+        [array(4 * zone + 8, LANES)] * 2 + [array(4 * zone, LANES)] * 2,
         ((counts,), (), state2, coef2),
-        [message, message, rest, rest],
-        limit=4,
+        [message, message, edge, edge],
+        limit=6,
         vmem_ins=(0, 1),
     )
-    faces_in = swaps(faces_out, "curve")
-    rest_in = swaps((rest_a, rest_b), "curve")
-    message = (8 * zone, LANES)
-    front, pack, *sweep_out = call(
+    in_1 = swaps(outs[:2], "curve")
+    in_3 = swaps(outs[2:], "curve", inner=True)
+    front, pack, ends = call(
         sweep_kernel,
-        [array(rows + 2 * PAD, LANES)] * 2 + [array(*message)] * 2,
-        ((counts,), (), state2, coef2, *faces_in),
-        [(rows + 2 * PAD, LANES), (2, 8, LANES), message, message],
-        limit=24,
+        [array(rows + 2 * PAD, LANES)] * 2 + [array(6 * 64, LANES)],
+        ((counts,), (), state2, coef2),
+        [(rows + 2 * PAD, LANES)],
+        limit=16,
         vmem_ins=(0, 1),
-        vmem_outs=(0, 1),
+        vmem_outs=(0, 1, 2),
         us=6,
+    )
+    pack, *sweep_out = call(
+        edge_kernel,
+        [array(rows + 2 * PAD, LANES)] + [array(*message)] * 2,
+        ((counts,), (), pack, ends, *in_1),
+        [(2, 8, LANES), message, message],
+        limit=8,
+        vmem_ins=(0, 1),
+        vmem_outs=(0,),
+        aliases={1: 0},
     )
     sweep_in = swaps(sweep_out, "curve")
     *near_out, faces, sides = call(
         align_kernel,
         [array(win, LANES)] * 2 + [array(2 * win, LANES), array(32 * WIN, LANES)],
-        ((counts,), others, front, *faces_in),
-        [(2 * zone + 2 * PAD, LANES), (2 * zone + 2 * PAD, LANES), (2, 8, LANES)],
+        ((counts,), others, front, *in_1),
+        [(3 * zone + 2 * PAD, LANES), (3 * zone + 2 * PAD, LANES), (2, 8, LANES)],
         limit=8,
         vmem_ins=(0,),
         vmem_outs=(2, 3),
@@ -641,13 +764,13 @@
     near_a, near_b, end_a, end_b, new, below, inner = call(
         face_kernel,
         [array(win, LANES)] * 2 + [array(16, LANES)] * 2 + [array(2 * win, LANES)] * 3,
-        ((counts,), others, front, *rest_in, *near_in, faces, sides),
+        ((counts,), others, front, *in_1, *in_3, *near_in, faces, sides),
         [
-            (6 * zone + 2 * PAD, LANES), (6 * zone + 2 * PAD, LANES),
+            (12 * zone + 2 * PAD, LANES), (12 * zone + 2 * PAD, LANES),
             (2 * win, LANES), (2 * win, LANES), (2, 16, LANES),
         ],
         limit=8,
-        vmem_ins=(0, 5, 6),
+        vmem_ins=(0, 7, 8),
         vmem_outs=(4, 5, 6),
         us=3,
     )

time: 90.2 us -> 75.8 us (0.84)
  waiting for transfers between devices: 31.6 us -> 16.7 us
  Pallas kernels: 16.5 us -> 18.7 us
  starting transfers between devices: 30.3 us -> 28.3 us
    ppermute x3 -> x2, waiting for transfers between devices: 16.6 us -> 0.96 us  [held_before(): other = lax.ppermute(total, 'curve', pairs)]
    pallas_call x5 -> x6, Pallas kernels: 16.5 us -> 18.7 us  [call(): pl.pallas_call(body, out_shape=outs, in_specs=specs, out_specs=[vmem if i...]
    ppermute x3 -> x2, starting transfers between devices: 6.96 us -> 5.02 us  [held_before(): other = lax.ppermute(total, 'curve', pairs)]
    unnamed x8 -> x10, local copies, waits for them, and re-layouts: 7.45 us -> 8.14 us
  transfers between devices with their start and end apart: 15 -> 14, of which waited for: 4 -> 4; matrix products, arithmetic and copies ran while one was open for 0% -> 0% of each run, Pallas kernels for 12% -> 18%
where the time goes in v3:
time: 75.8 us; the launch traced here: 75.3 us
  starting transfers between devices  28.3 us (37%)
  Pallas kernels  18.7 us (25%)
  waiting for transfers between devices  16.7 us (22%)
  local copies, waits for them, and re-layouts  8.14 us (11%)
  between operations  3.42 us (5%)
    ppermute x12, starting transfers between devices, swapped(): return lax.ppermute(value, axis, pairs)  23.3 us
    pallas_call x6, Pallas kernels, call(): pl.pallas_call(body, out_shape=outs, in_specs=specs, out_specs=[vmem if i...  18.7 us
    ppermute x12, waiting for transfers between devices, swapped(): return lax.ppermute(value, axis, pairs)  15.8 us
    unnamed x10, local copies, waits for them, and re-layouts  8.14 us
    ppermute x2, starting transfers between devices, held_before(): other = lax.ppermute(total, 'curve', pairs)  5.02 us
  transfers between devices with their start and end apart: 14, of which 4 were waited for; matrix products, arithmetic and copies ran while one was open for 0% of the time, Pallas kernels for 18%

profile of v3, /device:TPU:6, one launch (start us, length us, event | category | flops | bytes accessed | tf_op | source)
XLA Modules:
  0.0 75.3 jit_solution(2139108216603162464)
XLA Ops:
  0.7 2.8 %copy-done = f32[2,512,1,1536]{3,2,1,0:T(1,128)S(1)} copy-done((f32[2,512,1,1536]{3,2,1,0:T(1,128)S(1)}, f32[2,512,1,1536]{3,2,1,0:T(1,128)}, u32[]{:S(2)}) %copy-start) | copy-done | bytes 6291480
  3.4 1.9 %copy-done.2 = f32[512,1,1536]{2,1,0:T(1,128)S(1)} copy-done((f32[512,1,1536]{2,1,0:T(1,128)S(1)}, f32[512,1,1536]{2,1,0:T(1,128)}, u32[]{:S(2)}) %copy-start.2) | copy-done | bytes 3145752
  5.3 1.3 %shard_map.38 = (f32[520,128]{1,0:T(8,128)}, f32[520,128]{1,0:T(8,128)}, f32[512,128]{1,0:T(8,128)}, f32[512,128]{1,0:T(8,128)S(1)}) custom-call(s32[1,1]{1,0:T(1,128)S(6)} %copy.7.held_ref, f32[12288,128]{1,0:T(8,128)S(1)} %bitcast.6, f32[6144,128]{1,0:T(8,128)S(1)} %bitcast.8), custom_call_target="tpu_custom_call" | custom-call | flops 8000000 | bytes 2000000 | tf_op jit(solution)/shard_map/pallas_call | solution.py:702
  6.7 0.7 copy-done.4
  7.4 0.5 collective-permute-start.2
  7.9 4.4 %collective-permute-start.3 = (f32[520,128]{1,0:T(8,128)}, f32[520,128]{1,0:T(8,128)}, u32[]{:S(2)}, u32[]{:S(2)}) collective-permute-start(f32[520,128]{1,0:T(8,128)} %get-tuple-element.37), channel_id=1, source_target_pairs={{4,8},{12,16},{20,24},{8,4},{16,12},{24,20},{5,9},{13,17},{21,25},... | collective-permute-start | bytes 798728 | tf_op jit(solution)/shard_map/ppermute | solution.py:661
  12.3 1.9 %collective-permute-start.6 = (f32[512,128]{1,0:T(8,128)}, f32[512,128]{1,0:T(8,128)}, u32[]{:S(2)}, u32[]{:S(2)}) collective-permute-start(f32[512,128]{1,0:T(8,128)} %get-tuple-element.42), channel_id=1, source_target_pairs={{1,5},{2,6},{9,13},{10,14},{17,21},{18,22},{25,29},{26,30},{5,1},{... | collective-permute-start | bytes 786440 | tf_op jit(solution)/shard_map/ppermute | solution.py:661
  14.2 2.1 %collective-permute-start = (s32[1,1]{1,0:T(1,128)}, s32[1,1]{1,0:T(1,128)}, u32[]{:S(2)}, u32[]{:S(2)}) collective-permute-start(s32[1,1]{1,0:T(1,128)} %param.5), channel_id=1, source_target_pairs={{0,4},{4,0},{8,12},{12,8},{16,20},{20,16},{24,28},{28,24},{1,5},{5... | collective-permute-start | bytes 20 | tf_op jit(solution)/shard_map/ppermute | solution.py:679
  16.3 2.9 %collective-permute-start.7 = (f32[512,128]{1,0:T(8,128)}, f32[512,128]{1,0:T(8,128)S(1)}, u32[]{:S(2)}, u32[]{:S(2)}) collective-permute-start(f32[512,128]{1,0:T(8,128)} %copy-done.4), channel_id=1, source_target_pairs={{5,9},{6,10},{13,17},{14,18},{21,25},{22,26},{9,5},{10,6},{17,13},... | collective-permute-start | bytes 786440 | tf_op jit(solution)/shard_map/ppermute | solution.py:661
  19.3 2.8 %copy-done.1 = f32[2,512,1,1536]{3,2,1,0:T(1,128)S(1)} copy-done((f32[2,512,1,1536]{3,2,1,0:T(1,128)S(1)}, f32[2,512,1,1536]{3,2,1,0:T(1,128)}, u32[]{:S(2)}) %copy-start.1) | copy-done | bytes 6291480
  22.1 4.3 %shard_map.37 = (f32[6176,128]{1,0:T(8,128)S(1)}, f32[6176,128]{1,0:T(8,128)S(1)}, f32[384,128]{1,0:T(8,128)S(1)}) custom-call(s32[1,1]{1,0:T(1,128)S(6)} %copy.7.held_ref, f32[12288,128]{1,0:T(8,128)S(1)} %bitcast.7, f32[6144,128]{1,0:T(8,128)S(1)} %bitcast.9), custom_call_target="tpu_custom_call" | custom-call | flops 24000000 | bytes 6000000 | tf_op jit(solution)/shard_map/pallas_call | solution.py:702
  26.3 0.9 %collective-permute-done = s32[1,1]{1,0:T(1,128)} collective-permute-done((s32[1,1]{1,0:T(1,128)}, s32[1,1]{1,0:T(1,128)}, u32[]{:S(2)}, u32[]{:S(2)}) %collective-permute-start) | collective-permute-done | bytes 36 | tf_op jit(solution)/shard_map/ppermute | solution.py:679
  27.8 2.9 %collective-permute-start.1 = (s32[1,1]{1,0:T(1,128)}, s32[1,1]{1,0:T(1,128)}, u32[]{:S(2)}, u32[]{:S(2)}) collective-permute-start(s32[1,1]{1,0:T(1,128)} %add.12), channel_id=1, source_target_pairs={{0,8},{4,12},{8,0},{12,4},{16,24},{20,28},{24,16},{28,20},{1,9},{5... | collective-permute-start | bytes 20 | tf_op jit(solution)/shard_map/ppermute | solution.py:679
  32.8 3.7 %shard_map.40 = (f32[512,128]{1,0:T(8,128)S(1)}, f32[512,128]{1,0:T(8,128)S(1)}, f32[1024,128]{1,0:T(8,128)S(1)}, f32[256,128]{1,0:T(8,128)S(1)}) custom-call(s32[1,1]{1,0:T(1,128)S(6)} %copy.7.held_ref, s32[1,1]{1,0:T(1,128)S(6)} %add.15.refs_0_, f32[6176,128]{1,0:T(8,128)S(1)} %get-tuple-element.41.refs_1_, f32[520,128]{1,0:T(8,128)S(1)} %collective-permute-done.2.refs_2_, ...), custom_call_target="tpu_custom_call" | custom-call | flops 8000000 | bytes 2000000 | tf_op jit(solution)/shard_map/pallas_call | solution.py:702
  36.6 1.9 %collective-permute-start.9 = (f32[512,128]{1,0:T(8,128)S(1)}, f32[512,128]{1,0:T(8,128)S(1)}, u32[]{:S(2)}, u32[]{:S(2)}) collective-permute-start(f32[512,128]{1,0:T(8,128)S(1)} %get-tuple-element.45), channel_id=1, source_target_pairs={{1,2},{2,1},{5,6},{6,5},{9,10},{10,9},{13,14},{14,13},{17,18},{18,... | collective-permute-start | bytes 786440 | tf_op jit(solution)/shard_map/ppermute | solution.py:661
  38.5 1.7 %shard_map.39 = (f32[6176,128]{1,0:T(8,128)S(1)}, f32[1024,128]{1,0:T(8,128)S(1)}, f32[1024,128]{1,0:T(8,128)S(1)}) custom-call(s32[1,1]{1,0:T(1,128)S(6)} %copy.7.held_ref, f32[6176,128]{1,0:T(8,128)S(1)} %get-tuple-element.34.refs_0_, f32[384,128]{1,0:T(8,128)S(1)} %get-tuple-element.35.refs_1_, ...), custom_call_target="tpu_custom_call", output_to_operand_aliasing={{0}: (1, {})} | custom-call | flops 8000000 | bytes 2000000 | tf_op jit(solution)/shard_map/pallas_call | solution.py:702
  40.2 0.4 collective-permute-start.4
  40.6 4.6 %collective-permute-start.5 = (f32[1024,128]{1,0:T(8,128)S(1)}, f32[1024,128]{1,0:T(8,128)S(1)}, u32[]{:S(2)}, u32[]{:S(2)}) collective-permute-start(f32[1024,128]{1,0:T(8,128)S(1)} %get-tuple-element.40), channel_id=1, source_target_pairs={{4,8},{12,16},{20,24},{8,4},{16,12},{24,20},{5,9},{13,17},{21,25},... | collective-permute-start | bytes 1572872 | tf_op jit(solution)/shard_map/ppermute | solution.py:661
  45.2 3.7 %shard_map.41 = (f32[512,128]{1,0:T(8,128)S(1)}, f32[512,128]{1,0:T(8,128)S(1)}, f32[16,128]{1,0:T(8,128)S(1)}, f32[16,128]{1,0:T(8,128)S(1)}, f32[1024,128]{1,0...) custom-call(s32[1,1]{1,0:T(1,128)S(6)} %copy.7.held_ref, s32[1,1]{1,0:T(1,128)S(6)} %add.15.refs_0_, ...), custom_call_target="tpu_custom_call" | custom-call | flops 12000000 | bytes 3000000 | tf_op jit(solution)/shard_map/pallas_call | solution.py:702
  49.0 3.1 %collective-permute-start.11 = (f32[512,128]{1,0:T(8,128)S(1)}, f32[512,128]{1,0:T(8,128)S(1)}, u32[]{:S(2)}, u32[]{:S(2)}) collective-permute-start(f32[512,128]{1,0:T(8,128)S(1)} %get-tuple-element.49), channel_id=1, source_target_pairs={{1,2},{2,1},{5,6},{6,5},{9,10},{10,9},{13,14},{14,13},{17,18},{18,... | collective-permute-start | bytes 786440 | tf_op jit(solution)/shard_map/ppermute | solution.py:661
  52.2 12.6 %collective-permute-done.12.refs_6_ = f32[16,128]{1,0:T(8,128)S(1)} collective-permute-done((f32[16,128]{1,0:T(8,128)S(1)}, f32[16,128]{1,0:T(8,128)S(1)}, u32[]{:S(2)}, u32[]{:S(2)}) %collective-permute-start.12) | collective-permute-done | bytes 8224 | tf_op jit(solution)/shard_map/ppermute | solution.py:661
  64.8 3.3 %collective-permute-start.13 = (f32[16,128]{1,0:T(8,128)S(1)}, f32[16,128]{1,0:T(8,128)S(1)}, u32[]{:S(2)}, u32[]{:S(2)}) collective-permute-start(f32[16,128]{1,0:T(8,128)S(1)} %get-tuple-element.51), channel_id=1, source_target_pairs={{4,8},{12,16},{20,24},{8,4},{16,12},{24,20},{5,9},{13,17},{21,25},... | collective-permute-start | bytes 24584 | tf_op jit(solution)/shard_map/ppermute | solution.py:661
  68.1 3.2 %collective-permute-done.13.refs_7_ = f32[16,128]{1,0:T(8,128)S(1)} collective-permute-done((f32[16,128]{1,0:T(8,128)S(1)}, f32[16,128]{1,0:T(8,128)S(1)}, u32[]{:S(2)}, u32[]{:S(2)}) %collective-permute-start.13) | collective-permute-done | bytes 8224 | tf_op jit(solution)/shard_map/ppermute | solution.py:661
  71.2 4.0 %shard_map.42 = f32[4096,128]{1,0:T(8,128)} custom-call(s32[1,1]{1,0:T(1,128)S(6)} %copy.7.held_ref, s32[1,1]{1,0:T(1,128)S(6)} %add.15.refs_0_, f32[6176,128]{1,0:T(8,128)S(1)} %get-tuple-element.38.refs_1_, f32[1024,128]{1,0:T(8,128)S(1)} %collective-permute-done.4.refs_2_, f32[1024,128]{1,0:T(8,128)S(1)} %collective-permute-done.5.refs_3_, ...), custom_call_target="tpu_custom_call" | custom-call | flops 12000000 | bytes 3000000 | tf_op jit(solution)/shard_map/pallas_call | solution.py:702
  (20 shorter events, 0.3 us)
Async XLA Ops:
  0.7 2.8 %copy-start = (f32[2,512,1,1536]{3,2,1,0:T(1,128)S(1)}, f32[2,512,1,1536]{3,2,1,0:T(1,128)}, u32[]{:S(2)}) copy-start(f32[2,512,1,1536]{3,2,1,0:T(1,128)} %param.3) | copy-start | bytes 18874372
  3.4 1.9 %copy-start.2 = (f32[512,1,1536]{2,1,0:T(1,128)S(1)}, f32[512,1,1536]{2,1,0:T(1,128)}, u32[]{:S(2)}) copy-start(f32[512,1,1536]{2,1,0:T(1,128)} %param.4) | copy-start | bytes 9437188
  5.3 13.9 %copy-start.3 = (f32[512,1,1536]{2,1,0:T(1,128)S(1)}, f32[512,1,1536]{2,1,0:T(1,128)}, u32[]{:S(2)}) copy-start(f32[512,1,1536]{2,1,0:T(1,128)} %param.4) | copy-start | bytes 9437188
  6.7 0.7 copy-start.4
  7.4 25.4 %collective-permute-start.2 = (f32[520,128]{1,0:T(8,128)}, f32[520,128]{1,0:T(8,128)S(1)}, u32[]{:S(2)}, u32[]{:S(2)}) collective-permute-start(f32[520,128]{1,0:T(8,128)} %get-tuple-element.36), channel_id=1, source_target_pairs={{0,4},{8,12},{16,20},{24,28},{4,0},{12,8},{20,16},{28,24},{1,5},{9... | collective-permute-start | bytes 798728 | tf_op jit(solution)/shard_map/ppermute | solution.py:661
  7.9 24.9 %collective-permute-start.3 = (f32[520,128]{1,0:T(8,128)}, f32[520,128]{1,0:T(8,128)}, u32[]{:S(2)}, u32[]{:S(2)}) collective-permute-start(f32[520,128]{1,0:T(8,128)} %get-tuple-element.37), channel_id=1, source_target_pairs={{4,8},{12,16},{20,24},{8,4},{16,12},{24,20},{5,9},{13,17},{21,25},... | collective-permute-start | bytes 798728 | tf_op jit(solution)/shard_map/ppermute | solution.py:661
  12.3 28.3 %collective-permute-start.6 = (f32[512,128]{1,0:T(8,128)}, f32[512,128]{1,0:T(8,128)}, u32[]{:S(2)}, u32[]{:S(2)}) collective-permute-start(f32[512,128]{1,0:T(8,128)} %get-tuple-element.42), channel_id=1, source_target_pairs={{1,5},{2,6},{9,13},{10,14},{17,21},{18,22},{25,29},{26,30},{5,1},{... | collective-permute-start | bytes 786440 | tf_op jit(solution)/shard_map/ppermute | solution.py:661
  14.2 13.0 %collective-permute-start = (s32[1,1]{1,0:T(1,128)}, s32[1,1]{1,0:T(1,128)}, u32[]{:S(2)}, u32[]{:S(2)}) collective-permute-start(s32[1,1]{1,0:T(1,128)} %param.5), channel_id=1, source_target_pairs={{0,4},{4,0},{8,12},{12,8},{16,20},{20,16},{24,28},{28,24},{1,5},{5... | collective-permute-start | bytes 20 | tf_op jit(solution)/shard_map/ppermute | solution.py:679
  16.3 28.9 %collective-permute-start.7 = (f32[512,128]{1,0:T(8,128)}, f32[512,128]{1,0:T(8,128)S(1)}, u32[]{:S(2)}, u32[]{:S(2)}) collective-permute-start(f32[512,128]{1,0:T(8,128)} %copy-done.4), channel_id=1, source_target_pairs={{5,9},{6,10},{13,17},{14,18},{21,25},{22,26},{9,5},{10,6},{17,13},... | collective-permute-start | bytes 786440 | tf_op jit(solution)/shard_map/ppermute | solution.py:661
  19.3 2.8 %copy-start.1 = (f32[2,512,1,1536]{3,2,1,0:T(1,128)S(1)}, f32[2,512,1,1536]{3,2,1,0:T(1,128)}, u32[]{:S(2)}) copy-start(f32[2,512,1,1536]{3,2,1,0:T(1,128)} %param.3) | copy-start | bytes 18874372
  27.8 3.6 %collective-permute-start.1 = (s32[1,1]{1,0:T(1,128)}, s32[1,1]{1,0:T(1,128)}, u32[]{:S(2)}, u32[]{:S(2)}) collective-permute-start(s32[1,1]{1,0:T(1,128)} %add.12), channel_id=1, source_target_pairs={{0,8},{4,12},{8,0},{12,4},{16,24},{20,28},{24,16},{28,20},{1,9},{5... | collective-permute-start | bytes 20 | tf_op jit(solution)/shard_map/ppermute | solution.py:679
  36.5 8.8 %collective-permute-start.8 = (f32[512,128]{1,0:T(8,128)S(1)}, f32[512,128]{1,0:T(8,128)S(1)}, u32[]{:S(2)}, u32[]{:S(2)}) collective-permute-start(f32[512,128]{1,0:T(8,128)S(1)} %get-tuple-element.44), channel_id=1, source_target_pairs={{0,1},{2,3},{1,0},{3,2},{4,5},{6,7},{5,4},{7,6},{8,9},{10,11},{9,8... | collective-permute-start | bytes 786440 | tf_op jit(solution)/shard_map/ppermute | solution.py:661
  36.6 8.7 %collective-permute-start.9 = (f32[512,128]{1,0:T(8,128)S(1)}, f32[512,128]{1,0:T(8,128)S(1)}, u32[]{:S(2)}, u32[]{:S(2)}) collective-permute-start(f32[512,128]{1,0:T(8,128)S(1)} %get-tuple-element.45), channel_id=1, source_target_pairs={{1,2},{2,1},{5,6},{6,5},{9,10},{10,9},{13,14},{14,13},{17,18},{18,... | collective-permute-start | bytes 786440 | tf_op jit(solution)/shard_map/ppermute | solution.py:661
  40.2 31.0 %collective-permute-start.4 = (f32[1024,128]{1,0:T(8,128)S(1)}, f32[1024,128]{1,0:T(8,128)S(1)}, u32[]{:S(2)}, u32[]{:S(2)}) collective-permute-start(f32[1024,128]{1,0:T(8,128)S(1)} %get-tuple-element.39), channel_id=1, source_target_pairs={{0,4},{8,12},{16,20},{24,28},{4,0},{12,8},{20,16},{28,24},{1,5},{9... | collective-permute-start | bytes 1572872 | tf_op jit(solution)/shard_map/ppermute | solution.py:661
  40.6 30.6 %collective-permute-start.5 = (f32[1024,128]{1,0:T(8,128)S(1)}, f32[1024,128]{1,0:T(8,128)S(1)}, u32[]{:S(2)}, u32[]{:S(2)}) collective-permute-start(f32[1024,128]{1,0:T(8,128)S(1)} %get-tuple-element.40), channel_id=1, source_target_pairs={{4,8},{12,16},{20,24},{8,4},{16,12},{24,20},{5,9},{13,17},{21,25},... | collective-permute-start | bytes 1572872 | tf_op jit(solution)/shard_map/ppermute | solution.py:661
  49.0 22.3 %collective-permute-start.10 = (f32[512,128]{1,0:T(8,128)S(1)}, f32[512,128]{1,0:T(8,128)S(1)}, u32[]{:S(2)}, u32[]{:S(2)}) collective-permute-start(f32[512,128]{1,0:T(8,128)S(1)} %get-tuple-element.48), channel_id=1, source_target_pairs={{0,1},{2,3},{1,0},{3,2},{4,5},{6,7},{5,4},{7,6},{8,9},{10,11},{9,8... | collective-permute-start | bytes 786440 | tf_op jit(solution)/shard_map/ppermute | solution.py:661
  49.0 22.2 %collective-permute-start.11 = (f32[512,128]{1,0:T(8,128)S(1)}, f32[512,128]{1,0:T(8,128)S(1)}, u32[]{:S(2)}, u32[]{:S(2)}) collective-permute-start(f32[512,128]{1,0:T(8,128)S(1)} %get-tuple-element.49), channel_id=1, source_target_pairs={{1,2},{2,1},{5,6},{6,5},{9,10},{10,9},{13,14},{14,13},{17,18},{18,... | collective-permute-start | bytes 786440 | tf_op jit(solution)/shard_map/ppermute | solution.py:661
  52.1 12.7 %collective-permute-start.12 = (f32[16,128]{1,0:T(8,128)S(1)}, f32[16,128]{1,0:T(8,128)S(1)}, u32[]{:S(2)}, u32[]{:S(2)}) collective-permute-start(f32[16,128]{1,0:T(8,128)S(1)} %get-tuple-element.50), channel_id=1, source_target_pairs={{0,4},{8,12},{16,20},{24,28},{4,0},{12,8},{20,16},{28,24},{1,5},{9... | collective-permute-start | bytes 24584 | tf_op jit(solution)/shard_map/ppermute | solution.py:661
  64.8 6.4 %collective-permute-start.13 = (f32[16,128]{1,0:T(8,128)S(1)}, f32[16,128]{1,0:T(8,128)S(1)}, u32[]{:S(2)}, u32[]{:S(2)}) collective-permute-start(f32[16,128]{1,0:T(8,128)S(1)} %get-tuple-element.51), channel_id=1, source_target_pairs={{4,8},{12,16},{20,24},{8,4},{16,12},{24,20},{5,9},{13,17},{21,25},... | collective-permute-start | bytes 24584 | tf_op jit(solution)/shard_map/ppermute | solution.py:661

commit v4 on v3

--- a/solution.py
+++ b/solution.py
@@ -128,7 +128,7 @@
 
 def front_kernel(
     held_ref, _, state, coef,
-    even_1, odd_1, even_3, odd_3,
+    even_edge, odd_edge, even_1, odd_1, even_2, odd_2, count,
     tail, head, tail_edge, head_edge, sem,
 ):
     held = held_ref[0, 0]
@@ -158,35 +158,42 @@
         for plane, load in enumerate(loads):
             put_zones(load, tail, head, (plane * 8 + x) * 8 * ZONE, place)
 
-    def out(zone, edge, message_1, message_3):
+    count[...] = jnp.full((8, LANES), held, jnp.int32).astype(F32)
+
+    def one_side(zone, message, _):
         return [
-            (zone.at[pl.ds(plane_of(0, 0, 1), PLANE)], message_1.at[pl.ds(0, PLANE)]),
-            (zone.at[pl.ds(plane_of(1, 2, 3), PLANE)], message_1.at[pl.ds(PLANE, PLANE)]),
-            (zone.at[pl.ds(plane_of(2, 4, 6), 2 * PLANE)], message_1.at[pl.ds(2 * PLANE, 2 * PLANE)]),
-            (edge, message_1.at[pl.ds(4 * PLANE, 8)]),
-            (zone.at[pl.ds(4 * PLANE, 4 * PLANE)], message_3),
+            (zone.at[pl.ds(plane_of(0, 0, 1), PLANE)], message.at[pl.ds(0, PLANE)]),
+            (zone.at[pl.ds(plane_of(1, 2, 3), PLANE)], message.at[pl.ds(PLANE, PLANE)]),
+            (zone.at[pl.ds(plane_of(2, 4, 6), 2 * PLANE)], message.at[pl.ds(2 * PLANE, 2 * PLANE)]),
         ]
 
-    for flag, t, h in (
-        (even, (even_1, even_3), (odd_1, odd_3)),
-        (jnp.logical_not(even), (odd_1, odd_3), (even_1, even_3)),
+    def both_sides(zone, _, message):
+        return [(zone, message)]
+
+    for flag, t, h, te, he in (
+        (even, (even_1, even_2), (odd_1, odd_2), even_edge, odd_edge),
+        (jnp.logical_not(even), (odd_1, odd_2), (even_1, even_2), odd_edge, even_edge),
     ):
-        @pl.when(flag)
-        def _():
-            run_copies(out(tail, tail_edge, *t) + out(head, head_edge, *h), sem)
-
-
-def take_edges(even_1, odd_1, edges, sem):
-    rows = pl.ds(4 * PLANE, 8)
-    take_zones(even_1.at[rows], odd_1.at[rows], edges.at[0], edges.at[1], sem, is_even("curve"))
-
-
-def by_parity(evens, odds, tail, head, copies_in, sem):
+        for kind, out in by_kind(one_side, both_sides):
+            @pl.when(jnp.logical_and(flag, kind))
+            def _():
+                edges = [(tail_edge, te), (head_edge, he)]
+                run_copies(edges + out(tail, *t) + out(head, *h), sem)
+
+
+def by_kind(one_side, both_sides):
+    first, last = end_curves()
+    edge = jnp.logical_or(first, last)
+    return (edge, one_side), (jnp.logical_not(edge), both_sides)
+
+
+def by_parity(evens, odds, tail, head, one_side, both_sides, sem):
     even = is_even("curve")
     for flag, t, h in ((even, odds, evens), (jnp.logical_not(even), evens, odds)):
-        @pl.when(flag)
-        def _():
-            run_copies(copies_in(tail, *t) + copies_in(head, *h), sem)
+        for kind, to in by_kind(one_side, both_sides):
+            @pl.when(jnp.logical_and(flag, kind))
+            def _():
+                run_copies(to(tail, *t) + to(head, *h), sem)
 
 
 def to_plane(zone, start, count=1):
@@ -339,14 +346,14 @@
 
 
 def edge_kernel(
-    held_ref, _, pack, ends, even_1, odd_1,
+    held_ref, _, pack, ends, even_edge, odd_edge,
     new_pack, even_out, odd_out,
     edges, tail, head, sem,
 ):
     held = held_ref[0, 0]
     rank, ranks = lax.axis_index("curve"), lax.axis_size("curve")
     first_curve, last_curve = end_curves()
-    take_edges(even_1, odd_1, edges, sem)
+    take_zones(even_edge, odd_edge, edges.at[0], edges.at[1], sem, is_even("curve"))
     w = new_pack.at[pl.ds(PAD, CELLS * OWN)]
     lane, row = iota((64, LANES), 1), iota((64, LANES), 0)
     lone = jnp.logical_or(
@@ -419,9 +426,17 @@
         return jnp.where(self.from_tail, prev, jnp.where(self.from_head, after, mine))
 
 
-def drifts(held_ref, before_refs):
-    before = before_refs[0][0, 0] - lax.axis_index("curve") * AVG
-    return before, before + held_ref[0, 0] - AVG
+def drifts(held_ref, other_refs):
+    rank, count = lax.axis_index("curve"), lax.axis_size("curve")
+    held = held_ref[0, 0]
+    total, before = held, -rank * AVG
+    for i, ref in enumerate(other_refs):
+        other = jnp.max(ref[...]).astype(jnp.int32)
+        before += jnp.where(jnp.bitwise_and(rank, 1 << i) != 0, other, 0)
+        total += other
+    upper = jnp.bitwise_and(rank, 1 << len(other_refs)) != 0
+    before += jnp.where(upper, count * AVG - total, 0)
+    return before, before + held - AVG
 
 
 def send_faces(low, high, even_out, odd_out, sem):
@@ -449,23 +464,21 @@
 
 
 def align_kernel(
-    held_ref, before_refs, own, even_1, odd_1,
+    held_ref, before_refs, own, even_edge, odd_edge, even_1, odd_1, even_2, odd_2,
     even_out, odd_out, faces, sides,
     tail, head, edges, sem,
 ):
     before, after = drifts(held_ref, before_refs)
     even = is_even("curve")
 
-    def copies_in(zone, message):
-        first, last = end_curves()
-        other = pl.multiple_of(jnp.where(jnp.logical_or(first, last), 2 * PLANE, PLANE), 8)
-        return [
-            (message.at[pl.ds(0, PLANE)], to_plane(zone, plane_of(0, 0, 1))),
-            (message.at[pl.ds(PLANE, PLANE)], to_plane(zone, other)),
-        ]
-
-    by_parity((even_1,), (odd_1,), tail, head, copies_in, sem)
-    take_edges(even_1, odd_1, edges, sem)
+    def one_side(zone, message, _):
+        return [(message.at[pl.ds(0, PLANE)], to_plane(zone, plane_of(0, 0, 1)))]
+
+    def both_sides(zone, _, message):
+        return [(message.at[pl.ds(0, 2 * PLANE)], to_plane(zone, 0, 2))]
+
+    by_parity((even_1, even_2), (odd_1, odd_2), tail, head, one_side, both_sides, sem)
+    take_zones(even_edge, odd_edge, edges.at[0], edges.at[1], sem, even)
     here = Window(before, after)
 
     def body(k, carry):
@@ -515,7 +528,7 @@
 
 
 def face_kernel(
-    held_ref, before_refs, own, even_1, odd_1, even_3, odd_3,
+    held_ref, before_refs, own, even_1, odd_1, even_2, odd_2,
     even_face, odd_face, faces, sides,
     even_out, odd_out, even_end, odd_end, new, below, inner,
     tail, head, near, q, ends, sem,
@@ -524,16 +537,16 @@
     even = is_even("curve")
     half = 64 * WIN
 
-    def copies_in(zone, message_1, message_3):
-        first, last = end_curves()
-        rest = jnp.where(jnp.logical_or(first, last), 8 * PLANE, 4 * PLANE)
+    def one_side(zone, message, _):
         return [
-            (message_1.at[pl.ds(PLANE, PLANE)], to_plane(zone, plane_of(1, 2, 3))),
-            (message_1.at[pl.ds(2 * PLANE, 2 * PLANE)], to_plane(zone, plane_of(2, 4, 6), 2)),
-            (message_3, to_plane(zone, rest, 4)),
+            (message.at[pl.ds(PLANE, PLANE)], to_plane(zone, plane_of(1, 2, 3))),
+            (message.at[pl.ds(2 * PLANE, 2 * PLANE)], to_plane(zone, plane_of(2, 4, 6), 2)),
         ]
 
-    by_parity((even_1, even_3), (odd_1, odd_3), tail, head, copies_in, sem)
+    def both_sides(zone, _, message):
+        return [(message.at[pl.ds(2 * PLANE, 6 * PLANE)], to_plane(zone, 2 * PLANE, 6))]
+
+    by_parity((even_1, even_2), (odd_1, odd_2), tail, head, one_side, both_sides, sem)
     take_faces(even_face, odd_face, near.at[pl.ds(0, half)], near.at[pl.ds(half, half)], sem)
     here = Window(before, after)
 
@@ -588,17 +601,33 @@
 def last_kernel(
     held_ref, before_refs, own, even_in, odd_in, even_face, odd_face, even_end, odd_end,
     new, below, inner,
-    out,
-    tail, head, near, ends, sem,
+    result,
+    out, tail, head, near, ends, sem,
 ):
     before, after = drifts(held_ref, before_refs)
-    even = is_even("curve")
-    size = 8 * 64 * ZONE
+    even, even_curve = is_even("curve"), is_even("grp")
     half = 64 * WIN
-    zone = pl.ds(PAD, size)
-    take_zones(even_in, odd_in, tail.at[zone], head.at[zone], sem, even)
-    take_zones(even_end, odd_end, ends.at[0], ends.at[1], sem, even)
-    take_faces(even_face, odd_face, near.at[pl.ds(0, half)], near.at[pl.ds(half, half)], sem)
+    zone = pl.ds(PAD, 8 * 64 * ZONE)
+    low, high = near.at[pl.ds(0, half)], near.at[pl.ds(half, half)]
+    places = (tail.at[zone], head.at[zone], ends.at[0], ends.at[1], low, high)
+    evens = (odd_in, even_in, odd_end, even_end)
+    odds = (even_in, odd_in, even_end, odd_end)
+    for flag, sources in ((even, evens), (jnp.logical_not(even), odds)):
+        @pl.when(flag)
+        def _():
+            for copy in copies(list(zip(sources, places)), sem):
+                copy.start()
+
+    for flag, sources in (
+        (even_curve, (odd_face, even_face)), (jnp.logical_not(even_curve), (even_face, odd_face))
+    ):
+        @pl.when(flag)
+        def _():
+            for i, source in enumerate(sources):
+                pltpu.make_async_copy(source, places[4 + i], sem.at[4 + i]).start()
+
+    for copy in copies(list(zip(evens + (even_face, odd_face), places)), sem):
+        copy.wait()
     here = Window(before, after)
     lane, row = here.lane, here.row
     outer = end_curves()
@@ -646,42 +675,55 @@
         for y in range(2, 6):
             for z in range(8):
                 put(x, y, z, get(y, x, z))
+        store(x).start()
+
+    def store(x):
+        start = x * half
+        rows = pl.ds(start if isinstance(start, int) else pl.multiple_of(start, 8), half)
+        return pltpu.make_async_copy(out.at[rows], result.at[rows], sem.at[6 + x])
 
     each_x(run)
-
-
-def swapped(value, axis, first, inner):
+    for x in range(8):
+        store(x).wait()
+
+
+def swapped(value, axis, first, curves):
     count = lax.axis_size(axis)
     pairs = [(i, i + 1) for i in range(first, count - 1, 2)]
     pairs += [(b, a) for a, b in pairs]
-    if inner:
-        curves = lax.axis_size("grp")
-        pairs = [(a * curves + g, b * curves + g) for a, b in pairs for g in range(1, curves - 1)]
+    if curves is not None:
+        all_curves = lax.axis_size("grp")
+        pairs = [(a * all_curves + g, b * all_curves + g) for a, b in pairs for g in curves]
         axis = (axis, "grp")
     return lax.ppermute(value, axis, pairs)
 
 
-def swaps(values, axis, inner=False):
+def swaps(values, axis, curves=None):
     got = []
     for first, value in enumerate(values):
-        got.append(swapped(value, axis, first, inner))
+        got.append(swapped(value, axis, first, curves))
     return got
 
 
-def held_before(counts):
-    rank, count = lax.axis_index("curve"), lax.axis_size("curve")
-    places = [i for i in range(count) if 1 << i < count]
-    above = [jnp.bitwise_and(rank >> i, 1).reshape(1, 1) for i in places]
-    total, *above = lax.optimization_barrier((counts, *above))
-    before = jnp.zeros_like(counts)
-    for i in places[:-1]:
+def add_kernel(a_ref, b_ref, sum_ref):
+    sum_ref[...] = a_ref[...] + b_ref[...]
+
+
+def counts_swapped(total):
+    count, others = lax.axis_size("curve"), []
+    vmem = pl.BlockSpec(memory_space=pltpu.VMEM)
+    for i in range((count - 1).bit_length() - 1):
+        if others:
+            total = pl.pallas_call(
+                add_kernel,
+                out_shape=array(8, LANES),
+                in_specs=[vmem, vmem],
+                out_specs=vmem,
+                compiler_params=pltpu.CompilerParams(vmem_limit_bytes=2**20),
+            )(total, others[-1])
         pairs = [(a, a ^ 1 << i) for a in range(count) if a ^ 1 << i < count]
-        other = lax.ppermute(total, "curve", pairs)
-        before += above[i] * other
-        total += other
-    for top in above[len(places) - 1 :]:
-        before += top * (count * AVG - total)
-    return before
+        others.append(lax.ppermute(total, "curve", pairs))
+    return others
 
 
 def array(*shape):
@@ -691,7 +733,7 @@
 def call(kernel, outs, ins, scratch, limit, vmem_ins=(), vmem_outs=(), hbm_ins=(), us=2, aliases={}):
     (held,), others, *arrays = ins
     vmem = pl.BlockSpec(memory_space=pltpu.VMEM)
-    specs = [SMEM] * (1 + len(others))
+    specs = [SMEM] + [vmem] * len(others)
     specs += [
         vmem if i in vmem_ins else HBM if i in hbm_ins else ANY for i in range(len(arrays))
     ]
@@ -704,7 +746,7 @@
         out_shape=outs,
         in_specs=specs,
         out_specs=[vmem if i in vmem_outs else ANY for i in range(len(outs))],
-        scratch_shapes=[pltpu.VMEM(shape, F32) for shape in scratch] + [pltpu.SemaphoreType.DMA((10,))],
+        scratch_shapes=[pltpu.VMEM(shape, F32) for shape in scratch] + [pltpu.SemaphoreType.DMA((16,))],
         compiler_params=pltpu.CompilerParams(vmem_limit_bytes=limit * 2**20),
         cost_estimate=pl.CostEstimate(flops=us * 4_000_000, bytes_accessed=us * 10**6, transcendentals=0),
         input_output_aliases=aliases,
@@ -718,18 +760,21 @@
     zone = 64 * ZONE
     win = 64 * WIN
 
-    others = (held_before(counts),)
     message, edge = (8 * zone, LANES), (8, LANES)
-    outs = call(
+    *outs, count = call(
         front_kernel,
-        [array(4 * zone + 8, LANES)] * 2 + [array(4 * zone, LANES)] * 2,
+        [array(*edge)] * 2 + [array(4 * zone, LANES)] * 2 + [array(*message)] * 2 + [array(8, LANES)],
         ((counts,), (), state2, coef2),
         [message, message, edge, edge],
         limit=6,
         vmem_ins=(0, 1),
+        vmem_outs=(6,),
     )
-    in_1 = swaps(outs[:2], "curve")
-    in_3 = swaps(outs[2:], "curve", inner=True)
+    curves = lax.axis_size("grp")
+    edges_in = swaps(outs[:2], "curve")
+    others = counts_swapped(count)
+    planes_in = swaps(outs[2:4], "curve", (0, curves - 1))
+    planes_in += swaps(outs[4:], "curve", range(1, curves - 1))
     front, pack, ends = call(
         sweep_kernel,
         [array(rows + 2 * PAD, LANES)] * 2 + [array(6 * 64, LANES)],
@@ -743,7 +788,7 @@
     pack, *sweep_out = call(
         edge_kernel,
         [array(rows + 2 * PAD, LANES)] + [array(*message)] * 2,
-        ((counts,), (), pack, ends, *in_1),
+        ((counts,), (), pack, ends, *edges_in),
         [(2, 8, LANES), message, message],
         limit=8,
         vmem_ins=(0, 1),
@@ -754,8 +799,8 @@
     *near_out, faces, sides = call(
         align_kernel,
         [array(win, LANES)] * 2 + [array(2 * win, LANES), array(32 * WIN, LANES)],
-        ((counts,), others, front, *in_1),
-        [(3 * zone + 2 * PAD, LANES), (3 * zone + 2 * PAD, LANES), (2, 8, LANES)],
+        ((counts,), others, front, *edges_in, *planes_in),
+        [(2 * zone + 2 * PAD, LANES), (2 * zone + 2 * PAD, LANES), (2, 8, LANES)],
         limit=8,
         vmem_ins=(0,),
         vmem_outs=(2, 3),
@@ -764,9 +809,9 @@
     near_a, near_b, end_a, end_b, new, below, inner = call(
         face_kernel,
         [array(win, LANES)] * 2 + [array(16, LANES)] * 2 + [array(2 * win, LANES)] * 3,
-        ((counts,), others, front, *in_1, *in_3, *near_in, faces, sides),
+        ((counts,), others, front, *planes_in, *near_in, faces, sides),
         [
-            (12 * zone + 2 * PAD, LANES), (12 * zone + 2 * PAD, LANES),
+            (8 * zone + 2 * PAD, LANES), (8 * zone + 2 * PAD, LANES),
             (2 * win, LANES), (2 * win, LANES), (2, 16, LANES),
         ],
         limit=8,
@@ -781,12 +826,11 @@
         [array(CELLS * WIN, LANES)],
         ((counts,), others, pack, *sweep_in, *near_in, *end_in, new, below, inner),
         [
-            (8 * zone + 2 * PAD, LANES), (8 * zone + 2 * PAD, LANES),
+            (CELLS * WIN, LANES), (8 * zone + 2 * PAD, LANES), (8 * zone + 2 * PAD, LANES),
             (2 * win, LANES), (2, 16, LANES),
         ],
         limit=12,
         vmem_ins=(0, 7, 8, 9),
-        vmem_outs=(0,),
         us=3,
     )
     return out.reshape(CELLS, 1, AVG)

time: 75.8 us -> 77.6 us (1.024)
  the two profiles are of different devices: /device:TPU:6 before, /device:TPU:16 now
where the time goes in v4:
time: 77.6 us; the launch traced here: 77.3 us
  starting transfers between devices  29.4 us (38%)
  waiting for transfers between devices  26 us (34%)
  Pallas kernels  16.4 us (21%)
  local copies, waits for them, and re-layouts  4.67 us (6%)
  between operations  0.88 us (1%)
    ppermute x14, starting transfers between devices, swapped(): return lax.ppermute(value, axis, pairs)  25.1 us
    pallas_call x6, Pallas kernels, call(): pl.pallas_call(body, out_shape=outs, in_specs=specs, out_specs=[vmem if i...  16.4 us
    ppermute x14, waiting for transfers between devices, swapped(): return lax.ppermute(value, axis, pairs)  15.1 us
    ppermute x2, waiting for transfers between devices, counts_swapped(): others.append(lax.ppermute(total, 'curve', pairs))  11 us
    unnamed x8, local copies, waits for them, and re-layouts  4.67 us
    ppermute x2, starting transfers between devices, counts_swapped(): others.append(lax.ppermute(total, 'curve', pairs))  4.26 us
  transfers between devices with their start and end apart: 16, of which 5 were waited for; matrix products, arithmetic and copies ran while one was open for 0% of the time, Pallas kernels for 15%

profile of v4, /device:TPU:16, one launch (start us, length us, event | category | flops | bytes accessed | tf_op | source)
XLA Modules:
  0.0 77.3 jit_solution(15189202998902990547)
XLA Ops:
  0.7 2.8 %copy-done = f32[2,512,1,1536]{3,2,1,0:T(1,128)S(1)} copy-done((f32[2,512,1,1536]{3,2,1,0:T(1,128)S(1)}, f32[2,512,1,1536]{3,2,1,0:T(1,128)}, u32[]{:S(2)}) %copy-start) | copy-done | bytes 6291480
  3.4 1.9 %copy-done.2 = f32[512,1,1536]{2,1,0:T(1,128)S(1)} copy-done((f32[512,1,1536]{2,1,0:T(1,128)S(1)}, f32[512,1,1536]{2,1,0:T(1,128)}, u32[]{:S(2)}) %copy-start.2) | copy-done | bytes 3145752
  5.3 1.2 %shard_map.37 = (f32[8,128]{1,0:T(8,128)S(1)}, f32[8,128]{1,0:T(8,128)S(1)}, f32[512,128]{1,0:T(8,128)S(1)}, f32[512,128]{1,0:T(8,128)S(1)}, f32[1024,128]{1,0:T...) custom-call(s32[1,1]{1,0:T(1,128)S(6)} %copy.7.held_ref, f32[12288,128]{1,0:T(8,128)S(1)} %bitcast.3, ...), custom_call_target="tpu_custom_call" | custom-call | flops 8000000 | bytes 2000000 | tf_op jit(solution)/shard_map/pallas_call | solution.py:744
  6.6 0.8 %collective-permute-start.8 = (f32[1024,128]{1,0:T(8,128)S(1)}, f32[1024,128]{1,0:T(8,128)S(1)}, u32[]{:S(2)}, u32[]{:S(2)}) collective-permute-start(f32[1024,128]{1,0:T(8,128)S(1)} %get-tuple-element.40), channel_id=1, source_target_pairs={{1,5},{2,6},{9,13},{10,14},{17,21},{18,22},{25,29},{26,30},{5,1},{... | collective-permute-start | bytes 1572872 | tf_op jit(solution)/shard_map/ppermute | solution.py:698
  8.2 3.4 %collective-permute-start.6 = (f32[512,128]{1,0:T(8,128)S(1)}, f32[512,128]{1,0:T(8,128)S(1)}, u32[]{:S(2)}, u32[]{:S(2)}) collective-permute-start(f32[512,128]{1,0:T(8,128)S(1)} %get-tuple-element.38), channel_id=1, source_target_pairs={{0,4},{3,7},{8,12},{11,15},{16,20},{19,23},{24,28},{27,31},{4,0},{... | collective-permute-start | bytes 786440 | tf_op jit(solution)/shard_map/ppermute | solution.py:698
  11.6 2.3 %collective-permute-start.7 = (f32[512,128]{1,0:T(8,128)S(1)}, f32[512,128]{1,0:T(8,128)S(1)}, u32[]{:S(2)}, u32[]{:S(2)}) collective-permute-start(f32[512,128]{1,0:T(8,128)S(1)} %get-tuple-element.39), channel_id=1, source_target_pairs={{4,8},{7,11},{12,16},{15,19},{20,24},{23,27},{8,4},{11,7},{16,12},... | collective-permute-start | bytes 786440 | tf_op jit(solution)/shard_map/ppermute | solution.py:698
  14.0 2.7 %collective-permute-start = (f32[8,128]{1,0:T(8,128)S(1)}, f32[8,128]{1,0:T(8,128)S(1)}, u32[]{:S(2)}, u32[]{:S(2)}) collective-permute-start(f32[8,128]{1,0:T(8,128)S(1)} %get-tuple-element.29.a_ref), channel_id=1, source_target_pairs={{0,4},{4,0},{8,12},{12,8},{16,20},{20,16},{24,28},{28,24},{1,5},{5... | collective-permute-start | bytes 12296 | tf_op jit(solution)/shard_map/ppermute | solution.py:725
  16.6 10.9 %collective-permute-done.b_ref.refs_0_ = f32[8,128]{1,0:T(8,128)S(1)} collective-permute-done((f32[8,128]{1,0:T(8,128)S(1)}, f32[8,128]{1,0:T(8,128)S(1)}, u32[]{:S(2)}, u32[]{:S(2)}) %collective-permute-start) | collective-permute-done | bytes 4128 | tf_op jit(solution)/shard_map/ppermute | solution.py:725
  27.6 1.4 %collective-permute-start.2 = (f32[8,128]{1,0:T(8,128)S(1)}, f32[8,128]{1,0:T(8,128)S(1)}, u32[]{:S(2)}, u32[]{:S(2)}) collective-permute-start(f32[8,128]{1,0:T(8,128)S(1)} %get-tuple-element.32), channel_id=1, source_target_pairs={{0,4},{8,12},{16,20},{24,28},{4,0},{12,8},{20,16},{28,24},{1,5},{9... | collective-permute-start | bytes 12296 | tf_op jit(solution)/shard_map/ppermute | solution.py:698
  29.0 2.2 %collective-permute-done.2.refs_2_.refs_3_ = f32[8,128]{1,0:T(8,128)S(1)} collective-permute-done((f32[8,128]{1,0:T(8,128)S(1)}, f32[8,128]{1,0:T(8,128)S(1)}, u32[]{:S(2)}, u32[]{:S(2)}) %collective-permute-start.2) | collective-permute-done | bytes 4128 | tf_op jit(solution)/shard_map/ppermute | solution.py:698
  31.2 3.1 %collective-permute-start.3 = (f32[8,128]{1,0:T(8,128)S(1)}, f32[8,128]{1,0:T(8,128)S(1)}, u32[]{:S(2)}, u32[]{:S(2)}) collective-permute-start(f32[8,128]{1,0:T(8,128)S(1)} %get-tuple-element.33), channel_id=1, source_target_pairs={{4,8},{12,16},{20,24},{8,4},{16,12},{24,20},{5,9},{13,17},{21,25},... | collective-permute-start | bytes 12296 | tf_op jit(solution)/shard_map/ppermute | solution.py:698
  34.4 3.2 %collective-permute-done.3.refs_3_.refs_4_ = f32[8,128]{1,0:T(8,128)S(1)} collective-permute-done((f32[8,128]{1,0:T(8,128)S(1)}, f32[8,128]{1,0:T(8,128)S(1)}, u32[]{:S(2)}, u32[]{:S(2)}) %collective-permute-start.3) | collective-permute-done | bytes 4128 | tf_op jit(solution)/shard_map/ppermute | solution.py:698
  37.6 1.6 %collective-permute-start.1 = (f32[8,128]{1,0:T(8,128)S(1)}, f32[8,128]{1,0:T(8,128)S(1)}, u32[]{:S(2)}, u32[]{:S(2)}) collective-permute-start(f32[8,128]{1,0:T(8,128)S(1)} %shard_map.38), channel_id=1, source_target_pairs={{0,8},{4,12},{8,0},{12,4},{16,24},{20,28},{24,16},{28,20},{1,9},{5... | collective-permute-start | bytes 12296 | tf_op jit(solution)/shard_map/ppermute | solution.py:725
  39.2 5.1 %shard_map.39 = (f32[6176,128]{1,0:T(8,128)S(1)}, f32[6176,128]{1,0:T(8,128)S(1)}, f32[384,128]{1,0:T(8,128)S(1)}) custom-call(s32[1,1]{1,0:T(1,128)S(6)} %copy.7.held_ref, f32[12288,128]{1,0:T(8,128)S(1)} %bitcast.4, f32[6144,128]{1,0:T(8,128)S(1)} %bitcast.6), custom_call_target="tpu_custom_call" | custom-call | flops 24000000 | bytes 6000000 | tf_op jit(solution)/shard_map/pallas_call | solution.py:744
  44.3 1.1 %shard_map.40 = (f32[6176,128]{1,0:T(8,128)S(1)}, f32[1024,128]{1,0:T(8,128)S(1)}, f32[1024,128]{1,0:T(8,128)S(1)}) custom-call(s32[1,1]{1,0:T(1,128)S(6)} %copy.7.held_ref, f32[6176,128]{1,0:T(8,128)S(1)} %get-tuple-element.30.refs_0_, f32[384,128]{1,0:T(8,128)S(1)} %get-tuple-element.31.refs_1_, ...), custom_call_target="tpu_custom_call", output_to_operand_aliasing={{0}: (1, {})} | custom-call | flops 8000000 | bytes 2000000 | tf_op jit(solution)/shard_map/pallas_call | solution.py:744
  45.6 2.3 %shard_map.41 = (f32[512,128]{1,0:T(8,128)S(1)}, f32[512,128]{1,0:T(8,128)S(1)}, f32[1024,128]{1,0:T(8,128)S(1)}, f32[256,128]{1,0:T(8,128)S(1)}) custom-call(s32[1,1]{1,0:T(1,128)S(6)} %copy.7.held_ref, f32[8,128]{1,0:T(8,128)S(1)} %collective-permute-done.b_ref.refs_0_, f32[8,128]{1,0:T(8,128)S(1)} %collective-permute-done.1.refs_1_, ...), custom_call_target="tpu_custom_call" | custom-call | flops 8000000 | bytes 2000000 | tf_op jit(solution)/shard_map/pallas_call | solution.py:744
  48.6 2.2 %collective-permute-start.5 = (f32[1024,128]{1,0:T(8,128)S(1)}, f32[1024,128]{1,0:T(8,128)S(1)}, u32[]{:S(2)}, u32[]{:S(2)}) collective-permute-start(f32[1024,128]{1,0:T(8,128)S(1)} %get-tuple-element.36), channel_id=1, source_target_pairs={{4,8},{12,16},{20,24},{8,4},{16,12},{24,20},{5,9},{13,17},{21,25},... | collective-permute-start | bytes 1572872 | tf_op jit(solution)/shard_map/ppermute | solution.py:698
  50.9 3.0 %shard_map.42 = (f32[512,128]{1,0:T(8,128)S(1)}, f32[512,128]{1,0:T(8,128)S(1)}, f32[16,128]{1,0:T(8,128)S(1)}, f32[16,128]{1,0:T(8,128)S(1)}, f32[1024,128]{1,0...) custom-call(s32[1,1]{1,0:T(1,128)S(6)} %copy.7.held_ref, ...), custom_call_target="tpu_custom_call" | custom-call | flops 12000000 | bytes 3000000 | tf_op jit(solution)/shard_map/pallas_call | solution.py:744
  53.9 5.5 %collective-permute-start.12 = (f32[512,128]{1,0:T(8,128)S(1)}, f32[512,128]{1,0:T(8,128)S(1)}, u32[]{:S(2)}, u32[]{:S(2)}) collective-permute-start(f32[512,128]{1,0:T(8,128)S(1)} %get-tuple-element.46), channel_id=1, source_target_pairs={{0,1},{2,3},{1,0},{3,2},{4,5},{6,7},{5,4},{7,6},{8,9},{10,11},{9,8... | collective-permute-start | bytes 786440 | tf_op jit(solution)/shard_map/ppermute | solution.py:698
  60.1 2.1 %collective-permute-start.14 = (f32[16,128]{1,0:T(8,128)S(1)}, f32[16,128]{1,0:T(8,128)S(1)}, u32[]{:S(2)}, u32[]{:S(2)}) collective-permute-start(f32[16,128]{1,0:T(8,128)S(1)} %get-tuple-element.48), channel_id=1, source_target_pairs={{0,4},{8,12},{16,20},{24,28},{4,0},{12,8},{20,16},{28,24},{1,5},{9... | collective-permute-start | bytes 24584 | tf_op jit(solution)/shard_map/ppermute | solution.py:698
  62.1 5.2 %collective-permute-done.4.refs_3_ = f32[1024,128]{1,0:T(8,128)S(1)} collective-permute-done((f32[1024,128]{1,0:T(8,128)S(1)}, f32[1024,128]{1,0:T(8,128)S(1)}, u32[]{:S(2)}, u32[]{:S(2)}) %collective-permute-start.4) | collective-permute-done | bytes 524320 | tf_op jit(solution)/shard_map/ppermute | solution.py:698
  67.3 2.0 %collective-permute-start.15 = (f32[16,128]{1,0:T(8,128)S(1)}, f32[16,128]{1,0:T(8,128)S(1)}, u32[]{:S(2)}, u32[]{:S(2)}) collective-permute-start(f32[16,128]{1,0:T(8,128)S(1)} %get-tuple-element.49), channel_id=1, source_target_pairs={{4,8},{12,16},{20,24},{8,4},{16,12},{24,20},{5,9},{13,17},{21,25},... | collective-permute-start | bytes 24584 | tf_op jit(solution)/shard_map/ppermute | solution.py:698
  69.3 4.4 %collective-permute-done.15.refs_8_ = f32[16,128]{1,0:T(8,128)S(1)} collective-permute-done((f32[16,128]{1,0:T(8,128)S(1)}, f32[16,128]{1,0:T(8,128)S(1)}, u32[]{:S(2)}, u32[]{:S(2)}) %collective-permute-start.15) | collective-permute-done | bytes 8224 | tf_op jit(solution)/shard_map/ppermute | solution.py:698
  73.7 3.6 %shard_map.43 = f32[4096,128]{1,0:T(8,128)} custom-call(s32[1,1]{1,0:T(1,128)S(6)} %copy.7.held_ref, f32[8,128]{1,0:T(8,128)S(1)} %collective-permute-done.b_ref.refs_0_, f32[8,128]{1,0:T(8,128)S(1)} %collective-permute-done.1.refs_1_, f32[6176,128]{1,0:T(8,128)S(1)} %get-tuple-element.34.refs_2_, f32[1024,128]{1,0:T(8,128)S(1)} %collective-permute-done.4.refs_3_, ...), custom_call_target="tpu_custom_call" | custom-call | flops 12000000 | bytes 3000000 | tf_op jit(solution)/shard_map/pallas_call | solution.py:744
  (23 shorter events, 2.4 us)
Async XLA Ops:
  0.7 2.8 %copy-start = (f32[2,512,1,1536]{3,2,1,0:T(1,128)S(1)}, f32[2,512,1,1536]{3,2,1,0:T(1,128)}, u32[]{:S(2)}) copy-start(f32[2,512,1,1536]{3,2,1,0:T(1,128)} %param.3) | copy-start | bytes 18874372
  3.4 1.9 %copy-start.2 = (f32[512,1,1536]{2,1,0:T(1,128)S(1)}, f32[512,1,1536]{2,1,0:T(1,128)}, u32[]{:S(2)}) copy-start(f32[512,1,1536]{2,1,0:T(1,128)} %param.4) | copy-start | bytes 9437188
  5.3 33.8 %copy-start.1 = (f32[2,512,1,1536]{3,2,1,0:T(1,128)S(1)}, f32[2,512,1,1536]{3,2,1,0:T(1,128)}, u32[]{:S(2)}) copy-start(f32[2,512,1,1536]{3,2,1,0:T(1,128)} %param.3) | copy-start | bytes 18874372
  5.3 33.8 %copy-start.3 = (f32[512,1,1536]{2,1,0:T(1,128)S(1)}, f32[512,1,1536]{2,1,0:T(1,128)}, u32[]{:S(2)}) copy-start(f32[512,1,1536]{2,1,0:T(1,128)} %param.4) | copy-start | bytes 9437188
  6.6 39.0 %collective-permute-start.8 = (f32[1024,128]{1,0:T(8,128)S(1)}, f32[1024,128]{1,0:T(8,128)S(1)}, u32[]{:S(2)}, u32[]{:S(2)}) collective-permute-start(f32[1024,128]{1,0:T(8,128)S(1)} %get-tuple-element.40), channel_id=1, source_target_pairs={{1,5},{2,6},{9,13},{10,14},{17,21},{18,22},{25,29},{26,30},{5,1},{... | collective-permute-start | bytes 1572872 | tf_op jit(solution)/shard_map/ppermute | solution.py:698
  7.4 38.2 %collective-permute-start.9 = (f32[1024,128]{1,0:T(8,128)S(1)}, f32[1024,128]{1,0:T(8,128)S(1)}, u32[]{:S(2)}, u32[]{:S(2)}) collective-permute-start(f32[1024,128]{1,0:T(8,128)S(1)} %get-tuple-element.41), channel_id=1, source_target_pairs={{5,9},{6,10},{13,17},{14,18},{21,25},{22,26},{9,5},{10,6},{17,13},... | collective-permute-start | bytes 1572872 | tf_op jit(solution)/shard_map/ppermute | solution.py:698
  8.2 37.3 %collective-permute-start.6 = (f32[512,128]{1,0:T(8,128)S(1)}, f32[512,128]{1,0:T(8,128)S(1)}, u32[]{:S(2)}, u32[]{:S(2)}) collective-permute-start(f32[512,128]{1,0:T(8,128)S(1)} %get-tuple-element.38), channel_id=1, source_target_pairs={{0,4},{3,7},{8,12},{11,15},{16,20},{19,23},{24,28},{27,31},{4,0},{... | collective-permute-start | bytes 786440 | tf_op jit(solution)/shard_map/ppermute | solution.py:698
  11.6 33.9 %collective-permute-start.7 = (f32[512,128]{1,0:T(8,128)S(1)}, f32[512,128]{1,0:T(8,128)S(1)}, u32[]{:S(2)}, u32[]{:S(2)}) collective-permute-start(f32[512,128]{1,0:T(8,128)S(1)} %get-tuple-element.39), channel_id=1, source_target_pairs={{4,8},{7,11},{12,16},{15,19},{20,24},{23,27},{8,4},{11,7},{16,12},... | collective-permute-start | bytes 786440 | tf_op jit(solution)/shard_map/ppermute | solution.py:698
  14.0 13.6 %collective-permute-start = (f32[8,128]{1,0:T(8,128)S(1)}, f32[8,128]{1,0:T(8,128)S(1)}, u32[]{:S(2)}, u32[]{:S(2)}) collective-permute-start(f32[8,128]{1,0:T(8,128)S(1)} %get-tuple-element.29.a_ref), channel_id=1, source_target_pairs={{0,4},{4,0},{8,12},{12,8},{16,20},{20,16},{24,28},{28,24},{1,5},{5... | collective-permute-start | bytes 12296 | tf_op jit(solution)/shard_map/ppermute | solution.py:725
  27.6 3.6 %collective-permute-start.2 = (f32[8,128]{1,0:T(8,128)S(1)}, f32[8,128]{1,0:T(8,128)S(1)}, u32[]{:S(2)}, u32[]{:S(2)}) collective-permute-start(f32[8,128]{1,0:T(8,128)S(1)} %get-tuple-element.32), channel_id=1, source_target_pairs={{0,4},{8,12},{16,20},{24,28},{4,0},{12,8},{20,16},{28,24},{1,5},{9... | collective-permute-start | bytes 12296 | tf_op jit(solution)/shard_map/ppermute | solution.py:698
  31.2 6.4 %collective-permute-start.3 = (f32[8,128]{1,0:T(8,128)S(1)}, f32[8,128]{1,0:T(8,128)S(1)}, u32[]{:S(2)}, u32[]{:S(2)}) collective-permute-start(f32[8,128]{1,0:T(8,128)S(1)} %get-tuple-element.33), channel_id=1, source_target_pairs={{4,8},{12,16},{20,24},{8,4},{16,12},{24,20},{5,9},{13,17},{21,25},... | collective-permute-start | bytes 12296 | tf_op jit(solution)/shard_map/ppermute | solution.py:698
  37.6 7.9 %collective-permute-start.1 = (f32[8,128]{1,0:T(8,128)S(1)}, f32[8,128]{1,0:T(8,128)S(1)}, u32[]{:S(2)}, u32[]{:S(2)}) collective-permute-start(f32[8,128]{1,0:T(8,128)S(1)} %shard_map.38), channel_id=1, source_target_pairs={{0,8},{4,12},{8,0},{12,4},{16,24},{20,28},{24,16},{28,20},{1,9},{5... | collective-permute-start | bytes 12296 | tf_op jit(solution)/shard_map/ppermute | solution.py:725
  45.5 21.8 %collective-permute-start.4 = (f32[1024,128]{1,0:T(8,128)S(1)}, f32[1024,128]{1,0:T(8,128)S(1)}, u32[]{:S(2)}, u32[]{:S(2)}) collective-permute-start(f32[1024,128]{1,0:T(8,128)S(1)} %get-tuple-element.35), channel_id=1, source_target_pairs={{0,4},{8,12},{16,20},{24,28},{4,0},{12,8},{20,16},{28,24},{1,5},{9... | collective-permute-start | bytes 1572872 | tf_op jit(solution)/shard_map/ppermute | solution.py:698
  47.9 3.0 %collective-permute-start.10 = (f32[512,128]{1,0:T(8,128)S(1)}, f32[512,128]{1,0:T(8,128)S(1)}, u32[]{:S(2)}, u32[]{:S(2)}) collective-permute-start(f32[512,128]{1,0:T(8,128)S(1)} %get-tuple-element.42), channel_id=1, source_target_pairs={{0,1},{2,3},{1,0},{3,2},{4,5},{6,7},{5,4},{7,6},{8,9},{10,11},{9,8... | collective-permute-start | bytes 786440 | tf_op jit(solution)/shard_map/ppermute | solution.py:698
  47.9 2.9 %collective-permute-start.11 = (f32[512,128]{1,0:T(8,128)S(1)}, f32[512,128]{1,0:T(8,128)S(1)}, u32[]{:S(2)}, u32[]{:S(2)}) collective-permute-start(f32[512,128]{1,0:T(8,128)S(1)} %get-tuple-element.43), channel_id=1, source_target_pairs={{1,2},{2,1},{5,6},{6,5},{9,10},{10,9},{13,14},{14,13},{17,18},{18,... | collective-permute-start | bytes 786440 | tf_op jit(solution)/shard_map/ppermute | solution.py:698
  48.6 20.7 %collective-permute-start.5 = (f32[1024,128]{1,0:T(8,128)S(1)}, f32[1024,128]{1,0:T(8,128)S(1)}, u32[]{:S(2)}, u32[]{:S(2)}) collective-permute-start(f32[1024,128]{1,0:T(8,128)S(1)} %get-tuple-element.36), channel_id=1, source_target_pairs={{4,8},{12,16},{20,24},{8,4},{16,12},{24,20},{5,9},{13,17},{21,25},... | collective-permute-start | bytes 1572872 | tf_op jit(solution)/shard_map/ppermute | solution.py:698
  53.9 19.8 %collective-permute-start.12 = (f32[512,128]{1,0:T(8,128)S(1)}, f32[512,128]{1,0:T(8,128)S(1)}, u32[]{:S(2)}, u32[]{:S(2)}) collective-permute-start(f32[512,128]{1,0:T(8,128)S(1)} %get-tuple-element.46), channel_id=1, source_target_pairs={{0,1},{2,3},{1,0},{3,2},{4,5},{6,7},{5,4},{7,6},{8,9},{10,11},{9,8... | collective-permute-start | bytes 786440 | tf_op jit(solution)/shard_map/ppermute | solution.py:698
  59.4 14.3 %collective-permute-start.13 = (f32[512,128]{1,0:T(8,128)S(1)}, f32[512,128]{1,0:T(8,128)S(1)}, u32[]{:S(2)}, u32[]{:S(2)}) collective-permute-start(f32[512,128]{1,0:T(8,128)S(1)} %get-tuple-element.47), channel_id=1, source_target_pairs={{1,2},{2,1},{5,6},{6,5},{9,10},{10,9},{13,14},{14,13},{17,18},{18,... | collective-permute-start | bytes 786440 | tf_op jit(solution)/shard_map/ppermute | solution.py:698
  60.1 9.2 %collective-permute-start.14 = (f32[16,128]{1,0:T(8,128)S(1)}, f32[16,128]{1,0:T(8,128)S(1)}, u32[]{:S(2)}, u32[]{:S(2)}) collective-permute-start(f32[16,128]{1,0:T(8,128)S(1)} %get-tuple-element.48), channel_id=1, source_target_pairs={{0,4},{8,12},{16,20},{24,28},{4,0},{12,8},{20,16},{28,24},{1,5},{9... | collective-permute-start | bytes 24584 | tf_op jit(solution)/shard_map/ppermute | solution.py:698
  67.3 6.4 %collective-permute-start.15 = (f32[16,128]{1,0:T(8,128)S(1)}, f32[16,128]{1,0:T(8,128)S(1)}, u32[]{:S(2)}, u32[]{:S(2)}) collective-permute-start(f32[16,128]{1,0:T(8,128)S(1)} %get-tuple-element.49), channel_id=1, source_target_pairs={{4,8},{12,16},{20,24},{8,4},{16,12},{24,20},{5,9},{13,17},{21,25},... | collective-permute-start | bytes 24584 | tf_op jit(solution)/shard_map/ppermute | solution.py:698

commit v5 on v4

--- a/solution.py
+++ b/solution.py
@@ -160,15 +160,18 @@
 
     count[...] = jnp.full((8, LANES), held, jnp.int32).astype(F32)
 
-    def one_side(zone, message, _):
+    def common(zone, edge, message):
         return [
             (zone.at[pl.ds(plane_of(0, 0, 1), PLANE)], message.at[pl.ds(0, PLANE)]),
             (zone.at[pl.ds(plane_of(1, 2, 3), PLANE)], message.at[pl.ds(PLANE, PLANE)]),
-            (zone.at[pl.ds(plane_of(2, 4, 6), 2 * PLANE)], message.at[pl.ds(2 * PLANE, 2 * PLANE)]),
+            (edge, message.at[pl.ds(2 * PLANE, 8)]),
         ]
 
+    def one_side(zone, message, _):
+        return [(zone.at[pl.ds(plane_of(2, 4, 6), 2 * PLANE)], message)]
+
     def both_sides(zone, _, message):
-        return [(zone, message)]
+        return [(zone.at[pl.ds(2 * PLANE, 6 * PLANE)], message)]
 
     for flag, t, h, te, he in (
         (even, (even_1, even_2), (odd_1, odd_2), even_edge, odd_edge),
@@ -177,8 +180,8 @@
         for kind, out in by_kind(one_side, both_sides):
             @pl.when(jnp.logical_and(flag, kind))
             def _():
-                edges = [(tail_edge, te), (head_edge, he)]
-                run_copies(edges + out(tail, *t) + out(head, *h), sem)
+                first = common(tail, tail_edge, te) + common(head, head_edge, he)
+                run_copies(first + out(tail, *t) + out(head, *h), sem)
 
 
 def by_kind(one_side, both_sides):
@@ -194,6 +197,13 @@
             @pl.when(jnp.logical_and(flag, kind))
             def _():
                 run_copies(to(tail, *t) + to(head, *h), sem)
+
+
+def take_edges(even_edge, odd_edge, edges, sem):
+    rows = pl.ds(2 * PLANE, 8)
+    take_zones(
+        even_edge.at[rows], odd_edge.at[rows], edges.at[0], edges.at[1], sem, is_even("curve")
+    )
 
 
 def to_plane(zone, start, count=1):
@@ -353,7 +363,7 @@
     held = held_ref[0, 0]
     rank, ranks = lax.axis_index("curve"), lax.axis_size("curve")
     first_curve, last_curve = end_curves()
-    take_zones(even_edge, odd_edge, edges.at[0], edges.at[1], sem, is_even("curve"))
+    take_edges(even_edge, odd_edge, edges, sem)
     w = new_pack.at[pl.ds(PAD, CELLS * OWN)]
     lane, row = iota((64, LANES), 1), iota((64, LANES), 0)
     lone = jnp.logical_or(
@@ -464,21 +474,21 @@
 
 
 def align_kernel(
-    held_ref, before_refs, own, even_edge, odd_edge, even_1, odd_1, even_2, odd_2,
+    held_ref, before_refs, own, even_edge, odd_edge,
     even_out, odd_out, faces, sides,
     tail, head, edges, sem,
 ):
     before, after = drifts(held_ref, before_refs)
     even = is_even("curve")
 
-    def one_side(zone, message, _):
+    def one_side(zone, message):
         return [(message.at[pl.ds(0, PLANE)], to_plane(zone, plane_of(0, 0, 1)))]
 
-    def both_sides(zone, _, message):
+    def both_sides(zone, message):
         return [(message.at[pl.ds(0, 2 * PLANE)], to_plane(zone, 0, 2))]
 
-    by_parity((even_1, even_2), (odd_1, odd_2), tail, head, one_side, both_sides, sem)
-    take_zones(even_edge, odd_edge, edges.at[0], edges.at[1], sem, even)
+    by_parity((even_edge,), (odd_edge,), tail, head, one_side, both_sides, sem)
+    take_edges(even_edge, odd_edge, edges, sem)
     here = Window(before, after)
 
     def body(k, carry):
@@ -528,7 +538,7 @@
 
 
 def face_kernel(
-    held_ref, before_refs, own, even_1, odd_1, even_2, odd_2,
+    held_ref, before_refs, own, even_0, odd_0, even_1, odd_1, even_2, odd_2,
     even_face, odd_face, faces, sides,
     even_out, odd_out, even_end, odd_end, new, below, inner,
     tail, head, near, q, ends, sem,
@@ -537,16 +547,16 @@
     even = is_even("curve")
     half = 64 * WIN
 
-    def one_side(zone, message, _):
+    def one_side(zone, common, message, _):
         return [
-            (message.at[pl.ds(PLANE, PLANE)], to_plane(zone, plane_of(1, 2, 3))),
-            (message.at[pl.ds(2 * PLANE, 2 * PLANE)], to_plane(zone, plane_of(2, 4, 6), 2)),
+            (common.at[pl.ds(PLANE, PLANE)], to_plane(zone, plane_of(1, 2, 3))),
+            (message, to_plane(zone, plane_of(2, 4, 6), 2)),
         ]
 
-    def both_sides(zone, _, message):
-        return [(message.at[pl.ds(2 * PLANE, 6 * PLANE)], to_plane(zone, 2 * PLANE, 6))]
-
-    by_parity((even_1, even_2), (odd_1, odd_2), tail, head, one_side, both_sides, sem)
+    def both_sides(zone, _, __, message):
+        return [(message, to_plane(zone, 2 * PLANE, 6))]
+
+    by_parity((even_0, even_1, even_2), (odd_0, odd_1, odd_2), tail, head, one_side, both_sides, sem)
     take_faces(even_face, odd_face, near.at[pl.ds(0, half)], near.at[pl.ds(half, half)], sem)
     here = Window(before, after)
 
@@ -763,7 +773,10 @@
     message, edge = (8 * zone, LANES), (8, LANES)
     *outs, count = call(
         front_kernel,
-        [array(*edge)] * 2 + [array(4 * zone, LANES)] * 2 + [array(*message)] * 2 + [array(8, LANES)],
+        [array(2 * zone + 8, LANES)] * 2
+        + [array(2 * zone, LANES)] * 2
+        + [array(6 * zone, LANES)] * 2
+        + [array(8, LANES)],
         ((counts,), (), state2, coef2),
         [message, message, edge, edge],
         limit=6,
@@ -799,7 +812,7 @@
     *near_out, faces, sides = call(
         align_kernel,
         [array(win, LANES)] * 2 + [array(2 * win, LANES), array(32 * WIN, LANES)],
-        ((counts,), others, front, *edges_in, *planes_in),
+        ((counts,), others, front, *edges_in),
         [(2 * zone + 2 * PAD, LANES), (2 * zone + 2 * PAD, LANES), (2, 8, LANES)],
         limit=8,
         vmem_ins=(0,),
@@ -809,13 +822,13 @@
     near_a, near_b, end_a, end_b, new, below, inner = call(
         face_kernel,
         [array(win, LANES)] * 2 + [array(16, LANES)] * 2 + [array(2 * win, LANES)] * 3,
-        ((counts,), others, front, *planes_in, *near_in, faces, sides),
+        ((counts,), others, front, *edges_in, *planes_in, *near_in, faces, sides),
         [
             (8 * zone + 2 * PAD, LANES), (8 * zone + 2 * PAD, LANES),
             (2 * win, LANES), (2 * win, LANES), (2, 16, LANES),
         ],
         limit=8,
-        vmem_ins=(0, 7, 8),
+        vmem_ins=(0, 9, 10),
         vmem_outs=(4, 5, 6),
         us=3,
     )

time: 77.6 us -> 74.9 us (0.965)
  the two profiles are of different devices: /device:TPU:16 before, /device:TPU:12 now
where the time goes in v5:
time: 74.9 us; the launch traced here: 74.6 us
  waiting for transfers between devices  28 us (37%)
  starting transfers between devices  25.4 us (34%)
  Pallas kernels  15.7 us (21%)
  local copies, waits for them, and re-layouts  4.67 us (6%)
  between operations  0.88 us (1%)
    ppermute x14, starting transfers between devices, swapped(): return lax.ppermute(value, axis, pairs)  23.7 us
    ppermute x14, waiting for transfers between devices, swapped(): return lax.ppermute(value, axis, pairs)  21.1 us
    pallas_call x6, Pallas kernels, call(): pl.pallas_call(body, out_shape=outs, in_specs=specs, out_specs=[vmem if i...  15.7 us
    ppermute x2, waiting for transfers between devices, counts_swapped(): others.append(lax.ppermute(total, 'curve', pairs))  6.9 us
    unnamed x8, local copies, waits for them, and re-layouts  4.67 us
    ppermute x2, starting transfers between devices, counts_swapped(): others.append(lax.ppermute(total, 'curve', pairs))  1.7 us
  transfers between devices with their start and end apart: 16, of which 4 were waited for; matrix products, arithmetic and copies ran while one was open for 0% of the time, Pallas kernels for 15%

profile of v5, /device:TPU:12, one launch (start us, length us, event | category | flops | bytes accessed | tf_op | source)
XLA Modules:
  0.0 74.6 jit_solution(7759946409373940122)
XLA Ops:
  0.7 2.8 %copy-done = f32[2,512,1,1536]{3,2,1,0:T(1,128)S(1)} copy-done((f32[2,512,1,1536]{3,2,1,0:T(1,128)S(1)}, f32[2,512,1,1536]{3,2,1,0:T(1,128)}, u32[]{:S(2)}) %copy-start) | copy-done | bytes 6291480
  3.4 1.9 %copy-done.2 = f32[512,1,1536]{2,1,0:T(1,128)S(1)} copy-done((f32[512,1,1536]{2,1,0:T(1,128)S(1)}, f32[512,1,1536]{2,1,0:T(1,128)}, u32[]{:S(2)}) %copy-start.2) | copy-done | bytes 3145752
  5.3 1.2 %shard_map.37 = (f32[264,128]{1,0:T(8,128)S(1)}, f32[264,128]{1,0:T(8,128)S(1)}, f32[256,128]{1,0:T(8,128)S(1)}, f32[256,128]{1,0:T(8,128)S(1)}, f32[768,128]{1,...) custom-call(s32[1,1]{1,0:T(1,128)S(6)} %copy.7.held_ref, f32[12288,128]{1,0:T(8,128)S(1)} %bitcast.3, ...), custom_call_target="tpu_custom_call" | custom-call | flops 8000000 | bytes 2000000 | tf_op jit(solution)/shard_map/pallas_call | solution.py:754
  6.6 3.7 %collective-permute-start.8 = (f32[768,128]{1,0:T(8,128)S(1)}, f32[768,128]{1,0:T(8,128)S(1)}, u32[]{:S(2)}, u32[]{:S(2)}) collective-permute-start(f32[768,128]{1,0:T(8,128)S(1)} %get-tuple-element.40), channel_id=1, source_target_pairs={{1,5},{2,6},{9,13},{10,14},{17,21},{18,22},{25,29},{26,30},{5,1},{... | collective-permute-start | bytes 1179656 | tf_op jit(solution)/shard_map/ppermute | solution.py:708
  10.3 0.6 collective-permute-start.2
  10.9 1.5 %collective-permute-start = (f32[8,128]{1,0:T(8,128)S(1)}, f32[8,128]{1,0:T(8,128)S(1)}, u32[]{:S(2)}, u32[]{:S(2)}) collective-permute-start(f32[8,128]{1,0:T(8,128)S(1)} %get-tuple-element.29.a_ref), channel_id=1, source_target_pairs={{0,4},{4,0},{8,12},{12,8},{16,20},{20,16},{24,28},{28,24},{1,5},{5... | collective-permute-start | bytes 12296 | tf_op jit(solution)/shard_map/ppermute | solution.py:735
  12.3 2.3 %collective-permute-start.3 = (f32[264,128]{1,0:T(8,128)S(1)}, f32[264,128]{1,0:T(8,128)S(1)}, u32[]{:S(2)}, u32[]{:S(2)}) collective-permute-start(f32[264,128]{1,0:T(8,128)S(1)} %get-tuple-element.33), channel_id=1, source_target_pairs={{4,8},{12,16},{20,24},{8,4},{16,12},{24,20},{5,9},{13,17},{21,25},... | collective-permute-start | bytes 405512 | tf_op jit(solution)/shard_map/ppermute | solution.py:708
  14.7 6.9 %collective-permute-done.b_ref.refs_0_ = f32[8,128]{1,0:T(8,128)S(1)} collective-permute-done((f32[8,128]{1,0:T(8,128)S(1)}, f32[8,128]{1,0:T(8,128)S(1)}, u32[]{:S(2)}, u32[]{:S(2)}) %collective-permute-start) | collective-permute-done | bytes 4128 | tf_op jit(solution)/shard_map/ppermute | solution.py:735
  21.8 6.8 %collective-permute-start.9 = (f32[768,128]{1,0:T(8,128)S(1)}, f32[768,128]{1,0:T(8,128)S(1)}, u32[]{:S(2)}, u32[]{:S(2)}) collective-permute-start(f32[768,128]{1,0:T(8,128)S(1)} %get-tuple-element.41), channel_id=1, source_target_pairs={{5,9},{6,10},{13,17},{14,18},{21,25},{22,26},{9,5},{10,6},{17,13},... | collective-permute-start | bytes 1179656 | tf_op jit(solution)/shard_map/ppermute | solution.py:708
  28.6 0.7 collective-permute-start.6
  29.3 0.7 collective-permute-start.7
  30.0 4.4 %shard_map.39 = (f32[6176,128]{1,0:T(8,128)S(1)}, f32[6176,128]{1,0:T(8,128)S(1)}, f32[384,128]{1,0:T(8,128)S(1)}) custom-call(s32[1,1]{1,0:T(1,128)S(6)} %copy.7.held_ref, f32[12288,128]{1,0:T(8,128)S(1)} %bitcast.4, f32[6144,128]{1,0:T(8,128)S(1)} %bitcast.6), custom_call_target="tpu_custom_call" | custom-call | flops 24000000 | bytes 6000000 | tf_op jit(solution)/shard_map/pallas_call | solution.py:754
  34.4 2.5 %shard_map.41 = (f32[512,128]{1,0:T(8,128)S(1)}, f32[512,128]{1,0:T(8,128)S(1)}, f32[1024,128]{1,0:T(8,128)S(1)}, f32[256,128]{1,0:T(8,128)S(1)}) custom-call(s32[1,1]{1,0:T(1,128)S(6)} %copy.7.held_ref, f32[8,128]{1,0:T(8,128)S(1)} %collective-permute-done.b_ref.refs_0_, f32[8,128]{1,0:T(8,128)S(1)} %collective-permute-done.1.refs_1_, ...), custom_call_target="tpu_custom_call" | custom-call | flops 8000000 | bytes 2000000 | tf_op jit(solution)/shard_map/pallas_call | solution.py:754
  37.0 1.9 %collective-permute-start.11 = (f32[512,128]{1,0:T(8,128)S(1)}, f32[512,128]{1,0:T(8,128)S(1)}, u32[]{:S(2)}, u32[]{:S(2)}) collective-permute-start(f32[512,128]{1,0:T(8,128)S(1)} %get-tuple-element.43), channel_id=1, source_target_pairs={{1,2},{2,1},{5,6},{6,5},{9,10},{10,9},{13,14},{14,13},{17,18},{18,... | collective-permute-start | bytes 786440 | tf_op jit(solution)/shard_map/ppermute | solution.py:708
  38.9 1.1 %shard_map.40 = (f32[6176,128]{1,0:T(8,128)S(1)}, f32[1024,128]{1,0:T(8,128)S(1)}, f32[1024,128]{1,0:T(8,128)S(1)}) custom-call(s32[1,1]{1,0:T(1,128)S(6)} %copy.7.held_ref, f32[6176,128]{1,0:T(8,128)S(1)} %get-tuple-element.30.refs_0_, f32[384,128]{1,0:T(8,128)S(1)} %get-tuple-element.31.refs_1_, ...), custom_call_target="tpu_custom_call", output_to_operand_aliasing={{0}: (1, {})} | custom-call | flops 8000000 | bytes 2000000 | tf_op jit(solution)/shard_map/pallas_call | solution.py:754
  40.3 1.9 %collective-permute-start.5 = (f32[1024,128]{1,0:T(8,128)S(1)}, f32[1024,128]{1,0:T(8,128)S(1)}, u32[]{:S(2)}, u32[]{:S(2)}) collective-permute-start(f32[1024,128]{1,0:T(8,128)S(1)} %get-tuple-element.36), channel_id=1, source_target_pairs={{4,8},{12,16},{20,24},{8,4},{16,12},{24,20},{5,9},{13,17},{21,25},... | collective-permute-start | bytes 1572872 | tf_op jit(solution)/shard_map/ppermute | solution.py:708
  42.3 2.4 %collective-permute-done.11.refs_10_ = f32[512,128]{1,0:T(8,128)S(1)} collective-permute-done((f32[512,128]{1,0:T(8,128)S(1)}, f32[512,128]{1,0:T(8,128)S(1)}, u32[]{:S(2)}, u32[]{:S(2)}) %collective-permute-start.11) | collective-permute-done | bytes 262176 | tf_op jit(solution)/shard_map/ppermute | solution.py:708
  44.7 2.9 %shard_map.42 = (f32[512,128]{1,0:T(8,128)S(1)}, f32[512,128]{1,0:T(8,128)S(1)}, f32[16,128]{1,0:T(8,128)S(1)}, f32[16,128]{1,0:T(8,128)S(1)}, f32[1024,128]{1,0...) custom-call(s32[1,1]{1,0:T(1,128)S(6)} %copy.7.held_ref, ...), custom_call_target="tpu_custom_call" | custom-call | flops 12000000 | bytes 3000000 | tf_op jit(solution)/shard_map/pallas_call | solution.py:754
  47.6 2.2 %collective-permute-start.13 = (f32[512,128]{1,0:T(8,128)S(1)}, f32[512,128]{1,0:T(8,128)S(1)}, u32[]{:S(2)}, u32[]{:S(2)}) collective-permute-start(f32[512,128]{1,0:T(8,128)S(1)} %get-tuple-element.47), channel_id=1, source_target_pairs={{1,2},{2,1},{5,6},{6,5},{9,10},{10,9},{13,14},{14,13},{17,18},{18,... | collective-permute-start | bytes 786440 | tf_op jit(solution)/shard_map/ppermute | solution.py:708
  49.9 0.7 collective-permute-start.14
  50.5 14.1 %collective-permute-done.14.refs_7_ = f32[16,128]{1,0:T(8,128)S(1)} collective-permute-done((f32[16,128]{1,0:T(8,128)S(1)}, f32[16,128]{1,0:T(8,128)S(1)}, u32[]{:S(2)}, u32[]{:S(2)}) %collective-permute-start.14) | collective-permute-done | bytes 8224 | tf_op jit(solution)/shard_map/ppermute | solution.py:708
  64.6 1.9 %collective-permute-start.15 = (f32[16,128]{1,0:T(8,128)S(1)}, f32[16,128]{1,0:T(8,128)S(1)}, u32[]{:S(2)}, u32[]{:S(2)}) collective-permute-start(f32[16,128]{1,0:T(8,128)S(1)} %get-tuple-element.49), channel_id=1, source_target_pairs={{4,8},{12,16},{20,24},{8,4},{16,12},{24,20},{5,9},{13,17},{21,25},... | collective-permute-start | bytes 24584 | tf_op jit(solution)/shard_map/ppermute | solution.py:708
  66.5 4.5 %collective-permute-done.15.refs_8_ = f32[16,128]{1,0:T(8,128)S(1)} collective-permute-done((f32[16,128]{1,0:T(8,128)S(1)}, f32[16,128]{1,0:T(8,128)S(1)}, u32[]{:S(2)}, u32[]{:S(2)}) %collective-permute-start.15) | collective-permute-done | bytes 8224 | tf_op jit(solution)/shard_map/ppermute | solution.py:708
  71.1 3.5 %shard_map.43 = f32[4096,128]{1,0:T(8,128)} custom-call(s32[1,1]{1,0:T(1,128)S(6)} %copy.7.held_ref, f32[8,128]{1,0:T(8,128)S(1)} %collective-permute-done.b_ref.refs_0_, f32[8,128]{1,0:T(8,128)S(1)} %collective-permute-done.1.refs_1_, f32[6176,128]{1,0:T(8,128)S(1)} %get-tuple-element.34.refs_2_, f32[1024,128]{1,0:T(8,128)S(1)} %collective-permute-done.4.refs_3_, ...), custom_call_target="tpu_custom_call" | custom-call | flops 12000000 | bytes 3000000 | tf_op jit(solution)/shard_map/pallas_call | solution.py:754
  (23 shorter events, 0.6 us)
Async XLA Ops:
  0.7 2.8 %copy-start = (f32[2,512,1,1536]{3,2,1,0:T(1,128)S(1)}, f32[2,512,1,1536]{3,2,1,0:T(1,128)}, u32[]{:S(2)}) copy-start(f32[2,512,1,1536]{3,2,1,0:T(1,128)} %param.3) | copy-start | bytes 18874372
  3.4 1.9 %copy-start.2 = (f32[512,1,1536]{2,1,0:T(1,128)S(1)}, f32[512,1,1536]{2,1,0:T(1,128)}, u32[]{:S(2)}) copy-start(f32[512,1,1536]{2,1,0:T(1,128)} %param.4) | copy-start | bytes 9437188
  5.3 24.6 %copy-start.1 = (f32[2,512,1,1536]{3,2,1,0:T(1,128)S(1)}, f32[2,512,1,1536]{3,2,1,0:T(1,128)}, u32[]{:S(2)}) copy-start(f32[2,512,1,1536]{3,2,1,0:T(1,128)} %param.3) | copy-start | bytes 18874372
  5.3 24.6 %copy-start.3 = (f32[512,1,1536]{2,1,0:T(1,128)S(1)}, f32[512,1,1536]{2,1,0:T(1,128)}, u32[]{:S(2)}) copy-start(f32[512,1,1536]{2,1,0:T(1,128)} %param.4) | copy-start | bytes 9437188
  6.6 33.8 %collective-permute-start.8 = (f32[768,128]{1,0:T(8,128)S(1)}, f32[768,128]{1,0:T(8,128)S(1)}, u32[]{:S(2)}, u32[]{:S(2)}) collective-permute-start(f32[768,128]{1,0:T(8,128)S(1)} %get-tuple-element.40), channel_id=1, source_target_pairs={{1,5},{2,6},{9,13},{10,14},{17,21},{18,22},{25,29},{26,30},{5,1},{... | collective-permute-start | bytes 1179656 | tf_op jit(solution)/shard_map/ppermute | solution.py:708
  10.3 19.0 %collective-permute-start.2 = (f32[264,128]{1,0:T(8,128)S(1)}, f32[264,128]{1,0:T(8,128)S(1)}, u32[]{:S(2)}, u32[]{:S(2)}) collective-permute-start(f32[264,128]{1,0:T(8,128)S(1)} %get-tuple-element.32), channel_id=1, source_target_pairs={{0,4},{8,12},{16,20},{24,28},{4,0},{12,8},{20,16},{28,24},{1,5},{9... | collective-permute-start | bytes 405512 | tf_op jit(solution)/shard_map/ppermute | solution.py:708
  10.9 10.7 %collective-permute-start = (f32[8,128]{1,0:T(8,128)S(1)}, f32[8,128]{1,0:T(8,128)S(1)}, u32[]{:S(2)}, u32[]{:S(2)}) collective-permute-start(f32[8,128]{1,0:T(8,128)S(1)} %get-tuple-element.29.a_ref), channel_id=1, source_target_pairs={{0,4},{4,0},{8,12},{12,8},{16,20},{20,16},{24,28},{28,24},{1,5},{5... | collective-permute-start | bytes 12296 | tf_op jit(solution)/shard_map/ppermute | solution.py:735
  12.3 22.1 %collective-permute-start.3 = (f32[264,128]{1,0:T(8,128)S(1)}, f32[264,128]{1,0:T(8,128)S(1)}, u32[]{:S(2)}, u32[]{:S(2)}) collective-permute-start(f32[264,128]{1,0:T(8,128)S(1)} %get-tuple-element.33), channel_id=1, source_target_pairs={{4,8},{12,16},{20,24},{8,4},{16,12},{24,20},{5,9},{13,17},{21,25},... | collective-permute-start | bytes 405512 | tf_op jit(solution)/shard_map/ppermute | solution.py:708
  21.6 7.0 %collective-permute-start.1 = (f32[8,128]{1,0:T(8,128)S(1)}, f32[8,128]{1,0:T(8,128)S(1)}, u32[]{:S(2)}, u32[]{:S(2)}) collective-permute-start(f32[8,128]{1,0:T(8,128)S(1)} %shard_map.38), channel_id=1, source_target_pairs={{0,8},{4,12},{8,0},{12,4},{16,24},{20,28},{24,16},{28,20},{1,9},{5... | collective-permute-start | bytes 12296 | tf_op jit(solution)/shard_map/ppermute | solution.py:735
  21.8 20.5 %collective-permute-start.9 = (f32[768,128]{1,0:T(8,128)S(1)}, f32[768,128]{1,0:T(8,128)S(1)}, u32[]{:S(2)}, u32[]{:S(2)}) collective-permute-start(f32[768,128]{1,0:T(8,128)S(1)} %get-tuple-element.41), channel_id=1, source_target_pairs={{5,9},{6,10},{13,17},{14,18},{21,25},{22,26},{9,5},{10,6},{17,13},... | collective-permute-start | bytes 1179656 | tf_op jit(solution)/shard_map/ppermute | solution.py:708
  28.6 8.4 %collective-permute-start.6 = (f32[256,128]{1,0:T(8,128)S(1)}, f32[256,128]{1,0:T(8,128)S(1)}, u32[]{:S(2)}, u32[]{:S(2)}) collective-permute-start(f32[256,128]{1,0:T(8,128)S(1)} %get-tuple-element.38), channel_id=1, source_target_pairs={{0,4},{3,7},{8,12},{11,15},{16,20},{19,23},{24,28},{27,31},{4,0},{... | collective-permute-start | bytes 393224 | tf_op jit(solution)/shard_map/ppermute | solution.py:708
  29.3 10.8 %collective-permute-start.7 = (f32[256,128]{1,0:T(8,128)S(1)}, f32[256,128]{1,0:T(8,128)S(1)}, u32[]{:S(2)}, u32[]{:S(2)}) collective-permute-start(f32[256,128]{1,0:T(8,128)S(1)} %get-tuple-element.39), channel_id=1, source_target_pairs={{4,8},{7,11},{12,16},{15,19},{20,24},{23,27},{8,4},{11,7},{16,12},... | collective-permute-start | bytes 393224 | tf_op jit(solution)/shard_map/ppermute | solution.py:708
  36.9 5.4 %collective-permute-start.10 = (f32[512,128]{1,0:T(8,128)S(1)}, f32[512,128]{1,0:T(8,128)S(1)}, u32[]{:S(2)}, u32[]{:S(2)}) collective-permute-start(f32[512,128]{1,0:T(8,128)S(1)} %get-tuple-element.42), channel_id=1, source_target_pairs={{0,1},{2,3},{1,0},{3,2},{4,5},{6,7},{5,4},{7,6},{8,9},{10,11},{9,8... | collective-permute-start | bytes 786440 | tf_op jit(solution)/shard_map/ppermute | solution.py:708
  37.0 7.7 %collective-permute-start.11 = (f32[512,128]{1,0:T(8,128)S(1)}, f32[512,128]{1,0:T(8,128)S(1)}, u32[]{:S(2)}, u32[]{:S(2)}) collective-permute-start(f32[512,128]{1,0:T(8,128)S(1)} %get-tuple-element.43), channel_id=1, source_target_pairs={{1,2},{2,1},{5,6},{6,5},{9,10},{10,9},{13,14},{14,13},{17,18},{18,... | collective-permute-start | bytes 786440 | tf_op jit(solution)/shard_map/ppermute | solution.py:708
  40.1 31.0 %collective-permute-start.4 = (f32[1024,128]{1,0:T(8,128)S(1)}, f32[1024,128]{1,0:T(8,128)S(1)}, u32[]{:S(2)}, u32[]{:S(2)}) collective-permute-start(f32[1024,128]{1,0:T(8,128)S(1)} %get-tuple-element.35), channel_id=1, source_target_pairs={{0,4},{8,12},{16,20},{24,28},{4,0},{12,8},{20,16},{28,24},{1,5},{9... | collective-permute-start | bytes 1572872 | tf_op jit(solution)/shard_map/ppermute | solution.py:708
  40.3 30.7 %collective-permute-start.5 = (f32[1024,128]{1,0:T(8,128)S(1)}, f32[1024,128]{1,0:T(8,128)S(1)}, u32[]{:S(2)}, u32[]{:S(2)}) collective-permute-start(f32[1024,128]{1,0:T(8,128)S(1)} %get-tuple-element.36), channel_id=1, source_target_pairs={{4,8},{12,16},{20,24},{8,4},{16,12},{24,20},{5,9},{13,17},{21,25},... | collective-permute-start | bytes 1572872 | tf_op jit(solution)/shard_map/ppermute | solution.py:708
  47.6 23.5 %collective-permute-start.12 = (f32[512,128]{1,0:T(8,128)S(1)}, f32[512,128]{1,0:T(8,128)S(1)}, u32[]{:S(2)}, u32[]{:S(2)}) collective-permute-start(f32[512,128]{1,0:T(8,128)S(1)} %get-tuple-element.46), channel_id=1, source_target_pairs={{0,1},{2,3},{1,0},{3,2},{4,5},{6,7},{5,4},{7,6},{8,9},{10,11},{9,8... | collective-permute-start | bytes 786440 | tf_op jit(solution)/shard_map/ppermute | solution.py:708
  47.6 23.4 %collective-permute-start.13 = (f32[512,128]{1,0:T(8,128)S(1)}, f32[512,128]{1,0:T(8,128)S(1)}, u32[]{:S(2)}, u32[]{:S(2)}) collective-permute-start(f32[512,128]{1,0:T(8,128)S(1)} %get-tuple-element.47), channel_id=1, source_target_pairs={{1,2},{2,1},{5,6},{6,5},{9,10},{10,9},{13,14},{14,13},{17,18},{18,... | collective-permute-start | bytes 786440 | tf_op jit(solution)/shard_map/ppermute | solution.py:708
  49.9 14.8 %collective-permute-start.14 = (f32[16,128]{1,0:T(8,128)S(1)}, f32[16,128]{1,0:T(8,128)S(1)}, u32[]{:S(2)}, u32[]{:S(2)}) collective-permute-start(f32[16,128]{1,0:T(8,128)S(1)} %get-tuple-element.48), channel_id=1, source_target_pairs={{0,4},{8,12},{16,20},{24,28},{4,0},{12,8},{20,16},{28,24},{1,5},{9... | collective-permute-start | bytes 24584 | tf_op jit(solution)/shard_map/ppermute | solution.py:708
  64.6 6.4 %collective-permute-start.15 = (f32[16,128]{1,0:T(8,128)S(1)}, f32[16,128]{1,0:T(8,128)S(1)}, u32[]{:S(2)}, u32[]{:S(2)}) collective-permute-start(f32[16,128]{1,0:T(8,128)S(1)} %get-tuple-element.49), channel_id=1, source_target_pairs={{4,8},{12,16},{20,24},{8,4},{16,12},{24,20},{5,9},{13,17},{21,25},... | collective-permute-start | bytes 24584 | tf_op jit(solution)/shard_map/ppermute | solution.py:708

commit v6 on v5

--- a/solution.py
+++ b/solution.py
@@ -139,7 +139,7 @@
     even = is_even("curve")
     end = held - 1
     row, lane = lax.div(end, LANES), lax.rem(end, LANES)
-    blank = jnp.zeros((6, LANES), F32)
+    blank = jnp.full((6, LANES), held, jnp.int32).astype(F32)
     first = edge_rows(u, s, c, 0, 0, 0, ZONE)
     head_edge[...] = jnp.concatenate(first + [blank], 0)
     last = edge_rows(u, s, c, 7, row, lane, row - ZONE)
@@ -715,24 +715,38 @@
     return got
 
 
+def first_sum_kernel(count_ref, edge_ref, other_ref, sum_ref):
+    other = jnp.broadcast_to(edge_ref[2 * PLANE + 2 : 2 * PLANE + 3, :], (8, LANES))
+    other_ref[...] = other
+    sum_ref[...] = count_ref[...] + other
+
+
 def add_kernel(a_ref, b_ref, sum_ref):
     sum_ref[...] = a_ref[...] + b_ref[...]
 
 
-def counts_swapped(total):
-    count, others = lax.axis_size("curve"), []
+def small_call(kernel, outs, *ins):
     vmem = pl.BlockSpec(memory_space=pltpu.VMEM)
-    for i in range((count - 1).bit_length() - 1):
-        if others:
-            total = pl.pallas_call(
-                add_kernel,
-                out_shape=array(8, LANES),
-                in_specs=[vmem, vmem],
-                out_specs=vmem,
-                compiler_params=pltpu.CompilerParams(vmem_limit_bytes=2**20),
-            )(total, others[-1])
-        pairs = [(a, a ^ 1 << i) for a in range(count) if a ^ 1 << i < count]
-        others.append(lax.ppermute(total, "curve", pairs))
+    return pl.pallas_call(
+        kernel,
+        out_shape=[array(8, LANES)] * outs,
+        in_specs=[vmem] * len(ins),
+        out_specs=[vmem] * outs,
+        compiler_params=pltpu.CompilerParams(vmem_limit_bytes=2**20),
+    )(*ins)
+
+
+def counts_swapped(count, edge):
+    ranks, others = lax.axis_size("curve"), []
+    for i in range((ranks - 1).bit_length() - 1):
+        if i == 0:
+            other, total = small_call(first_sum_kernel, 2, count, edge)
+        else:
+            pairs = [(a, a ^ 1 << i) for a in range(ranks) if a ^ 1 << i < ranks]
+            other = lax.ppermute(total, "curve", pairs)
+            if 2 << i < ranks // 2:
+                (total,) = small_call(add_kernel, 1, total, other)
+        others.append(other)
     return others
 
 
@@ -785,7 +799,7 @@
     )
     curves = lax.axis_size("grp")
     edges_in = swaps(outs[:2], "curve")
-    others = counts_swapped(count)
+    others = counts_swapped(count, edges_in[0])
     planes_in = swaps(outs[2:4], "curve", (0, curves - 1))
     planes_in += swaps(outs[4:], "curve", range(1, curves - 1))
     front, pack, ends = call(

time: 74.9 us -> 77.6 us (1.036)
  the two profiles are of different devices: /device:TPU:12 before, /device:TPU:16 now
where the time goes in v6:
time: 77.6 us; the launch traced here: 77.2 us
  starting transfers between devices  35 us (45%)
  waiting for transfers between devices  20.4 us (26%)
  Pallas kernels  16.3 us (21%)
  local copies, waits for them, and re-layouts  4.67 us (6%)
  between operations  0.88 us (1%)
    ppermute x14, starting transfers between devices, swapped(): return lax.ppermute(value, axis, pairs)  33.4 us
    ppermute x14, waiting for transfers between devices, swapped(): return lax.ppermute(value, axis, pairs)  20.4 us
    pallas_call x6, Pallas kernels, call(): pl.pallas_call(body, out_shape=outs, in_specs=specs, out_specs=[vmem if i...  16.3 us
    unnamed x8, local copies, waits for them, and re-layouts  4.67 us
  transfers between devices with their start and end apart: 15, of which 2 were waited for; matrix products, arithmetic and copies ran while one was open for 0% of the time, Pallas kernels for 15%

profile of v6, /device:TPU:16, one launch (start us, length us, event | category | flops | bytes accessed | tf_op | source)
XLA Modules:
  0.0 77.2 jit_solution(10323095546299456499)
XLA Ops:
  0.7 2.8 %copy-done = f32[2,512,1,1536]{3,2,1,0:T(1,128)S(1)} copy-done((f32[2,512,1,1536]{3,2,1,0:T(1,128)S(1)}, f32[2,512,1,1536]{3,2,1,0:T(1,128)}, u32[]{:S(2)}) %copy-start) | copy-done | bytes 6291480
  3.4 1.9 %copy-done.2 = f32[512,1,1536]{2,1,0:T(1,128)S(1)} copy-done((f32[512,1,1536]{2,1,0:T(1,128)S(1)}, f32[512,1,1536]{2,1,0:T(1,128)}, u32[]{:S(2)}) %copy-start.2) | copy-done | bytes 3145752
  5.3 1.2 %shard_map.37 = (f32[264,128]{1,0:T(8,128)S(1)}, f32[264,128]{1,0:T(8,128)S(1)}, f32[256,128]{1,0:T(8,128)S(1)}, f32[256,128]{1,0:T(8,128)S(1)}, f32[768,128]{1,...) custom-call(s32[1,1]{1,0:T(1,128)S(6)} %copy.7.held_ref, f32[12288,128]{1,0:T(8,128)S(1)} %bitcast.3, ...), custom_call_target="tpu_custom_call" | custom-call | flops 8000000 | bytes 2000000 | tf_op jit(solution)/shard_map/pallas_call | solution.py:768
  6.6 0.8 %collective-permute-start.7 = (f32[768,128]{1,0:T(8,128)S(1)}, f32[768,128]{1,0:T(8,128)S(1)}, u32[]{:S(2)}, u32[]{:S(2)}) collective-permute-start(f32[768,128]{1,0:T(8,128)S(1)} %get-tuple-element.44), channel_id=1, source_target_pairs={{1,5},{2,6},{9,13},{10,14},{17,21},{18,22},{25,29},{26,30},{5,1},{... | collective-permute-start | bytes 1179656 | tf_op jit(solution)/shard_map/ppermute | solution.py:708
  7.4 1.6 %collective-permute-start = (f32[264,128]{1,0:T(8,128)S(1)}, f32[264,128]{1,0:T(8,128)S(1)}, u32[]{:S(2)}, u32[]{:S(2)}) collective-permute-start(f32[264,128]{1,0:T(8,128)S(1)} %get-tuple-element.32), channel_id=1, source_target_pairs={{0,4},{8,12},{16,20},{24,28},{4,0},{12,8},{20,16},{28,24},{1,5},{9... | collective-permute-start | bytes 405512 | tf_op jit(solution)/shard_map/ppermute | solution.py:708
  8.9 2.4 %collective-permute-start.2 = (f32[264,128]{1,0:T(8,128)S(1)}, f32[264,128]{1,0:T(8,128)S(1)}, u32[]{:S(2)}, u32[]{:S(2)}) collective-permute-start(f32[264,128]{1,0:T(8,128)S(1)} %get-tuple-element.37), channel_id=1, source_target_pairs={{4,8},{12,16},{20,24},{8,4},{16,12},{24,20},{5,9},{13,17},{21,25},... | collective-permute-start | bytes 405512 | tf_op jit(solution)/shard_map/ppermute | solution.py:708
  11.4 0.7 collective-permute-start.8
  12.1 4.4 %collective-permute-start.5 = (f32[256,128]{1,0:T(8,128)S(1)}, f32[256,128]{1,0:T(8,128)S(1)}, u32[]{:S(2)}, u32[]{:S(2)}) collective-permute-start(f32[256,128]{1,0:T(8,128)S(1)} %get-tuple-element.42), channel_id=1, source_target_pairs={{0,4},{3,7},{8,12},{11,15},{16,20},{19,23},{24,28},{27,31},{4,0},{... | collective-permute-start | bytes 393224 | tf_op jit(solution)/shard_map/ppermute | solution.py:708
  16.5 1.9 %collective-permute-start.6 = (f32[256,128]{1,0:T(8,128)S(1)}, f32[256,128]{1,0:T(8,128)S(1)}, u32[]{:S(2)}, u32[]{:S(2)}) collective-permute-start(f32[256,128]{1,0:T(8,128)S(1)} %get-tuple-element.43), channel_id=1, source_target_pairs={{4,8},{7,11},{12,16},{15,19},{20,24},{23,27},{8,4},{11,7},{16,12},... | collective-permute-start | bytes 393224 | tf_op jit(solution)/shard_map/ppermute | solution.py:708
  18.4 1.5 %collective-permute-start.1 = (f32[8,128]{1,0:T(8,128)S(1)}, f32[8,128]{1,0:T(8,128)S(1)}, u32[]{:S(2)}, u32[]{:S(2)}) collective-permute-start(f32[8,128]{1,0:T(8,128)S(1)} %get-tuple-element.34), channel_id=1, source_target_pairs={{0,8},{4,12},{8,0},{12,4},{16,24},{20,28},{24,16},{28,20},{1,9},{5... | collective-permute-start | bytes 12296 | tf_op jit(solution)/shard_map/ppermute | solution.py:746
  20.0 5.1 %shard_map.39 = (f32[6176,128]{1,0:T(8,128)S(1)}, f32[6176,128]{1,0:T(8,128)S(1)}, f32[384,128]{1,0:T(8,128)S(1)}) custom-call(s32[1,1]{1,0:T(1,128)S(6)} %copy.7.held_ref, f32[12288,128]{1,0:T(8,128)S(1)} %bitcast.4, f32[6144,128]{1,0:T(8,128)S(1)} %bitcast.6), custom_call_target="tpu_custom_call" | custom-call | flops 24000000 | bytes 6000000 | tf_op jit(solution)/shard_map/pallas_call | solution.py:768
  25.1 2.3 %shard_map.41 = (f32[512,128]{1,0:T(8,128)S(1)}, f32[512,128]{1,0:T(8,128)S(1)}, f32[1024,128]{1,0:T(8,128)S(1)}, f32[256,128]{1,0:T(8,128)S(1)}) custom-call(s32[1,1]{1,0:T(1,128)S(6)} %copy.7.held_ref, f32[8,128]{1,0:T(8,128)S(1)} %get-tuple-element.33.refs_0_, f32[8,128]{1,0:T(8,128)S(1)} %collective-permute-done.1.refs_1_, ...), custom_call_target="tpu_custom_call" | custom-call | flops 8000000 | bytes 2000000 | tf_op jit(solution)/shard_map/pallas_call | solution.py:768
  27.4 0.7 collective-permute-start.10
  28.1 12.6 %collective-permute-start.9 = (f32[512,128]{1,0:T(8,128)S(1)}, f32[512,128]{1,0:T(8,128)S(1)}, u32[]{:S(2)}, u32[]{:S(2)}) collective-permute-start(f32[512,128]{1,0:T(8,128)S(1)} %get-tuple-element.46), channel_id=1, source_target_pairs={{0,1},{2,3},{1,0},{3,2},{4,5},{6,7},{5,4},{7,6},{8,9},{10,11},{9,8... | collective-permute-start | bytes 786440 | tf_op jit(solution)/shard_map/ppermute | solution.py:708
  40.8 1.1 %shard_map.40 = (f32[6176,128]{1,0:T(8,128)S(1)}, f32[1024,128]{1,0:T(8,128)S(1)}, f32[1024,128]{1,0:T(8,128)S(1)}) custom-call(s32[1,1]{1,0:T(1,128)S(6)} %copy.7.held_ref, f32[6176,128]{1,0:T(8,128)S(1)} %get-tuple-element.35.refs_0_, f32[384,128]{1,0:T(8,128)S(1)} %get-tuple-element.36.refs_1_, ...), custom_call_target="tpu_custom_call", output_to_operand_aliasing={{0}: (1, {})} | custom-call | flops 8000000 | bytes 2000000 | tf_op jit(solution)/shard_map/pallas_call | solution.py:768
  42.0 2.2 %collective-permute-start.4 = (f32[1024,128]{1,0:T(8,128)S(1)}, f32[1024,128]{1,0:T(8,128)S(1)}, u32[]{:S(2)}, u32[]{:S(2)}) collective-permute-start(f32[1024,128]{1,0:T(8,128)S(1)} %get-tuple-element.40), channel_id=1, source_target_pairs={{4,8},{12,16},{20,24},{8,4},{16,12},{24,20},{5,9},{13,17},{21,25},... | collective-permute-start | bytes 1572872 | tf_op jit(solution)/shard_map/ppermute | solution.py:708
  44.3 3.0 %shard_map.42 = (f32[512,128]{1,0:T(8,128)S(1)}, f32[512,128]{1,0:T(8,128)S(1)}, f32[16,128]{1,0:T(8,128)S(1)}, f32[16,128]{1,0:T(8,128)S(1)}, f32[1024,128]{1,0...) custom-call(s32[1,1]{1,0:T(1,128)S(6)} %copy.7.held_ref, f32[8,128]{1,0:T(8,128)S(1)} %get-tuple-element.33.refs_0_, ...), custom_call_target="tpu_custom_call" | custom-call | flops 12000000 | bytes 3000000 | tf_op jit(solution)/shard_map/pallas_call | solution.py:768
  47.3 0.4 collective-permute-start.11
  47.7 0.7 collective-permute-start.12
  48.4 2.9 %collective-permute-start.13 = (f32[16,128]{1,0:T(8,128)S(1)}, f32[16,128]{1,0:T(8,128)S(1)}, u32[]{:S(2)}, u32[]{:S(2)}) collective-permute-start(f32[16,128]{1,0:T(8,128)S(1)} %get-tuple-element.52), channel_id=1, source_target_pairs={{0,4},{8,12},{16,20},{24,28},{4,0},{12,8},{20,16},{28,24},{1,5},{9... | collective-permute-start | bytes 24584 | tf_op jit(solution)/shard_map/ppermute | solution.py:708
  51.2 16.0 %collective-permute-done.13.refs_7_ = f32[16,128]{1,0:T(8,128)S(1)} collective-permute-done((f32[16,128]{1,0:T(8,128)S(1)}, f32[16,128]{1,0:T(8,128)S(1)}, u32[]{:S(2)}, u32[]{:S(2)}) %collective-permute-start.13) | collective-permute-done | bytes 8224 | tf_op jit(solution)/shard_map/ppermute | solution.py:708
  67.2 2.1 %collective-permute-start.14 = (f32[16,128]{1,0:T(8,128)S(1)}, f32[16,128]{1,0:T(8,128)S(1)}, u32[]{:S(2)}, u32[]{:S(2)}) collective-permute-start(f32[16,128]{1,0:T(8,128)S(1)} %get-tuple-element.53), channel_id=1, source_target_pairs={{4,8},{12,16},{20,24},{8,4},{16,12},{24,20},{5,9},{13,17},{21,25},... | collective-permute-start | bytes 24584 | tf_op jit(solution)/shard_map/ppermute | solution.py:708
  69.4 4.3 %collective-permute-done.14.refs_8_ = f32[16,128]{1,0:T(8,128)S(1)} collective-permute-done((f32[16,128]{1,0:T(8,128)S(1)}, f32[16,128]{1,0:T(8,128)S(1)}, u32[]{:S(2)}, u32[]{:S(2)}) %collective-permute-start.14) | collective-permute-done | bytes 8224 | tf_op jit(solution)/shard_map/ppermute | solution.py:708
  73.7 3.5 %shard_map.43 = f32[4096,128]{1,0:T(8,128)} custom-call(s32[1,1]{1,0:T(1,128)S(6)} %copy.7.held_ref, f32[8,128]{1,0:T(8,128)S(1)} %get-tuple-element.33.refs_0_, f32[8,128]{1,0:T(8,128)S(1)} %collective-permute-done.1.refs_1_, f32[6176,128]{1,0:T(8,128)S(1)} %get-tuple-element.38.refs_2_, f32[1024,128]{1,0:T(8,128)S(1)} %collective-permute-done.3.refs_3_, ...), custom_call_target="tpu_custom_call" | custom-call | flops 12000000 | bytes 3000000 | tf_op jit(solution)/shard_map/pallas_call | solution.py:768
  (21 shorter events, 0.1 us)
Async XLA Ops:
  0.7 2.8 %copy-start = (f32[2,512,1,1536]{3,2,1,0:T(1,128)S(1)}, f32[2,512,1,1536]{3,2,1,0:T(1,128)}, u32[]{:S(2)}) copy-start(f32[2,512,1,1536]{3,2,1,0:T(1,128)} %param.3) | copy-start | bytes 18874372
  3.4 1.9 %copy-start.2 = (f32[512,1,1536]{2,1,0:T(1,128)S(1)}, f32[512,1,1536]{2,1,0:T(1,128)}, u32[]{:S(2)}) copy-start(f32[512,1,1536]{2,1,0:T(1,128)} %param.4) | copy-start | bytes 9437188
  5.3 14.7 %copy-start.1 = (f32[2,512,1,1536]{3,2,1,0:T(1,128)S(1)}, f32[2,512,1,1536]{3,2,1,0:T(1,128)}, u32[]{:S(2)}) copy-start(f32[2,512,1,1536]{3,2,1,0:T(1,128)} %param.3) | copy-start | bytes 18874372
  5.3 14.7 %copy-start.3 = (f32[512,1,1536]{2,1,0:T(1,128)S(1)}, f32[512,1,1536]{2,1,0:T(1,128)}, u32[]{:S(2)}) copy-start(f32[512,1,1536]{2,1,0:T(1,128)} %param.4) | copy-start | bytes 9437188
  6.6 35.4 %collective-permute-start.7 = (f32[768,128]{1,0:T(8,128)S(1)}, f32[768,128]{1,0:T(8,128)S(1)}, u32[]{:S(2)}, u32[]{:S(2)}) collective-permute-start(f32[768,128]{1,0:T(8,128)S(1)} %get-tuple-element.44), channel_id=1, source_target_pairs={{1,5},{2,6},{9,13},{10,14},{17,21},{18,22},{25,29},{26,30},{5,1},{... | collective-permute-start | bytes 1179656 | tf_op jit(solution)/shard_map/ppermute | solution.py:708
  7.4 9.1 %collective-permute-start = (f32[264,128]{1,0:T(8,128)S(1)}, f32[264,128]{1,0:T(8,128)S(1)}, u32[]{:S(2)}, u32[]{:S(2)}) collective-permute-start(f32[264,128]{1,0:T(8,128)S(1)} %get-tuple-element.32), channel_id=1, source_target_pairs={{0,4},{8,12},{16,20},{24,28},{4,0},{12,8},{20,16},{28,24},{1,5},{9... | collective-permute-start | bytes 405512 | tf_op jit(solution)/shard_map/ppermute | solution.py:708
  8.9 9.5 %collective-permute-start.2 = (f32[264,128]{1,0:T(8,128)S(1)}, f32[264,128]{1,0:T(8,128)S(1)}, u32[]{:S(2)}, u32[]{:S(2)}) collective-permute-start(f32[264,128]{1,0:T(8,128)S(1)} %get-tuple-element.37), channel_id=1, source_target_pairs={{4,8},{12,16},{20,24},{8,4},{16,12},{24,20},{5,9},{13,17},{21,25},... | collective-permute-start | bytes 405512 | tf_op jit(solution)/shard_map/ppermute | solution.py:708
  11.4 32.9 %collective-permute-start.8 = (f32[768,128]{1,0:T(8,128)S(1)}, f32[768,128]{1,0:T(8,128)S(1)}, u32[]{:S(2)}, u32[]{:S(2)}) collective-permute-start(f32[768,128]{1,0:T(8,128)S(1)} %get-tuple-element.45), channel_id=1, source_target_pairs={{5,9},{6,10},{13,17},{14,18},{21,25},{22,26},{9,5},{10,6},{17,13},... | collective-permute-start | bytes 1179656 | tf_op jit(solution)/shard_map/ppermute | solution.py:708
  12.1 16.1 %collective-permute-start.5 = (f32[256,128]{1,0:T(8,128)S(1)}, f32[256,128]{1,0:T(8,128)S(1)}, u32[]{:S(2)}, u32[]{:S(2)}) collective-permute-start(f32[256,128]{1,0:T(8,128)S(1)} %get-tuple-element.42), channel_id=1, source_target_pairs={{0,4},{3,7},{8,12},{11,15},{16,20},{19,23},{24,28},{27,31},{4,0},{... | collective-permute-start | bytes 393224 | tf_op jit(solution)/shard_map/ppermute | solution.py:708
  16.5 25.4 %collective-permute-start.6 = (f32[256,128]{1,0:T(8,128)S(1)}, f32[256,128]{1,0:T(8,128)S(1)}, u32[]{:S(2)}, u32[]{:S(2)}) collective-permute-start(f32[256,128]{1,0:T(8,128)S(1)} %get-tuple-element.43), channel_id=1, source_target_pairs={{4,8},{7,11},{12,16},{15,19},{20,24},{23,27},{8,4},{11,7},{16,12},... | collective-permute-start | bytes 393224 | tf_op jit(solution)/shard_map/ppermute | solution.py:708
  18.4 6.7 %collective-permute-start.1 = (f32[8,128]{1,0:T(8,128)S(1)}, f32[8,128]{1,0:T(8,128)S(1)}, u32[]{:S(2)}, u32[]{:S(2)}) collective-permute-start(f32[8,128]{1,0:T(8,128)S(1)} %get-tuple-element.34), channel_id=1, source_target_pairs={{0,8},{4,12},{8,0},{12,4},{16,24},{20,28},{24,16},{28,20},{1,9},{5... | collective-permute-start | bytes 12296 | tf_op jit(solution)/shard_map/ppermute | solution.py:746
  27.4 16.8 %collective-permute-start.10 = (f32[512,128]{1,0:T(8,128)S(1)}, f32[512,128]{1,0:T(8,128)S(1)}, u32[]{:S(2)}, u32[]{:S(2)}) collective-permute-start(f32[512,128]{1,0:T(8,128)S(1)} %get-tuple-element.47), channel_id=1, source_target_pairs={{1,2},{2,1},{5,6},{6,5},{9,10},{10,9},{13,14},{14,13},{17,18},{18,... | collective-permute-start | bytes 786440 | tf_op jit(solution)/shard_map/ppermute | solution.py:708
  28.1 16.1 %collective-permute-start.9 = (f32[512,128]{1,0:T(8,128)S(1)}, f32[512,128]{1,0:T(8,128)S(1)}, u32[]{:S(2)}, u32[]{:S(2)}) collective-permute-start(f32[512,128]{1,0:T(8,128)S(1)} %get-tuple-element.46), channel_id=1, source_target_pairs={{0,1},{2,3},{1,0},{3,2},{4,5},{6,7},{5,4},{7,6},{8,9},{10,11},{9,8... | collective-permute-start | bytes 786440 | tf_op jit(solution)/shard_map/ppermute | solution.py:708
  41.9 31.8 %collective-permute-start.3 = (f32[1024,128]{1,0:T(8,128)S(1)}, f32[1024,128]{1,0:T(8,128)S(1)}, u32[]{:S(2)}, u32[]{:S(2)}) collective-permute-start(f32[1024,128]{1,0:T(8,128)S(1)} %get-tuple-element.39), channel_id=1, source_target_pairs={{0,4},{8,12},{16,20},{24,28},{4,0},{12,8},{20,16},{28,24},{1,5},{9... | collective-permute-start | bytes 1572872 | tf_op jit(solution)/shard_map/ppermute | solution.py:708
  42.0 31.7 %collective-permute-start.4 = (f32[1024,128]{1,0:T(8,128)S(1)}, f32[1024,128]{1,0:T(8,128)S(1)}, u32[]{:S(2)}, u32[]{:S(2)}) collective-permute-start(f32[1024,128]{1,0:T(8,128)S(1)} %get-tuple-element.40), channel_id=1, source_target_pairs={{4,8},{12,16},{20,24},{8,4},{16,12},{24,20},{5,9},{13,17},{21,25},... | collective-permute-start | bytes 1572872 | tf_op jit(solution)/shard_map/ppermute | solution.py:708
  47.3 26.4 %collective-permute-start.11 = (f32[512,128]{1,0:T(8,128)S(1)}, f32[512,128]{1,0:T(8,128)S(1)}, u32[]{:S(2)}, u32[]{:S(2)}) collective-permute-start(f32[512,128]{1,0:T(8,128)S(1)} %get-tuple-element.50), channel_id=1, source_target_pairs={{0,1},{2,3},{1,0},{3,2},{4,5},{6,7},{5,4},{7,6},{8,9},{10,11},{9,8... | collective-permute-start | bytes 786440 | tf_op jit(solution)/shard_map/ppermute | solution.py:708
  47.7 26.0 %collective-permute-start.12 = (f32[512,128]{1,0:T(8,128)S(1)}, f32[512,128]{1,0:T(8,128)S(1)}, u32[]{:S(2)}, u32[]{:S(2)}) collective-permute-start(f32[512,128]{1,0:T(8,128)S(1)} %get-tuple-element.51), channel_id=1, source_target_pairs={{1,2},{2,1},{5,6},{6,5},{9,10},{10,9},{13,14},{14,13},{17,18},{18,... | collective-permute-start | bytes 786440 | tf_op jit(solution)/shard_map/ppermute | solution.py:708
  48.4 18.9 %collective-permute-start.13 = (f32[16,128]{1,0:T(8,128)S(1)}, f32[16,128]{1,0:T(8,128)S(1)}, u32[]{:S(2)}, u32[]{:S(2)}) collective-permute-start(f32[16,128]{1,0:T(8,128)S(1)} %get-tuple-element.52), channel_id=1, source_target_pairs={{0,4},{8,12},{16,20},{24,28},{4,0},{12,8},{20,16},{28,24},{1,5},{9... | collective-permute-start | bytes 24584 | tf_op jit(solution)/shard_map/ppermute | solution.py:708
  67.2 6.4 %collective-permute-start.14 = (f32[16,128]{1,0:T(8,128)S(1)}, f32[16,128]{1,0:T(8,128)S(1)}, u32[]{:S(2)}, u32[]{:S(2)}) collective-permute-start(f32[16,128]{1,0:T(8,128)S(1)} %get-tuple-element.53), channel_id=1, source_target_pairs={{4,8},{12,16},{20,24},{8,4},{16,12},{24,20},{5,9},{13,17},{21,25},... | collective-permute-start | bytes 24584 | tf_op jit(solution)/shard_map/ppermute | solution.py:708
